TPU v7x, 32 devices: a whole 2x2x4 slice. The times are simulated.
32 devices in a mesh: gz: 4 (over z), gy: 4 (over y, x), gx: 2 (over core).
Axes of the slice: x: 2, y: 2, z: 4, core: 2. Of those that a mesh axis runs over, the one named last changes fastest.
Arguments:
- rhs: float32 [16, 64, 8192], P('gz', 'gy', 'gx'), may hold values from -20 to 20
- guess: float32 [16, 64, 8192], P('gz', 'gy', 'gx'), may hold values from -0.6 to 0.6
- shifts: float32 [64], replicated, may hold values from 0.5 to 4
Outputs:
- normalized: float32 [16, 64, 8192], P('gz', 'gy', 'gx')
- gram_mean: float32 [64, 64], replicated
All inputs are finite; a program needn't handle non-finite values.
Results may differ from a plain program's by a relative error of at most 0.000088.
Values sent between devices are 32-bit elements; how exact they have to be, the bound alone decides.
No kernel may reach another device: no remote copies, remote signals or barrier semaphores. Data moves between devices by JAX's collectives and lax.ppermute only.
A program may use at most 64 MiB of HBM per device.

v0:
```python
import jax
import jax.numpy as jnp
from jax import lax
from jax.sharding import PartitionSpec as P


def padded(array, sides, width):
    for axis, dim in sides:
        peers, length = (lax.axis_size(axis), array.shape[dim])
        up = [(i, (i + 1) % peers) for i in range(peers)]
        down = [(j, i) for i, j in up]
        last = lax.slice_in_dim(array, length - width, length, axis=dim)
        initial = lax.slice_in_dim(array, 0, width, axis=dim)
        before = lax.ppermute(last, axis, up)
        after = lax.ppermute(initial, axis, down)
        array = jnp.concatenate([before, array, after], axis=dim)
    return array


def local(rhs, guess, shifts):
    z_cells, y_cells, lane_count = guess.shape
    columns = shifts.shape[0]
    x_cells = lane_count // columns
    z_padded = padded(guess, (("gz", 0),), 1)
    y_padded = padded(guess, (("gy", 1),), 1)
    neighbours = z_padded[2:] + z_padded[:-2] + y_padded[:, 2:] + y_padded[:, :-2]
    x_padded = padded(guess, (("gx", 2),), columns)
    neighbours = neighbours + x_padded[:, :, 2 * columns :] + x_padded[:, :, : -2 * columns]
    centre = jnp.tile(6.0 + shifts, x_cells)
    resid = rhs - (centre * guess - neighbours)
    flattened = resid.reshape(-1, columns)
    partial_gram = lax.dot_general(
        flattened,
        flattened,
        (((0,), (0,)), ((), ())),
        precision=lax.Precision.HIGHEST,
        preferred_element_type=jnp.float32,
    )
    gram = lax.psum(partial_gram, ("gz", "gy", "gx"))
    total_cells = (
        z_cells
        * y_cells
        * x_cells
        * lax.axis_size("gz")
        * lax.axis_size("gy")
        * lax.axis_size("gx")
    )
    gram_mean = gram / jnp.float32(total_cells)
    inverse_norm = lax.rsqrt(jnp.diagonal(gram_mean) + 1e-06)
    normalized = resid * jnp.tile(inverse_norm, x_cells)
    return (normalized, gram_mean)


def solution(mesh):
    placed = (P("gz", "gy", "gx"), P("gz", "gy", "gx"), P())
    return jax.shard_map(
        local, mesh=mesh, in_specs=placed, out_specs=(P("gz", "gy", "gx"), P()), check_vma=False
    )
```

profile of v0, /device:TPU:0, one launch (start us, length us, event | category | flops | bytes accessed | tf_op | source)
XLA Modules:
  0.0 67.7 jit_solution(4555758197529277649)
XLA Ops:
  0.6 0.0 copy-start.1
  0.6 1.2 %fusion.7 = (f32[1,16,4096]{2,1,0:T(8,128)S(1)}, f32[1,16,4096]{2,1,0:T(8,128)S(1)}) fusion(f32[4,16,4096]{2,1,0:T(8,128)} %param.4), kind=kLoop, calls=%fused_computation.19 | loop fusion | bytes 1048576 | tf_op jit(solution)/shard_map/slice | solution.py:13
  1.8 5.1 %collective-permute-start = (f32[1,16,4096]{2,1,0:T(8,128)S(1)}, f32[1,16,4096]{2,1,0:T(8,128)S(1)}, u32[]{:S(2)}, u32[]{:S(2)}) collective-permute-start(f32[1,16,4096]{2,1,0:T(8,128)S(1)} %get-tuple-element.2), channel_id=1, source_target_pairs={{8,0},{16,8},{24,16},{0,24},{9,1},{17,9},{25,17},{1,25},{10,2},{18... | collective-permute-start | bytes 786440 | tf_op jit(solution)/shard_map/ppermute | solution.py:15
  6.9 0.0 collective-permute-start.1
  6.9 1.3 %fusion.8 = (f32[4,1,4096]{2,1,0:T(1,128)S(1)}, f32[4,1,4096]{2,1,0:T(1,128)S(1)}) fusion(f32[4,16,4096]{2,1,0:T(8,128)} %param.4), kind=kLoop, calls=%fused_computation.20 | loop fusion | bytes 262144 | tf_op jit(solution)/shard_map/slice | solution.py:13
  8.2 2.5 %collective-permute-start.2 = (f32[4,1,4096]{2,1,0:T(1,128)S(1)}, f32[4,1,4096]{2,1,0:T(1,128)S(1)}, u32[]{:S(2)}, u32[]{:S(2)}) collective-permute-start(f32[4,1,4096]{2,1,0:T(1,128)S(1)} %get-tuple-element.4), channel_id=1, source_target_pairs={{2,0},{4,2},{6,4},{0,6},{3,1},{5,3},{7,5},{1,7},{10,8},{12,10},{14... | collective-permute-start | bytes 196616 | tf_op jit(solution)/shard_map/ppermute | solution.py:15
  10.7 0.0 collective-permute-start.3
  10.7 0.8 %fusion.9 = (f32[4,16,64]{2,1,0:T(8,128)S(1)}, f32[4,16,64]{2,1,0:T(8,128)S(1)}) fusion(f32[4,16,4096]{2,1,0:T(8,128)} %param.4), kind=kLoop, calls=%fused_computation.21 | loop fusion | bytes 65536 | tf_op jit(solution)/shard_map/slice | solution.py:13
  11.6 0.0 collective-permute-start.4
  11.6 0.7 broadcast_add_fusion
  12.3 0.5 collective-permute-done.4
  12.8 0.2 collective-permute-start.5
  13.0 0.1 mul.20
  13.0 1.0 %collective-permute-done.5 = f32[4,16,64]{2,1,0:T(8,128)S(1)} collective-permute-done((f32[4,16,64]{2,1,0:T(8,128)S(1)}, f32[4,16,64]{2,1,0:T(8,128)S(1)}, u32[]{:S(2)}, u32[]{:S(2)}) %collective-permute-start.5) | collective-permute-done | bytes 16416 | tf_op jit(solution)/shard_map/ppermute | solution.py:14
  14.0 0.0 collective-permute-done.2
  14.0 1.9 %collective-permute-done.3 = f32[4,1,4096]{2,1,0:T(1,128)S(1)} collective-permute-done((f32[4,1,4096]{2,1,0:T(1,128)S(1)}, f32[4,1,4096]{2,1,0:T(1,128)S(1)}, u32[]{:S(2)}, u32[]{:S(2)}) %collective-permute-start.3) | collective-permute-done | bytes 65568 | tf_op jit(solution)/shard_map/ppermute | solution.py:14
  15.9 0.0 collective-permute-done
  15.9 3.1 %collective-permute-done.1 = f32[1,16,4096]{2,1,0:T(8,128)S(1)} collective-permute-done((f32[1,16,4096]{2,1,0:T(8,128)S(1)}, f32[1,16,4096]{2,1,0:T(8,128)S(1)}, u32[]{:S(2)}, u32[]{:S(2)}) %collective-permute-start.1) | collective-permute-done | bytes 262176 | tf_op jit(solution)/shard_map/ppermute | solution.py:14
  19.0 0.0 copy-done.1
  19.0 1.9 %fusion.2 = f32[4,16,4096]{2,1,0:T(8,128)S(1)} fusion(f32[4,16,4096]{2,1,0:T(8,128)} %param.3, f32[4,16,4096]{2,1,0:T(8,128)S(1)} %copy-done.1, f32[4,16,64]{2,1,0:T(8,128)S(1)} %collective-permute-done.5, f32[4,16,64]{2,1,0:T(8,128)S(1)} %collective-permute-done.4, f32[4,1,4096]{2,1,0:T(1,128)S(1)} %collective-permute-done.3, ...), kind=kLoop, calls=%fused_computation.4 | loop fusion | flops 3670016 | bytes 3850240 | tf_op jit(solution)/shard_map/sub | solution.py:30
  20.9 0.8 %reshape.14 = f32[4096,64]{1,0:T(8,128)S(1)} reshape(f32[4,16,4096]{2,1,0:T(8,128)S(1)} %fusion.2) | data formatting | bytes 2097152 | tf_op jit(solution)/shard_map/reshape | solution.py:31
  21.7 3.6 %fusion.10 = f32[64,64]{1,0:T(8,128)S(1)} fusion(f32[4096,64]{1,0:T(8,128)S(1)} %reshape.14), kind=kOutput, calls=%fused_computation.22 | convolution fusion | flops 201326592 | bytes 1064960 | tf_op jit(solution)/shard_map/dot_general | solution.py:32
  25.3 40.4 %psum.7 = f32[64,64]{1,0:T(8,128)S(1)} all-reduce(f32[64,64]{1,0:T(8,128)S(1)} %fusion.10), channel_id=1, replica_groups=mesh['gz'=4,'gy'=4,'gx'=2] {'gz','gy','gx'}, use_global_device_ids=true, to_apply=%region_0.0 | all-reduce | flops 4096 | bytes 32768 | tf_op jit(solution)/shard_map/psum | solution.py:39
  65.8 0.0 copy-start
  65.8 0.8 %gather_fusion = f32[64]{0:T(128)S(1)} fusion(f32[64,64]{1,0:T(8,128)S(1)} %broadcast_multiply_fusion.1, s32[64]{0:T(128)S(1)} %or_bitcast_fusion), kind=kCustom, calls=%fused_computation | custom fusion | bytes 1024 | tf_op jit(solution)/shard_map/jit(diagonal)/cond/branch_0_fun/gather | solution.py:49
  66.6 0.1 mul.23
  66.7 1.1 %broadcast_multiply_fusion = f32[4,16,4096]{2,1,0:T(8,128)} fusion(f32[4,16,4096]{2,1,0:T(8,128)S(1)} %fusion.2, f32[4096]{0:T(1024)S(1)} %mul.23), kind=kLoop, calls=%fused_computation.14 | loop fusion | flops 262144 | bytes 2113536 | tf_op jit(solution)/shard_map/mul | solution.py:50
  67.7 0.0 copy-done
  (5 shorter events, 0.0 us)
Async XLA Ops:
  0.6 18.4 %copy-start.1 = (f32[4,16,4096]{2,1,0:T(8,128)S(1)}, f32[4,16,4096]{2,1,0:T(8,128)}, u32[]{:S(2)}) copy-start(f32[4,16,4096]{2,1,0:T(8,128)} %param.4) | copy-start | bytes 3145732
  1.8 14.1 %collective-permute-start = (f32[1,16,4096]{2,1,0:T(8,128)S(1)}, f32[1,16,4096]{2,1,0:T(8,128)S(1)}, u32[]{:S(2)}, u32[]{:S(2)}) collective-permute-start(f32[1,16,4096]{2,1,0:T(8,128)S(1)} %get-tuple-element.2), channel_id=1, source_target_pairs={{8,0},{16,8},{24,16},{0,24},{9,1},{17,9},{25,17},{1,25},{10,2},{18... | collective-permute-start | bytes 786440 | tf_op jit(solution)/shard_map/ppermute | solution.py:15
  6.9 12.1 %collective-permute-start.1 = (f32[1,16,4096]{2,1,0:T(8,128)S(1)}, f32[1,16,4096]{2,1,0:T(8,128)S(1)}, u32[]{:S(2)}, u32[]{:S(2)}) collective-permute-start(f32[1,16,4096]{2,1,0:T(8,128)S(1)} %get-tuple-element.3), channel_id=1, source_target_pairs={{0,8},{8,16},{16,24},{24,0},{1,9},{9,17},{17,25},{25,1},{2,10},{10... | collective-permute-start | bytes 786440 | tf_op jit(solution)/shard_map/ppermute | solution.py:14
  8.2 5.8 %collective-permute-start.2 = (f32[4,1,4096]{2,1,0:T(1,128)S(1)}, f32[4,1,4096]{2,1,0:T(1,128)S(1)}, u32[]{:S(2)}, u32[]{:S(2)}) collective-permute-start(f32[4,1,4096]{2,1,0:T(1,128)S(1)} %get-tuple-element.4), channel_id=1, source_target_pairs={{2,0},{4,2},{6,4},{0,6},{3,1},{5,3},{7,5},{1,7},{10,8},{12,10},{14... | collective-permute-start | bytes 196616 | tf_op jit(solution)/shard_map/ppermute | solution.py:15
  10.7 5.2 %collective-permute-start.3 = (f32[4,1,4096]{2,1,0:T(1,128)S(1)}, f32[4,1,4096]{2,1,0:T(1,128)S(1)}, u32[]{:S(2)}, u32[]{:S(2)}) collective-permute-start(f32[4,1,4096]{2,1,0:T(1,128)S(1)} %get-tuple-element.5), channel_id=1, source_target_pairs={{0,2},{2,4},{4,6},{6,0},{1,3},{3,5},{5,7},{7,1},{8,10},{10,12},{12... | collective-permute-start | bytes 196616 | tf_op jit(solution)/shard_map/ppermute | solution.py:14
  11.6 1.2 %collective-permute-start.4 = (f32[4,16,64]{2,1,0:T(8,128)S(1)}, f32[4,16,64]{2,1,0:T(8,128)S(1)}, u32[]{:S(2)}, u32[]{:S(2)}) collective-permute-start(f32[4,16,64]{2,1,0:T(8,128)S(1)} %get-tuple-element.6), channel_id=1, source_target_pairs={{1,0},{0,1},{3,2},{2,3},{5,4},{4,5},{7,6},{6,7},{9,8},{8,9},{11,10... | collective-permute-start | bytes 49160 | tf_op jit(solution)/shard_map/ppermute | solution.py:15
  12.8 1.2 %collective-permute-start.5 = (f32[4,16,64]{2,1,0:T(8,128)S(1)}, f32[4,16,64]{2,1,0:T(8,128)S(1)}, u32[]{:S(2)}, u32[]{:S(2)}) collective-permute-start(f32[4,16,64]{2,1,0:T(8,128)S(1)} %get-tuple-element.7), channel_id=1, source_target_pairs={{0,1},{1,0},{2,3},{3,2},{4,5},{5,4},{6,7},{7,6},{8,9},{9,8},{10,11... | collective-permute-start | bytes 49160 | tf_op jit(solution)/shard_map/ppermute | solution.py:14
  65.8 2.0 %copy-start = (f32[64,64]{1,0:T(8,128)}, f32[64,64]{1,0:T(8,128)S(1)}, u32[]{:S(2)}) copy-start(f32[64,64]{1,0:T(8,128)S(1)} %broadcast_multiply_fusion.1) | copy-start | bytes 49156
where the time goes:
time: 68.1 us; the launch traced here: 67.7 us
  blocking collectives  40.4 us (59%)
  starting transfers between devices  7.81 us (11%)
  waiting for transfers between devices  6.51 us (10%)
  local copies, waits for them, and re-layouts  5.11 us (8%)
  other arithmetic  3.6 us (5%)
  matrix products  3.57 us (5%)
  between operations  0.71 us (1%)
    psum x1, blocking collectives, local(): gram = lax.psum(partial_gram, ('gz', 'gy', 'gx'))  40.4 us
    ppermute x3, starting transfers between devices, padded(): after = lax.ppermute(initial, axis, down)  7.64 us
    ppermute x3, waiting for transfers between devices, padded(): before = lax.ppermute(last, axis, up)  5.97 us
    dot_general x1, matrix products, local(): lax.dot_general(flattened, flattened, (((0,), (0,)), ((), ())), precision...  3.57 us
    slice x3, local copies, waits for them, and re-layouts, padded(): initial = lax.slice_in_dim(array, 0, width, axis=dim)  3.29 us
    sub x1, other arithmetic, local(): resid = rhs - (centre * guess - neighbours)  1.87 us
  transfers between devices with their start and end apart: 6, of which 4 were waited for; matrix products, arithmetic and copies ran while one was open for 4% of the time, Pallas kernels for 0%

commit v1 on v0

v1 whole, which is shorter than its diff:
```python
import jax
import jax.numpy as jnp
from jax import lax
from jax.sharding import PartitionSpec as P

AXES = ("gz", "gy", "gx")


def ring(array, axis, step):
    peers = lax.axis_size(axis)
    return lax.ppermute(array, axis, [(i, (i + step) % peers) for i in range(peers)])


def halos(array, axis, dim, width):
    length = array.shape[dim]
    last = lax.slice_in_dim(array, length - width, length, axis=dim)
    initial = lax.slice_in_dim(array, 0, width, axis=dim)
    return ring(last, axis, 1), ring(initial, axis, -1)


def pair_halos(array, axis, dim, width):
    if lax.axis_size(axis) != 2:
        return halos(array, axis, dim, width)
    length = array.shape[dim]
    last = lax.slice_in_dim(array, length - width, length, axis=dim)
    initial = lax.slice_in_dim(array, 0, width, axis=dim)
    both = ring(jnp.concatenate([last, initial], axis=dim), axis, 1)
    return (
        lax.slice_in_dim(both, 0, width, axis=dim),
        lax.slice_in_dim(both, width, 2 * width, axis=dim),
    )


def masks_of(devices):
    masks = [1]
    while 2 ** len(masks) < devices:
        masks.append(2 ** len(masks) + 1)
    return masks


def sum_over_all(value):
    devices = lax.axis_size(AXES)
    for mask in masks_of(devices):
        value = value + lax.ppermute(value, AXES, [(i, i ^ mask) for i in range(devices)])
    return value


def local(rhs, guess, shifts):
    z_cells, y_cells, lane_count = guess.shape
    columns = shifts.shape[0]
    x_cells = lane_count // columns
    z_before, z_after = halos(guess, "gz", 0, 1)
    y_before, y_after = halos(guess, "gy", 1, 1)
    x_before, x_after = pair_halos(guess, "gx", 2, columns)
    z_padded = jnp.concatenate([z_before, guess, z_after], axis=0)
    y_padded = jnp.concatenate([y_before, guess, y_after], axis=1)
    x_padded = jnp.concatenate([x_before, guess, x_after], axis=2)
    neighbours = z_padded[2:] + z_padded[:-2] + y_padded[:, 2:] + y_padded[:, :-2]
    neighbours = neighbours + x_padded[:, :, 2 * columns :] + x_padded[:, :, : -2 * columns]
    centre = jnp.tile(6.0 + shifts, x_cells)
    resid = rhs - (centre * guess - neighbours)
    flattened = resid.reshape(-1, columns)
    partial_gram = lax.dot_general(
        flattened,
        flattened,
        (((0,), (0,)), ((), ())),
        precision=lax.Precision.HIGHEST,
        preferred_element_type=jnp.float32,
    )
    gram = sum_over_all(partial_gram)
    total_cells = z_cells * y_cells * x_cells * lax.axis_size(AXES)
    gram_mean = gram / jnp.float32(total_cells)
    diagonal = jnp.sum(gram_mean * jnp.eye(columns, dtype=jnp.float32), axis=0)
    inverse_norm = lax.rsqrt(diagonal + 1e-06)
    normalized = resid * jnp.tile(inverse_norm, x_cells)
    return (normalized, gram_mean)


def solution(mesh):
    placed = (P("gz", "gy", "gx"), P("gz", "gy", "gx"), P())
    return jax.shard_map(
        local, mesh=mesh, in_specs=placed, out_specs=(P("gz", "gy", "gx"), P()), check_vma=False
    )
```

time: 68.1 us -> 48 us (0.70)
  blocking collectives: 40.4 us -> 0 us
  waiting for transfers between devices: 6.51 us -> 22.6 us
  starting transfers between devices: 7.81 us -> 12.3 us
  local copies, waits for them, and re-layouts: 5.11 us -> 4.37 us
  other arithmetic: 3.6 us -> 4.29 us
    psum x1 -> x0, blocking collectives: 40.4 us -> none  [local(): gram = lax.psum(partial_gram, ('gz', 'gy', 'gx'))]
    ppermute x6 -> x10, waiting for transfers between devices: 6.51 us -> 22.6 us  [the longest x5 11.6 us: ring(): lax.ppermute(array, axis, [(i, (i + step) % peers) for i in range(peers)])]
    ppermute x6 -> x10, starting transfers between devices: 7.81 us -> 12.3 us  [the longest x5 7.66 us: ring(): lax.ppermute(array, axis, [(i, (i + step) % peers) for i in range(peers)])]
    gather x1 -> x0, local copies, waits for them, and re-layouts: 0.81 us -> none  [local(): inverse_norm = lax.rsqrt(jnp.diagonal(gram_mean) + 1e-06)]
    slice x3 -> x4, local copies, waits for them, and re-layouts: 3.29 us -> 3.37 us  [the longest x2 2.36 us: halos(): initial = lax.slice_in_dim(array, 0, width, axis=dim)]
  transfers between devices with their start and end apart: 6 -> 10, of which waited for: 4 -> 7; matrix products, arithmetic and copies ran while one was open for 4% -> 7% of each run, Pallas kernels for 0% -> 0%
where the time goes in v1:
time: 48 us; the launch traced here: 47.8 us
  waiting for transfers between devices  22.6 us (47%)
  starting transfers between devices  12.3 us (26%)
  local copies, waits for them, and re-layouts  4.37 us (9%)
  other arithmetic  4.29 us (9%)
  matrix products  3.58 us (7%)
  between operations  0.7 us (1%)
    ppermute x5, waiting for transfers between devices, ring(): lax.ppermute(array, axis, [(i, (i + step) % peers) for i in range(peers)])  11.6 us
    ppermute x5, waiting for transfers between devices, sum_over_all(): lax.ppermute(value, AXES, [(i, i ^ mask) for i in range(devices)])  10.9 us
    ppermute x5, starting transfers between devices, ring(): lax.ppermute(array, axis, [(i, (i + step) % peers) for i in range(peers)])  7.66 us
    ppermute x5, starting transfers between devices, sum_over_all(): lax.ppermute(value, AXES, [(i, i ^ mask) for i in range(devices)])  4.6 us
    dot_general x1, matrix products, local(): lax.dot_general(flattened, flattened, (((0,), (0,)), ((), ())), precision...  3.58 us
    slice x2, local copies, waits for them, and re-layouts, halos(): initial = lax.slice_in_dim(array, 0, width, axis=dim)  2.36 us
    sub x1, other arithmetic, local(): resid = rhs - (centre * guess - neighbours)  1.84 us
    mul x1, other arithmetic, local(): normalized = resid * jnp.tile(inverse_norm, x_cells)  1.06 us
  transfers between devices with their start and end apart: 10, of which 7 were waited for; matrix products, arithmetic and copies ran while one was open for 7% of the time, Pallas kernels for 0%

profile of v1, /device:TPU:0, one launch (start us, length us, event | category | flops | bytes accessed | tf_op | source)
XLA Modules:
  0.0 47.8 jit_solution(15978654800129597112)
XLA Ops:
  0.6 0.0 copy-start
  0.6 0.9 %fusion.9 = (f32[4,16,64]{2,1,0:T(8,128)S(1)}, f32[4,16,64]{2,1,0:T(8,128)S(1)}) fusion(f32[4,16,4096]{2,1,0:T(8,128)} %param.4), kind=kLoop, calls=%fused_computation.22 | loop fusion | bytes 65536 | tf_op jit(solution)/shard_map/slice | solution.py:25
  1.6 0.1 pad_maximum_fusion.6
  1.7 0.5 %collective-permute-start.4 = (f32[4,16,128]{2,1,0:T(8,128)S(1)}, f32[4,16,128]{2,1,0:T(8,128)S(1)}, u32[]{:S(2)}, u32[]{:S(2)}) collective-permute-start(f32[4,16,128]{2,1,0:T(8,128)S(1)} %pad_maximum_fusion.6), channel_id=1, source_target_pairs={{0,1},{1,0},{2,3},{3,2},{4,5},{5,4},{6,7},{7,6},{8,9},{9,8},{10,11... | collective-permute-start | bytes 98312 | tf_op jit(solution)/shard_map/ppermute | solution.py:11
  2.2 1.3 %fusion.8 = (f32[4,1,4096]{2,1,0:T(1,128)S(1)}, f32[4,1,4096]{2,1,0:T(1,128)S(1)}) fusion(f32[4,16,4096]{2,1,0:T(8,128)} %param.4), kind=kLoop, calls=%fused_computation.21 | loop fusion | bytes 262144 | tf_op jit(solution)/shard_map/slice | solution.py:17
  3.5 3.5 %collective-permute-start.2 = (f32[4,1,4096]{2,1,0:T(1,128)S(1)}, f32[4,1,4096]{2,1,0:T(1,128)S(1)}, u32[]{:S(2)}, u32[]{:S(2)}) collective-permute-start(f32[4,1,4096]{2,1,0:T(1,128)S(1)} %get-tuple-element.6), channel_id=1, source_target_pairs={{0,6},{2,0},{4,2},{6,4},{1,7},{3,1},{5,3},{7,5},{8,14},{10,8},{12,... | collective-permute-start | bytes 196616 | tf_op jit(solution)/shard_map/ppermute | solution.py:11
  7.0 0.0 collective-permute-start.3
  7.0 1.1 %fusion.7 = (f32[1,16,4096]{2,1,0:T(8,128)S(1)}, f32[1,16,4096]{2,1,0:T(8,128)S(1)}) fusion(f32[4,16,4096]{2,1,0:T(8,128)} %param.4), kind=kLoop, calls=%fused_computation.20 | loop fusion | bytes 1048576 | tf_op jit(solution)/shard_map/slice | solution.py:17
  8.0 3.7 %collective-permute-start = (f32[1,16,4096]{2,1,0:T(8,128)S(1)}, f32[1,16,4096]{2,1,0:T(8,128)S(1)}, u32[]{:S(2)}, u32[]{:S(2)}) collective-permute-start(f32[1,16,4096]{2,1,0:T(8,128)S(1)} %get-tuple-element.4), channel_id=1, source_target_pairs={{0,24},{8,0},{16,8},{24,16},{1,25},{9,1},{17,9},{25,17},{2,26},{10... | collective-permute-start | bytes 786440 | tf_op jit(solution)/shard_map/ppermute | solution.py:11
  11.7 0.0 collective-permute-start.1
  11.7 0.7 %broadcast_add_fusion = f32[64]{0:T(128)S(1)} fusion(f32[64]{0:T(128)} %param.5), kind=kLoop, calls=%fused_computation.19 | loop fusion | flops 64 | bytes 512 | tf_op jit(solution)/shard_map/add | solution.py:60
  12.3 0.1 mul.23
  12.4 0.0 collective-permute-done.4
  12.4 0.1 fusion.10
  12.5 0.0 collective-permute-done.2
  12.5 0.0 collective-permute-done.3
  12.5 5.9 %collective-permute-done = f32[1,16,4096]{2,1,0:T(8,128)S(1)} collective-permute-done((f32[1,16,4096]{2,1,0:T(8,128)S(1)}, f32[1,16,4096]{2,1,0:T(8,128)S(1)}, u32[]{:S(2)}, u32[]{:S(2)}) %collective-permute-start) | collective-permute-done | bytes 262176 | tf_op jit(solution)/shard_map/ppermute | solution.py:11
  18.4 5.7 %collective-permute-done.1 = f32[1,16,4096]{2,1,0:T(8,128)S(1)} collective-permute-done((f32[1,16,4096]{2,1,0:T(8,128)S(1)}, f32[1,16,4096]{2,1,0:T(8,128)S(1)}, u32[]{:S(2)}, u32[]{:S(2)}) %collective-permute-start.1) | collective-permute-done | bytes 262176 | tf_op jit(solution)/shard_map/ppermute | solution.py:11
  24.1 0.0 copy-done
  24.1 1.8 %fusion.2 = f32[4,16,4096]{2,1,0:T(8,128)S(1)} fusion(f32[4,16,4096]{2,1,0:T(8,128)} %param.3, f32[4,16,4096]{2,1,0:T(8,128)S(1)} %copy-done, f32[4,16,64]{2,1,0:T(8,128)S(1)} %get-tuple-element.11, f32[4,16,64]{2,1,0:T(8,128)S(1)} %get-tuple-element.10, f32[4,1,4096]{2,1,0:T(1,128)S(1)} %collective-permute-done.3, ...), kind=kLoop, calls=%fused_computation.3 | loop fusion | flops 3670016 | bytes 3850240 | tf_op jit(solution)/shard_map/sub | solution.py:61
  26.0 0.8 %reshape.14 = f32[4096,64]{1,0:T(8,128)S(1)} reshape(f32[4,16,4096]{2,1,0:T(8,128)S(1)} %fusion.2) | data formatting | bytes 2097152 | tf_op jit(solution)/shard_map/reshape | solution.py:62
  26.8 3.6 %fusion.11 = f32[64,64]{1,0:T(8,128)S(1)} fusion(f32[4096,64]{1,0:T(8,128)S(1)} %reshape.14), kind=kOutput, calls=%fused_computation.24 | convolution fusion | flops 201326592 | bytes 1064960 | tf_op jit(solution)/shard_map/dot_general | solution.py:63
  30.4 0.1 collective-permute-start.5
  30.5 1.2 %collective-permute-done.5 = f32[64,64]{1,0:T(8,128)S(1)} collective-permute-done((f32[64,64]{1,0:T(8,128)S(1)}, f32[64,64]{1,0:T(8,128)S(1)}, u32[]{:S(2)}, u32[]{:S(2)}) %collective-permute-start.5) | collective-permute-done | bytes 16416 | tf_op jit(solution)/shard_map/ppermute | solution.py:44
  31.7 1.4 %collective-permute-start.6 = (f32[64,64]{1,0:T(8,128)S(1)}, f32[64,64]{1,0:T(8,128)S(1)}, u32[]{:S(2)}, u32[]{:S(2)}) collective-permute-start(f32[64,64]{1,0:T(8,128)S(1)} %add.53), channel_id=1, source_target_pairs={{0,3},{1,2},{2,1},{3,0},{4,7},{5,6},{6,5},{7,4},{8,11},{9,10},{10,... | collective-permute-start | bytes 49160 | tf_op jit(solution)/shard_map/ppermute | solution.py:44
  33.2 1.9 %collective-permute-done.6 = f32[64,64]{1,0:T(8,128)S(1)} collective-permute-done((f32[64,64]{1,0:T(8,128)S(1)}, f32[64,64]{1,0:T(8,128)S(1)}, u32[]{:S(2)}, u32[]{:S(2)}) %collective-permute-start.6) | collective-permute-done | bytes 16416 | tf_op jit(solution)/shard_map/ppermute | solution.py:44
  35.1 1.2 %collective-permute-start.7 = (f32[64,64]{1,0:T(8,128)S(1)}, f32[64,64]{1,0:T(8,128)S(1)}, u32[]{:S(2)}, u32[]{:S(2)}) collective-permute-start(f32[64,64]{1,0:T(8,128)S(1)} %add.54), channel_id=1, source_target_pairs={{0,5},{1,4},{2,7},{3,6},{4,1},{5,0},{6,3},{7,2},{8,13},{9,12},{10,... | collective-permute-start | bytes 49160 | tf_op jit(solution)/shard_map/ppermute | solution.py:44
  36.2 2.2 %collective-permute-done.7 = f32[64,64]{1,0:T(8,128)S(1)} collective-permute-done((f32[64,64]{1,0:T(8,128)S(1)}, f32[64,64]{1,0:T(8,128)S(1)}, u32[]{:S(2)}, u32[]{:S(2)}) %collective-permute-start.7) | collective-permute-done | bytes 16416 | tf_op jit(solution)/shard_map/ppermute | solution.py:44
  38.4 1.4 %collective-permute-start.8 = (f32[64,64]{1,0:T(8,128)S(1)}, f32[64,64]{1,0:T(8,128)S(1)}, u32[]{:S(2)}, u32[]{:S(2)}) collective-permute-start(f32[64,64]{1,0:T(8,128)S(1)} %add.55), channel_id=1, source_target_pairs={{0,9},{1,8},{2,11},{3,10},{4,13},{5,12},{6,15},{7,14},{8,1},{9,0},... | collective-permute-start | bytes 49160 | tf_op jit(solution)/shard_map/ppermute | solution.py:44
  39.8 1.9 %collective-permute-done.8 = f32[64,64]{1,0:T(8,128)S(1)} collective-permute-done((f32[64,64]{1,0:T(8,128)S(1)}, f32[64,64]{1,0:T(8,128)S(1)}, u32[]{:S(2)}, u32[]{:S(2)}) %collective-permute-start.8) | collective-permute-done | bytes 16416 | tf_op jit(solution)/shard_map/ppermute | solution.py:44
  41.8 0.5 %collective-permute-start.9 = (f32[64,64]{1,0:T(8,128)S(1)}, f32[64,64]{1,0:T(8,128)S(1)}, u32[]{:S(2)}, u32[]{:S(2)}) collective-permute-start(f32[64,64]{1,0:T(8,128)S(1)} %add.56), channel_id=1, source_target_pairs={{0,17},{1,16},{2,19},{3,18},{4,21},{5,20},{6,23},{7,22},{8,25},{9,... | collective-permute-start | bytes 49160 | tf_op jit(solution)/shard_map/ppermute | solution.py:44
  42.3 3.7 %collective-permute-done.9 = f32[64,64]{1,0:T(8,128)S(1)} collective-permute-done((f32[64,64]{1,0:T(8,128)S(1)}, f32[64,64]{1,0:T(8,128)S(1)}, u32[]{:S(2)}, u32[]{:S(2)}) %collective-permute-start.9) | collective-permute-done | bytes 16416 | tf_op jit(solution)/shard_map/ppermute | solution.py:44
  46.0 0.6 %select_reduce_fusion = (f32[64]{0:T(128)S(1)}, f32[64,64]{1,0:T(8,128)}) fusion(f32[64,64]{1,0:T(8,128)S(1)} %add.56, f32[64,64]{1,0:T(8,128)S(1)} %collective-permute-done.9), kind=kLoop, calls=%fused_computation.15 | loop fusion | flops 20416 | bytes 49408 | tf_op jit(solution)/shard_map/reduce_sum | solution.py:73
  46.6 0.1 mul.27
  46.7 1.1 %broadcast_multiply_fusion = f32[4,16,4096]{2,1,0:T(8,128)} fusion(f32[4,16,4096]{2,1,0:T(8,128)S(1)} %fusion.2, f32[4096]{0:T(1024)S(1)} %mul.27), kind=kLoop, calls=%fused_computation.13 | loop fusion | flops 262144 | bytes 2113536 | tf_op jit(solution)/shard_map/mul | solution.py:75
  (7 shorter events, 0.0 us)
Async XLA Ops:
  0.6 23.5 %copy-start = (f32[4,16,4096]{2,1,0:T(8,128)S(1)}, f32[4,16,4096]{2,1,0:T(8,128)}, u32[]{:S(2)}) copy-start(f32[4,16,4096]{2,1,0:T(8,128)} %param.4) | copy-start | bytes 3145732
  1.7 10.8 %collective-permute-start.4 = (f32[4,16,128]{2,1,0:T(8,128)S(1)}, f32[4,16,128]{2,1,0:T(8,128)S(1)}, u32[]{:S(2)}, u32[]{:S(2)}) collective-permute-start(f32[4,16,128]{2,1,0:T(8,128)S(1)} %pad_maximum_fusion.6), channel_id=1, source_target_pairs={{0,1},{1,0},{2,3},{3,2},{4,5},{5,4},{6,7},{7,6},{8,9},{9,8},{10,11... | collective-permute-start | bytes 98312 | tf_op jit(solution)/shard_map/ppermute | solution.py:11
  3.5 9.1 %collective-permute-start.2 = (f32[4,1,4096]{2,1,0:T(1,128)S(1)}, f32[4,1,4096]{2,1,0:T(1,128)S(1)}, u32[]{:S(2)}, u32[]{:S(2)}) collective-permute-start(f32[4,1,4096]{2,1,0:T(1,128)S(1)} %get-tuple-element.6), channel_id=1, source_target_pairs={{0,6},{2,0},{4,2},{6,4},{1,7},{3,1},{5,3},{7,5},{8,14},{10,8},{12,... | collective-permute-start | bytes 196616 | tf_op jit(solution)/shard_map/ppermute | solution.py:11
  7.0 5.6 %collective-permute-start.3 = (f32[4,1,4096]{2,1,0:T(1,128)S(1)}, f32[4,1,4096]{2,1,0:T(1,128)S(1)}, u32[]{:S(2)}, u32[]{:S(2)}) collective-permute-start(f32[4,1,4096]{2,1,0:T(1,128)S(1)} %get-tuple-element.7), channel_id=1, source_target_pairs={{0,2},{2,4},{4,6},{6,0},{1,3},{3,5},{5,7},{7,1},{8,10},{10,12},{12... | collective-permute-start | bytes 196616 | tf_op jit(solution)/shard_map/ppermute | solution.py:11
  8.0 10.4 %collective-permute-start = (f32[1,16,4096]{2,1,0:T(8,128)S(1)}, f32[1,16,4096]{2,1,0:T(8,128)S(1)}, u32[]{:S(2)}, u32[]{:S(2)}) collective-permute-start(f32[1,16,4096]{2,1,0:T(8,128)S(1)} %get-tuple-element.4), channel_id=1, source_target_pairs={{0,24},{8,0},{16,8},{24,16},{1,25},{9,1},{17,9},{25,17},{2,26},{10... | collective-permute-start | bytes 786440 | tf_op jit(solution)/shard_map/ppermute | solution.py:11
  11.7 12.5 %collective-permute-start.1 = (f32[1,16,4096]{2,1,0:T(8,128)S(1)}, f32[1,16,4096]{2,1,0:T(8,128)S(1)}, u32[]{:S(2)}, u32[]{:S(2)}) collective-permute-start(f32[1,16,4096]{2,1,0:T(8,128)S(1)} %get-tuple-element.5), channel_id=1, source_target_pairs={{0,8},{8,16},{16,24},{24,0},{1,9},{9,17},{17,25},{25,1},{2,10},{10... | collective-permute-start | bytes 786440 | tf_op jit(solution)/shard_map/ppermute | solution.py:11
  30.4 1.3 %collective-permute-start.5 = (f32[64,64]{1,0:T(8,128)S(1)}, f32[64,64]{1,0:T(8,128)S(1)}, u32[]{:S(2)}, u32[]{:S(2)}) collective-permute-start(f32[64,64]{1,0:T(8,128)S(1)} %fusion.11), channel_id=1, source_target_pairs={{0,1},{1,0},{2,3},{3,2},{4,5},{5,4},{6,7},{7,6},{8,9},{9,8},{10,11... | collective-permute-start | bytes 49160 | tf_op jit(solution)/shard_map/ppermute | solution.py:44
  31.7 3.3 %collective-permute-start.6 = (f32[64,64]{1,0:T(8,128)S(1)}, f32[64,64]{1,0:T(8,128)S(1)}, u32[]{:S(2)}, u32[]{:S(2)}) collective-permute-start(f32[64,64]{1,0:T(8,128)S(1)} %add.53), channel_id=1, source_target_pairs={{0,3},{1,2},{2,1},{3,0},{4,7},{5,6},{6,5},{7,4},{8,11},{9,10},{10,... | collective-permute-start | bytes 49160 | tf_op jit(solution)/shard_map/ppermute | solution.py:44
  35.1 3.3 %collective-permute-start.7 = (f32[64,64]{1,0:T(8,128)S(1)}, f32[64,64]{1,0:T(8,128)S(1)}, u32[]{:S(2)}, u32[]{:S(2)}) collective-permute-start(f32[64,64]{1,0:T(8,128)S(1)} %add.54), channel_id=1, source_target_pairs={{0,5},{1,4},{2,7},{3,6},{4,1},{5,0},{6,3},{7,2},{8,13},{9,12},{10,... | collective-permute-start | bytes 49160 | tf_op jit(solution)/shard_map/ppermute | solution.py:44
  38.4 3.3 %collective-permute-start.8 = (f32[64,64]{1,0:T(8,128)S(1)}, f32[64,64]{1,0:T(8,128)S(1)}, u32[]{:S(2)}, u32[]{:S(2)}) collective-permute-start(f32[64,64]{1,0:T(8,128)S(1)} %add.55), channel_id=1, source_target_pairs={{0,9},{1,8},{2,11},{3,10},{4,13},{5,12},{6,15},{7,14},{8,1},{9,0},... | collective-permute-start | bytes 49160 | tf_op jit(solution)/shard_map/ppermute | solution.py:44
  41.8 4.2 %collective-permute-start.9 = (f32[64,64]{1,0:T(8,128)S(1)}, f32[64,64]{1,0:T(8,128)S(1)}, u32[]{:S(2)}, u32[]{:S(2)}) collective-permute-start(f32[64,64]{1,0:T(8,128)S(1)} %add.56), channel_id=1, source_target_pairs={{0,17},{1,16},{2,19},{3,18},{4,21},{5,20},{6,23},{7,22},{8,25},{9,... | collective-permute-start | bytes 49160 | tf_op jit(solution)/shard_map/ppermute | solution.py:44

commit v2 on v1

v2 whole, which is shorter than its diff:
```python
import functools

import jax
import jax.numpy as jnp
from jax import lax
from jax.experimental import pallas as pl
from jax.experimental.pallas import tpu as pltpu
from jax.sharding import PartitionSpec as P


AXES = ("gz", "gy", "gx")
LANES = 128
VMEM = pl.BlockSpec(memory_space=pltpu.VMEM)


def ring(array, axis, step):
    peers = lax.axis_size(axis)
    return lax.ppermute(array, axis, [(i, (i + step) % peers) for i in range(peers)])


def faces(array, dim, width):
    length = array.shape[dim]
    last = lax.slice_in_dim(array, length - width, length, axis=dim)
    initial = lax.slice_in_dim(array, 0, width, axis=dim)
    return last, initial


def masks_of(devices):
    masks = [1]
    while 2 ** len(masks) < devices:
        masks.append(2 ** len(masks) + 1)
    return masks


def sum_over_all(value):
    devices = lax.axis_size(AXES)
    for mask in masks_of(devices):
        value = value + lax.ppermute(value, AXES, [(i, i ^ mask) for i in range(devices)])
    return value


def half_roll(tile):
    return pltpu.roll(tile, LANES // 2, axis=1)


def split_gram(tiles):
    block = jnp.concatenate(tiles, axis=0)
    hi = block.astype(jnp.bfloat16)
    lo = (block - hi.astype(jnp.float32)).astype(jnp.bfloat16)
    return lax.dot_general(
        hi,
        jnp.concatenate([hi, lo], axis=1),
        (((0,), (0,)), ((), ())),
        preferred_element_type=jnp.float32,
    )


def early(g_ref, b_ref, c_ref, yb_ref, ya_ref, xh_ref, l_ref, gram_ref):
    planes, rows, width = g_ref.shape
    chunks = width // LANES
    row = lax.broadcasted_iota(jnp.int32, (rows, LANES), 0)
    low = lax.broadcasted_iota(jnp.int32, (rows, LANES), 1) < LANES // 2
    centre = jnp.broadcast_to(c_ref[...], (rows, LANES))
    gram_ref[...] = jnp.zeros_like(gram_ref)

    def plane(z):
        xh = xh_ref[z]
        before, here = xh, half_roll(g_ref[z, :, pl.ds(0, LANES)])
        tiles = []
        for t in range(chunks):
            at = pl.ds(t * LANES, LANES)
            after = half_roll(g_ref[z, :, pl.ds((t + 1) * LANES, LANES)]) if t + 1 < chunks else xh
            x = g_ref[z, :, at]
            near = here + jnp.where(low, before, after)
            up = jnp.where(row == 0, yb_ref[z, :, at], pltpu.roll(x, 1, axis=0))
            down = jnp.where(row == rows - 1, ya_ref[z, :, at], pltpu.roll(x, rows - 1, axis=0))
            near = near + (up + down)
            if z > 0:
                near = near + g_ref[z - 1, :, at]
            if z < planes - 1:
                near = near + g_ref[z + 1, :, at]
            left = b_ref[z, :, at] - (centre * x - near)
            l_ref[z, :, at] = left
            tiles.append(left)
            before, here = here, after
        if 0 < z < planes - 1:
            gram_ref[...] += split_gram(tiles)

    for z in range(planes):
        plane(z)


def pack_gram(split):
    half, quarter = LANES // 2, LANES // 4
    hh, hl = split[:, :LANES], split[:, LANES:]
    full = hh + hl + hl.T
    low = lax.broadcasted_iota(jnp.int32, (quarter, LANES), 1) < half
    first = jnp.where(low, full[:quarter], half_roll(full[quarter:half]))
    second = jnp.where(
        low, half_roll(full[half : half + quarter]), full[half + quarter :]
    )
    return first + second


def late(l_ref, zb_ref, za_ref, g_ref, r_ref, p_ref):
    planes, _, width = l_ref.shape
    tiles = []
    for i, z, h_ref in ((0, 0, zb_ref), (1, planes - 1, za_ref)):
        for t in range(width // LANES):
            at = pl.ds(t * LANES, LANES)
            value = l_ref[z, :, at] + h_ref[0, :, at]
            r_ref[i, :, at] = value
            tiles.append(value)
    p_ref[...] = pack_gram(g_ref[...] + split_gram(tiles))


def final(cells, p_ref, l_ref, r_ref, n_ref, m_ref, buf, sem):
    planes, rows, width = l_ref.shape
    half, quarter = LANES // 2, LANES // 4
    mean = p_ref[...] / jnp.float32(cells)
    row = lax.broadcasted_iota(jnp.int32, (quarter, LANES), 0)
    lane = lax.broadcasted_iota(jnp.int32, (quarter, LANES), 1)
    own = (lane == row) | (lane == row + half + quarter)
    diagonal = jnp.sum(jnp.where(own, mean, 0.0), axis=0, keepdims=True)
    diagonal = diagonal + half_roll(diagonal)
    scale = jnp.broadcast_to(lax.rsqrt(diagonal + 1e-06), (rows, LANES))
    copies = []
    for z in range(planes):
        source = r_ref.at[0] if z == 0 else r_ref.at[1] if z == planes - 1 else l_ref.at[z]
        for t in range(width // LANES):
            at = pl.ds(t * LANES, LANES)
            buf[z, :, at] = source[:, at] * scale
        copy = pltpu.make_async_copy(buf.at[z], n_ref.at[z], sem.at[z])
        copy.start()
        copies.append(copy)
    m_ref[pl.ds(0, quarter), :] = mean[:, :half]
    m_ref[pl.ds(quarter, quarter), :] = half_roll(mean)[:, :half]
    for copy in copies:
        copy.wait()


def call(body, outs, cost, **kwargs):
    return pl.pallas_call(
        body,
        out_shape=outs,
        cost_estimate=pl.CostEstimate(flops=cost, bytes_accessed=1 << 20, transcendentals=0),
        compiler_params=pltpu.CompilerParams(vmem_limit_bytes=16 << 20),
        **kwargs,
    )


def local(rhs, guess, shifts):
    z_cells, y_cells, lane_count = guess.shape
    columns = shifts.shape[0]
    x_cells = lane_count // columns
    f32 = jnp.float32
    last, initial = faces(guess, 0, 1)
    z_before = ring(last, "gz", 1)
    z_after = ring(initial, "gz", -1)
    last, initial = faces(guess, 1, 1)
    y_before = ring(last, "gy", 1)
    y_after = ring(initial, "gy", -1)
    last, initial = faces(guess, 2, columns)
    if lax.axis_size("gx") == 2:
        x_halos = ring(jnp.concatenate([last, initial], axis=2), "gx", 1)
    else:
        x_halos = jnp.concatenate(
            [ring(last, "gx", 1), ring(initial, "gx", -1)], axis=2
        )
    centre = jnp.tile(6.0 + shifts, LANES // columns)[None]
    left, inner = call(
        early,
        (
            jax.ShapeDtypeStruct(guess.shape, f32),
            jax.ShapeDtypeStruct((LANES, 2 * LANES), f32),
        ),
        1 << 24,
        in_specs=[VMEM] * 6,
        out_specs=[VMEM] * 2,
    )(guess, rhs, centre, y_before, y_after, x_halos)
    outer, packed = call(
        late,
        (
            jax.ShapeDtypeStruct((2, y_cells, lane_count), f32),
            jax.ShapeDtypeStruct((columns // 2, LANES), f32),
        ),
        1 << 24,
        in_specs=[VMEM] * 4,
        out_specs=[VMEM] * 2,
    )(left, z_before, z_after, inner)
    packed = sum_over_all(packed)
    total_cells = z_cells * y_cells * x_cells * lax.axis_size(AXES)
    return call(
        functools.partial(final, total_cells),
        (
            jax.ShapeDtypeStruct(guess.shape, f32),
            jax.ShapeDtypeStruct((columns, columns), f32),
        ),
        1 << 22,
        in_specs=[VMEM] * 3,
        out_specs=[pl.BlockSpec(memory_space=pl.ANY), VMEM],
        scratch_shapes=[
            pltpu.VMEM(guess.shape, f32),
            pltpu.SemaphoreType.DMA((z_cells,)),
        ],
    )(packed, left, outer)


def solution(mesh):
    placed = (P("gz", "gy", "gx"), P("gz", "gy", "gx"), P())
    return jax.shard_map(
        local, mesh=mesh, in_specs=placed, out_specs=(P("gz", "gy", "gx"), P()), check_vma=False
    )
```

time: 48 us -> 37.8 us (0.79)
  other arithmetic: 4.29 us -> 0.1 us
  waiting for transfers between devices: 22.6 us -> 18.5 us
  matrix products: 3.58 us -> 0 us
  Pallas kernels: 0 us -> 2.76 us
  local copies, waits for them, and re-layouts: 4.37 us -> 3.42 us
    dot_general x1 -> x0, matrix products: 3.58 us -> none  [local(): lax.dot_general(flattened, flattened, (((0,), (0,)), ((), ())), precision...]
    ppermute x5, waiting for transfers between devices: 11.6 us -> 8.18 us  [ring(): lax.ppermute(array, axis, [(i, (i + step) % peers) for i in range(peers)])]
    pallas_call x0 -> x3, Pallas kernels: none -> 2.76 us  [the longest x1 1.72 us: local(): call(functools.partial(final, total_cells), (jax.ShapeDtypeStruct(guess.s...]
    sub x1 -> x0, other arithmetic: 1.84 us -> none  [local(): resid = rhs - (centre * guess - neighbours)]
    slice x4 -> x3, local copies, waits for them, and re-layouts: 3.37 us -> 2.09 us  [the longest x2 1.16 us: faces(): initial = lax.slice_in_dim(array, 0, width, axis=dim)]
    unnamed x2 -> x6, local copies, waits for them, and re-layouts: 0.01 us -> 1.24 us
    mul x1 -> x0, other arithmetic: 1.06 us -> none  [local(): normalized = resid * jnp.tile(inverse_norm, x_cells)]
    reshape x1 -> x0, local copies, waits for them, and re-layouts: 0.83 us -> none  [local(): flattened = resid.reshape(-1, columns)]
  transfers between devices with their start and end apart: 10 -> 10, of which waited for: 7 -> 8; matrix products, arithmetic and copies ran while one was open for 7% -> 3% of each run, Pallas kernels for 0% -> 2%
where the time goes in v2:
time: 37.8 us; the launch traced here: 37.6 us
  waiting for transfers between devices  18.5 us (49%)
  starting transfers between devices  12.2 us (32%)
  local copies, waits for them, and re-layouts  3.42 us (9%)
  Pallas kernels  2.76 us (7%)
  between operations  0.71 us (2%)
    ppermute x5, waiting for transfers between devices, sum_over_all(): lax.ppermute(value, AXES, [(i, i ^ mask) for i in range(devices)])  10.3 us
    ppermute x5, waiting for transfers between devices, ring(): lax.ppermute(array, axis, [(i, (i + step) % peers) for i in range(peers)])  8.18 us
    ppermute x5, starting transfers between devices, ring(): lax.ppermute(array, axis, [(i, (i + step) % peers) for i in range(peers)])  7.66 us
    ppermute x5, starting transfers between devices, sum_over_all(): lax.ppermute(value, AXES, [(i, i ^ mask) for i in range(devices)])  4.51 us
    pallas_call x1, Pallas kernels, local(): call(functools.partial(final, total_cells), (jax.ShapeDtypeStruct(guess.s...  1.72 us
    unnamed x6, local copies, waits for them, and re-layouts  1.24 us
    slice x2, local copies, waits for them, and re-layouts, faces(): initial = lax.slice_in_dim(array, 0, width, axis=dim)  1.16 us
    slice x1, local copies, waits for them, and re-layouts, faces(): last = lax.slice_in_dim(array, length - width, length, axis=dim)  0.94 us
  transfers between devices with their start and end apart: 10, of which 8 were waited for; matrix products, arithmetic and copies ran while one was open for 3% of the time, Pallas kernels for 2%

profile of v2, /device:TPU:0, one launch (start us, length us, event | category | flops | bytes accessed | tf_op | source)
XLA Modules:
  0.0 37.6 jit_solution(12067941549537819920)
XLA Ops:
  0.6 0.0 copy-start
  0.6 0.9 %fusion.1 = (f32[4,16,64]{2,1,0:T(8,128)S(1)}, f32[4,16,64]{2,1,0:T(8,128)S(1)}) fusion(f32[4,16,4096]{2,1,0:T(8,128)} %g_ref.1), kind=kLoop, calls=%fused_computation.3 | loop fusion | bytes 65536 | tf_op jit(solution)/shard_map/slice | solution.py:23
  1.6 0.1 pad_maximum_fusion
  1.7 0.5 %collective-permute-start.2 = (f32[4,16,128]{2,1,0:T(8,128)S(1)}, f32[4,16,128]{2,1,0:T(8,128)S(1)}, u32[]{:S(2)}, u32[]{:S(2)}) collective-permute-start(f32[4,16,128]{2,1,0:T(8,128)S(1)} %pad_maximum_fusion), channel_id=1, source_target_pairs={{0,1},{1,0},{2,3},{3,2},{4,5},{5,4},{6,7},{7,6},{8,9},{9,8},{10,11... | collective-permute-start | bytes 98312 | tf_op jit(solution)/shard_map/ppermute | solution.py:18
  2.2 1.1 %fusion = (f32[1,16,4096]{2,1,0:T(8,128)S(1)}, f32[1,16,4096]{2,1,0:T(8,128)S(1)}) fusion(f32[4,16,4096]{2,1,0:T(8,128)} %g_ref.1), kind=kLoop, calls=%fused_computation.2 | loop fusion | bytes 1048576 | tf_op jit(solution)/shard_map/slice | solution.py:24
  3.2 4.7 %collective-permute-start.4 = (f32[1,16,4096]{2,1,0:T(8,128)S(1)}, f32[1,16,4096]{2,1,0:T(8,128)S(1)}, u32[]{:S(2)}, u32[]{:S(2)}) collective-permute-start(f32[1,16,4096]{2,1,0:T(8,128)S(1)} %get-tuple-element.10), channel_id=1, source_target_pairs={{0,24},{8,0},{16,8},{24,16},{1,25},{9,1},{17,9},{25,17},{2,26},{10... | collective-permute-start | bytes 786440 | tf_op jit(solution)/shard_map/ppermute | solution.py:18
  7.9 0.0 collective-permute-start.3
  7.9 0.0 copy-done
  7.9 0.1 fusion.2
  8.0 0.0 copy-start.2
  8.0 2.5 %collective-permute-start.1 = (f32[4,1,4096]{2,1,0:T(1,128)S(1)}, f32[4,1,4096]{2,1,0:T(1,128)S(1)}, u32[]{:S(2)}, u32[]{:S(2)}) collective-permute-start(f32[4,1,4096]{2,1,0:T(1,128)S(1)} %get-tuple-element.14), channel_id=1, source_target_pairs={{0,6},{2,0},{4,2},{6,4},{1,7},{3,1},{5,3},{7,5},{8,14},{10,8},{12,... | collective-permute-start | bytes 196616 | tf_op jit(solution)/shard_map/ppermute | solution.py:18
  10.5 0.0 collective-permute-start
  10.5 0.0 copy-done.2
  10.5 0.1 broadcast_in_dim_tile.3.c_ref
  10.6 0.0 collective-permute-done.2.xh_ref
  10.6 2.4 %collective-permute-done.1.ya_ref = f32[4,1,4096]{2,1,0:T(1,128)S(1)} collective-permute-done((f32[4,1,4096]{2,1,0:T(1,128)S(1)}, f32[4,1,4096]{2,1,0:T(1,128)S(1)}, u32[]{:S(2)}, u32[]{:S(2)}) %collective-permute-start.1) | collective-permute-done | bytes 65568 | tf_op jit(solution)/shard_map/ppermute | solution.py:18
  13.0 2.7 %collective-permute-done.yb_ref = f32[4,1,4096]{2,1,0:T(1,128)S(1)} collective-permute-done((f32[4,1,4096]{2,1,0:T(1,128)S(1)}, f32[4,1,4096]{2,1,0:T(1,128)S(1)}, u32[]{:S(2)}, u32[]{:S(2)}) %collective-permute-start) | collective-permute-done | bytes 65568 | tf_op jit(solution)/shard_map/ppermute | solution.py:18
  15.7 0.0 copy-start.1
  15.7 1.2 %copy-done.1 = f32[4,16,4096]{2,1,0:T(8,128)S(1)} copy-done((f32[4,16,4096]{2,1,0:T(8,128)S(1)}, f32[4,16,4096]{2,1,0:T(8,128)}, u32[]{:S(2)}) %copy-start.1) | copy-done | bytes 1048600
  16.9 0.6 %shard_map.50 = (f32[4,16,4096]{2,1,0:T(8,128)S(1)}, f32[128,256]{1,0:T(8,128)S(1)}) custom-call(f32[4,16,4096]{2,1,0:T(8,128)S(1)} %copy-done, f32[4,16,4096]{2,1,0:T(8,128)S(1)} %copy-done.1, f32[1,128]{1,0:T(1,128)S(1)} %broadcast_in_dim_tile.3.c_ref, f32[4,1,4096]{2,1,0:T(1,128)S(1)} %collective-permute-done.yb_ref, ...), custom_call_target="tpu_custom_call" | custom-call | flops 16777216 | bytes 1048576 | tf_op jit(solution)/shard_map/pallas_call | solution.py:171
  17.5 0.0 collective-permute-done.4.za_ref
  17.5 3.1 %collective-permute-done.3.zb_ref = f32[1,16,4096]{2,1,0:T(8,128)S(1)} collective-permute-done((f32[1,16,4096]{2,1,0:T(8,128)S(1)}, f32[1,16,4096]{2,1,0:T(8,128)S(1)}, u32[]{:S(2)}, u32[]{:S(2)}) %collective-permute-start.3) | collective-permute-done | bytes 262176 | tf_op jit(solution)/shard_map/ppermute | solution.py:18
  20.6 0.4 %shard_map.51 = (f32[2,16,4096]{2,1,0:T(8,128)S(1)}, f32[32,128]{1,0:T(8,128)S(1)}) custom-call(f32[4,16,4096]{2,1,0:T(8,128)S(1)} %get-tuple-element.6.l_ref, f32[1,16,4096]{2,1,0:T(8,128)S(1)} %collective-permute-done.3.zb_ref, f32[1,16,4096]{2,1,0:T(8,128)S(1)} %collective-permute-done.4.za_ref, f32[128,256]{1,0:T(8,128)S(1)} %get-tuple-element.7.g_ref), custom_call_target="tpu_custom_call" | custom-call | flops 16777216 | bytes 1048576 | tf_op jit(solution)/shard_map/pallas_call | solution.py:181
  21.1 0.1 collective-permute-start.5
  21.1 1.2 %collective-permute-done.5 = f32[32,128]{1,0:T(8,128)S(1)} collective-permute-done((f32[32,128]{1,0:T(8,128)S(1)}, f32[32,128]{1,0:T(8,128)S(1)}, u32[]{:S(2)}, u32[]{:S(2)}) %collective-permute-start.5) | collective-permute-done | bytes 16416 | tf_op jit(solution)/shard_map/ppermute | solution.py:38
  22.3 1.3 %collective-permute-start.6 = (f32[32,128]{1,0:T(8,128)S(1)}, f32[32,128]{1,0:T(8,128)S(1)}, u32[]{:S(2)}, u32[]{:S(2)}) collective-permute-start(f32[32,128]{1,0:T(8,128)S(1)} %add.23), channel_id=1, source_target_pairs={{0,3},{1,2},{2,1},{3,0},{4,7},{5,6},{6,5},{7,4},{8,11},{9,10},{10,... | collective-permute-start | bytes 49160 | tf_op jit(solution)/shard_map/ppermute | solution.py:38
  23.6 1.9 %collective-permute-done.6 = f32[32,128]{1,0:T(8,128)S(1)} collective-permute-done((f32[32,128]{1,0:T(8,128)S(1)}, f32[32,128]{1,0:T(8,128)S(1)}, u32[]{:S(2)}, u32[]{:S(2)}) %collective-permute-start.6) | collective-permute-done | bytes 16416 | tf_op jit(solution)/shard_map/ppermute | solution.py:38
  25.5 1.3 %collective-permute-start.7 = (f32[32,128]{1,0:T(8,128)S(1)}, f32[32,128]{1,0:T(8,128)S(1)}, u32[]{:S(2)}, u32[]{:S(2)}) collective-permute-start(f32[32,128]{1,0:T(8,128)S(1)} %add.24), channel_id=1, source_target_pairs={{0,5},{1,4},{2,7},{3,6},{4,1},{5,0},{6,3},{7,2},{8,13},{9,12},{10,... | collective-permute-start | bytes 49160 | tf_op jit(solution)/shard_map/ppermute | solution.py:38
  26.8 1.9 %collective-permute-done.7 = f32[32,128]{1,0:T(8,128)S(1)} collective-permute-done((f32[32,128]{1,0:T(8,128)S(1)}, f32[32,128]{1,0:T(8,128)S(1)}, u32[]{:S(2)}, u32[]{:S(2)}) %collective-permute-start.7) | collective-permute-done | bytes 16416 | tf_op jit(solution)/shard_map/ppermute | solution.py:38
  28.7 1.4 %collective-permute-start.8 = (f32[32,128]{1,0:T(8,128)S(1)}, f32[32,128]{1,0:T(8,128)S(1)}, u32[]{:S(2)}, u32[]{:S(2)}) collective-permute-start(f32[32,128]{1,0:T(8,128)S(1)} %add.25), channel_id=1, source_target_pairs={{0,9},{1,8},{2,11},{3,10},{4,13},{5,12},{6,15},{7,14},{8,1},{9,0},... | collective-permute-start | bytes 49160 | tf_op jit(solution)/shard_map/ppermute | solution.py:38
  30.0 1.8 %collective-permute-done.8 = f32[32,128]{1,0:T(8,128)S(1)} collective-permute-done((f32[32,128]{1,0:T(8,128)S(1)}, f32[32,128]{1,0:T(8,128)S(1)}, u32[]{:S(2)}, u32[]{:S(2)}) %collective-permute-start.8) | collective-permute-done | bytes 16416 | tf_op jit(solution)/shard_map/ppermute | solution.py:38
  31.8 0.5 %collective-permute-start.9 = (f32[32,128]{1,0:T(8,128)S(1)}, f32[32,128]{1,0:T(8,128)S(1)}, u32[]{:S(2)}, u32[]{:S(2)}) collective-permute-start(f32[32,128]{1,0:T(8,128)S(1)} %add.26), channel_id=1, source_target_pairs={{0,17},{1,16},{2,19},{3,18},{4,21},{5,20},{6,23},{7,22},{8,25},{9,... | collective-permute-start | bytes 49160 | tf_op jit(solution)/shard_map/ppermute | solution.py:38
  32.3 3.6 %collective-permute-done.9 = f32[32,128]{1,0:T(8,128)S(1)} collective-permute-done((f32[32,128]{1,0:T(8,128)S(1)}, f32[32,128]{1,0:T(8,128)S(1)}, u32[]{:S(2)}, u32[]{:S(2)}) %collective-permute-start.9) | collective-permute-done | bytes 16416 | tf_op jit(solution)/shard_map/ppermute | solution.py:38
  35.9 1.7 %shard_map.52 = (f32[4,16,4096]{2,1,0:T(8,128)}, f32[64,64]{1,0:T(8,128)}) custom-call(f32[32,128]{1,0:T(8,128)S(1)} %add.27.p_ref, f32[4,16,4096]{2,1,0:T(8,128)S(1)} %get-tuple-element.6.l_ref, f32[2,16,4096]{2,1,0:T(8,128)S(1)} %get-tuple-element.9.r_ref), custom_call_target="tpu_custom_call" | custom-call | flops 4194304 | bytes 1048576 | tf_op jit(solution)/shard_map/pallas_call | solution.py:193
  (7 shorter events, 0.0 us)
Async XLA Ops:
  0.6 7.3 %copy-start = (f32[4,16,4096]{2,1,0:T(8,128)S(1)}, f32[4,16,4096]{2,1,0:T(8,128)}, u32[]{:S(2)}) copy-start(f32[4,16,4096]{2,1,0:T(8,128)} %g_ref.1) | copy-start | bytes 3145732
  1.7 8.9 %collective-permute-start.2 = (f32[4,16,128]{2,1,0:T(8,128)S(1)}, f32[4,16,128]{2,1,0:T(8,128)S(1)}, u32[]{:S(2)}, u32[]{:S(2)}) collective-permute-start(f32[4,16,128]{2,1,0:T(8,128)S(1)} %pad_maximum_fusion), channel_id=1, source_target_pairs={{0,1},{1,0},{2,3},{3,2},{4,5},{5,4},{6,7},{7,6},{8,9},{9,8},{10,11... | collective-permute-start | bytes 98312 | tf_op jit(solution)/shard_map/ppermute | solution.py:18
  3.2 14.3 %collective-permute-start.4 = (f32[1,16,4096]{2,1,0:T(8,128)S(1)}, f32[1,16,4096]{2,1,0:T(8,128)S(1)}, u32[]{:S(2)}, u32[]{:S(2)}) collective-permute-start(f32[1,16,4096]{2,1,0:T(8,128)S(1)} %get-tuple-element.10), channel_id=1, source_target_pairs={{0,24},{8,0},{16,8},{24,16},{1,25},{9,1},{17,9},{25,17},{2,26},{10... | collective-permute-start | bytes 786440 | tf_op jit(solution)/shard_map/ppermute | solution.py:18
  7.9 12.7 %collective-permute-start.3 = (f32[1,16,4096]{2,1,0:T(8,128)S(1)}, f32[1,16,4096]{2,1,0:T(8,128)S(1)}, u32[]{:S(2)}, u32[]{:S(2)}) collective-permute-start(f32[1,16,4096]{2,1,0:T(8,128)S(1)} %get-tuple-element.11), channel_id=1, source_target_pairs={{0,8},{8,16},{16,24},{24,0},{1,9},{9,17},{17,25},{25,1},{2,10},{10... | collective-permute-start | bytes 786440 | tf_op jit(solution)/shard_map/ppermute | solution.py:18
  8.0 2.5 %copy-start.2 = (f32[64]{0:T(128)S(1)}, f32[64]{0:T(128)}, u32[]{:S(2)}) copy-start(f32[64]{0:T(128)} %param.5) | copy-start | bytes 772
  8.0 5.0 %collective-permute-start.1 = (f32[4,1,4096]{2,1,0:T(1,128)S(1)}, f32[4,1,4096]{2,1,0:T(1,128)S(1)}, u32[]{:S(2)}, u32[]{:S(2)}) collective-permute-start(f32[4,1,4096]{2,1,0:T(1,128)S(1)} %get-tuple-element.14), channel_id=1, source_target_pairs={{0,6},{2,0},{4,2},{6,4},{1,7},{3,1},{5,3},{7,5},{8,14},{10,8},{12,... | collective-permute-start | bytes 196616 | tf_op jit(solution)/shard_map/ppermute | solution.py:18
  10.5 5.2 %collective-permute-start = (f32[4,1,4096]{2,1,0:T(1,128)S(1)}, f32[4,1,4096]{2,1,0:T(1,128)S(1)}, u32[]{:S(2)}, u32[]{:S(2)}) collective-permute-start(f32[4,1,4096]{2,1,0:T(1,128)S(1)} %get-tuple-element.15), channel_id=1, source_target_pairs={{0,2},{2,4},{4,6},{6,0},{1,3},{3,5},{5,7},{7,1},{8,10},{10,12},{12... | collective-permute-start | bytes 196616 | tf_op jit(solution)/shard_map/ppermute | solution.py:18
  15.7 1.2 %copy-start.1 = (f32[4,16,4096]{2,1,0:T(8,128)S(1)}, f32[4,16,4096]{2,1,0:T(8,128)}, u32[]{:S(2)}) copy-start(f32[4,16,4096]{2,1,0:T(8,128)} %b_ref.1) | copy-start | bytes 3145732
  21.1 1.2 %collective-permute-start.5 = (f32[32,128]{1,0:T(8,128)S(1)}, f32[32,128]{1,0:T(8,128)S(1)}, u32[]{:S(2)}, u32[]{:S(2)}) collective-permute-start(f32[32,128]{1,0:T(8,128)S(1)} %get-tuple-element.8), channel_id=1, source_target_pairs={{0,1},{1,0},{2,3},{3,2},{4,5},{5,4},{6,7},{7,6},{8,9},{9,8},{10,11... | collective-permute-start | bytes 49160 | tf_op jit(solution)/shard_map/ppermute | solution.py:38
  22.3 3.2 %collective-permute-start.6 = (f32[32,128]{1,0:T(8,128)S(1)}, f32[32,128]{1,0:T(8,128)S(1)}, u32[]{:S(2)}, u32[]{:S(2)}) collective-permute-start(f32[32,128]{1,0:T(8,128)S(1)} %add.23), channel_id=1, source_target_pairs={{0,3},{1,2},{2,1},{3,0},{4,7},{5,6},{6,5},{7,4},{8,11},{9,10},{10,... | collective-permute-start | bytes 49160 | tf_op jit(solution)/shard_map/ppermute | solution.py:38
  25.5 3.2 %collective-permute-start.7 = (f32[32,128]{1,0:T(8,128)S(1)}, f32[32,128]{1,0:T(8,128)S(1)}, u32[]{:S(2)}, u32[]{:S(2)}) collective-permute-start(f32[32,128]{1,0:T(8,128)S(1)} %add.24), channel_id=1, source_target_pairs={{0,5},{1,4},{2,7},{3,6},{4,1},{5,0},{6,3},{7,2},{8,13},{9,12},{10,... | collective-permute-start | bytes 49160 | tf_op jit(solution)/shard_map/ppermute | solution.py:38
  28.7 3.2 %collective-permute-start.8 = (f32[32,128]{1,0:T(8,128)S(1)}, f32[32,128]{1,0:T(8,128)S(1)}, u32[]{:S(2)}, u32[]{:S(2)}) collective-permute-start(f32[32,128]{1,0:T(8,128)S(1)} %add.25), channel_id=1, source_target_pairs={{0,9},{1,8},{2,11},{3,10},{4,13},{5,12},{6,15},{7,14},{8,1},{9,0},... | collective-permute-start | bytes 49160 | tf_op jit(solution)/shard_map/ppermute | solution.py:38
  31.8 4.1 %collective-permute-start.9 = (f32[32,128]{1,0:T(8,128)S(1)}, f32[32,128]{1,0:T(8,128)S(1)}, u32[]{:S(2)}, u32[]{:S(2)}) collective-permute-start(f32[32,128]{1,0:T(8,128)S(1)} %add.26), channel_id=1, source_target_pairs={{0,17},{1,16},{2,19},{3,18},{4,21},{5,20},{6,23},{7,22},{8,25},{9,... | collective-permute-start | bytes 49160 | tf_op jit(solution)/shard_map/ppermute | solution.py:38

commit v3 on v2

--- a/solution.py
+++ b/solution.py
@@ -25,17 +25,27 @@
     return last, initial
 
 
-def masks_of(devices):
-    masks = [1]
-    while 2 ** len(masks) < devices:
-        masks.append(2 ** len(masks) + 1)
-    return masks
+def stages_of(devices):
+    bits = [1 << k for k in range(1, (devices - 1).bit_length())]
+    stages = [(1,)]
+    for low, high in zip(bits[0::2], bits[1::2]):
+        stages.append((low | high, high | 1, low | 1))
+    if len(bits) % 2:
+        stages.append((bits[-1] | 1,))
+    return stages
 
 
 def sum_over_all(value):
     devices = lax.axis_size(AXES)
-    for mask in masks_of(devices):
-        value = value + lax.ppermute(value, AXES, [(i, i ^ mask) for i in range(devices)])
+    for masks in stages_of(devices):
+        got = []
+        for mask in masks:
+            got.append(lax.ppermute(value, AXES, [(i, i ^ mask) for i in range(devices)]))
+        if len(got) == 1:
+            value = value + got[0]
+        else:
+            far, second, first = got
+            value = (value + first) + (second + far)
     return value
 
 
@@ -114,17 +124,20 @@
     p_ref[...] = pack_gram(g_ref[...] + split_gram(tiles))
 
 
-def final(cells, p_ref, l_ref, r_ref, n_ref, m_ref, buf, sem):
+def final(cells, p_ref, l_ref, r_ref, n_ref, m_ref, buf, gram, sem):
     planes, rows, width = l_ref.shape
     half, quarter = LANES // 2, LANES // 4
     mean = p_ref[...] / jnp.float32(cells)
+    gram[pl.ds(0, quarter), :] = mean[:, :half]
+    gram[pl.ds(quarter, quarter), :] = half_roll(mean)[:, :half]
+    copies = [pltpu.make_async_copy(gram, m_ref, sem.at[planes])]
+    copies[0].start()
     row = lax.broadcasted_iota(jnp.int32, (quarter, LANES), 0)
     lane = lax.broadcasted_iota(jnp.int32, (quarter, LANES), 1)
     own = (lane == row) | (lane == row + half + quarter)
     diagonal = jnp.sum(jnp.where(own, mean, 0.0), axis=0, keepdims=True)
     diagonal = diagonal + half_roll(diagonal)
     scale = jnp.broadcast_to(lax.rsqrt(diagonal + 1e-06), (rows, LANES))
-    copies = []
     for z in range(planes):
         source = r_ref.at[0] if z == 0 else r_ref.at[1] if z == planes - 1 else l_ref.at[z]
         for t in range(width // LANES):
@@ -133,8 +146,6 @@
         copy = pltpu.make_async_copy(buf.at[z], n_ref.at[z], sem.at[z])
         copy.start()
         copies.append(copy)
-    m_ref[pl.ds(0, quarter), :] = mean[:, :half]
-    m_ref[pl.ds(quarter, quarter), :] = half_roll(mean)[:, :half]
     for copy in copies:
         copy.wait()
 
@@ -198,10 +209,11 @@
         ),
         1 << 22,
         in_specs=[VMEM] * 3,
-        out_specs=[pl.BlockSpec(memory_space=pl.ANY), VMEM],
+        out_specs=[pl.BlockSpec(memory_space=pl.ANY)] * 2,
         scratch_shapes=[
             pltpu.VMEM(guess.shape, f32),
-            pltpu.SemaphoreType.DMA((z_cells,)),
+            pltpu.VMEM((columns, columns), f32),
+            pltpu.SemaphoreType.DMA((z_cells + 1,)),
         ],
     )(packed, left, outer)
 

time: 37.8 us -> 35.5 us (0.939)
  waiting for transfers between devices: 18.5 us -> 13.8 us
  starting transfers between devices: 12.2 us -> 15.1 us
  Pallas kernels: 2.76 us -> 2.15 us
    ppermute x5 -> x7, waiting for transfers between devices: 10.3 us -> 5.66 us  [sum_over_all(): lax.ppermute(value, AXES, [(i, i ^ mask) for i in range(devices)])]
    ppermute x5 -> x7, starting transfers between devices: 4.51 us -> 7.45 us  [sum_over_all(): lax.ppermute(value, AXES, [(i, i ^ mask) for i in range(devices)])]
    pallas_call x1, Pallas kernels: 1.72 us -> 1.12 us  [local(): call(functools.partial(final, total_cells), (jax.ShapeDtypeStruct(guess.s...]
  transfers between devices with their start and end apart: 10 -> 12, of which waited for: 8 -> 9; matrix products, arithmetic and copies ran while one was open for 3% -> 4% of each run, Pallas kernels for 2% -> 2%
where the time goes in v3:
time: 35.5 us; the launch traced here: 35.3 us
  starting transfers between devices  15.1 us (43%)
  waiting for transfers between devices  13.8 us (39%)
  local copies, waits for them, and re-layouts  3.42 us (10%)
  Pallas kernels  2.15 us (6%)
  between operations  0.71 us (2%)
    ppermute x5, waiting for transfers between devices, ring(): lax.ppermute(array, axis, [(i, (i + step) % peers) for i in range(peers)])  8.18 us
    ppermute x5, starting transfers between devices, ring(): lax.ppermute(array, axis, [(i, (i + step) % peers) for i in range(peers)])  7.66 us
    ppermute x7, starting transfers between devices, sum_over_all(): lax.ppermute(value, AXES, [(i, i ^ mask) for i in range(devices)])  7.45 us
    ppermute x7, waiting for transfers between devices, sum_over_all(): lax.ppermute(value, AXES, [(i, i ^ mask) for i in range(devices)])  5.66 us
    unnamed x6, local copies, waits for them, and re-layouts  1.24 us
    slice x2, local copies, waits for them, and re-layouts, faces(): initial = lax.slice_in_dim(array, 0, width, axis=dim)  1.16 us
    pallas_call x1, Pallas kernels, local(): call(functools.partial(final, total_cells), (jax.ShapeDtypeStruct(guess.s...  1.12 us
    slice x1, local copies, waits for them, and re-layouts, faces(): last = lax.slice_in_dim(array, length - width, length, axis=dim)  0.94 us
  transfers between devices with their start and end apart: 12, of which 9 were waited for; matrix products, arithmetic and copies ran while one was open for 4% of the time, Pallas kernels for 2%

profile of v3, /device:TPU:0, one launch (start us, length us, event | category | flops | bytes accessed | tf_op | source)
XLA Modules:
  0.0 35.3 jit_solution(10172396232952513358)
XLA Ops:
  0.6 0.0 copy-start
  0.6 0.9 %fusion.1 = (f32[4,16,64]{2,1,0:T(8,128)S(1)}, f32[4,16,64]{2,1,0:T(8,128)S(1)}) fusion(f32[4,16,4096]{2,1,0:T(8,128)} %g_ref.1), kind=kLoop, calls=%fused_computation.5 | loop fusion | bytes 65536 | tf_op jit(solution)/shard_map/slice | solution.py:23
  1.6 0.1 pad_maximum_fusion
  1.7 0.5 %collective-permute-start.2 = (f32[4,16,128]{2,1,0:T(8,128)S(1)}, f32[4,16,128]{2,1,0:T(8,128)S(1)}, u32[]{:S(2)}, u32[]{:S(2)}) collective-permute-start(f32[4,16,128]{2,1,0:T(8,128)S(1)} %pad_maximum_fusion), channel_id=1, source_target_pairs={{0,1},{1,0},{2,3},{3,2},{4,5},{5,4},{6,7},{7,6},{8,9},{9,8},{10,11... | collective-permute-start | bytes 98312 | tf_op jit(solution)/shard_map/ppermute | solution.py:18
  2.2 1.1 %fusion = (f32[1,16,4096]{2,1,0:T(8,128)S(1)}, f32[1,16,4096]{2,1,0:T(8,128)S(1)}) fusion(f32[4,16,4096]{2,1,0:T(8,128)} %g_ref.1), kind=kLoop, calls=%fused_computation.4 | loop fusion | bytes 1048576 | tf_op jit(solution)/shard_map/slice | solution.py:24
  3.2 4.7 %collective-permute-start.4 = (f32[1,16,4096]{2,1,0:T(8,128)S(1)}, f32[1,16,4096]{2,1,0:T(8,128)S(1)}, u32[]{:S(2)}, u32[]{:S(2)}) collective-permute-start(f32[1,16,4096]{2,1,0:T(8,128)S(1)} %get-tuple-element.10), channel_id=1, source_target_pairs={{0,24},{8,0},{16,8},{24,16},{1,25},{9,1},{17,9},{25,17},{2,26},{10... | collective-permute-start | bytes 786440 | tf_op jit(solution)/shard_map/ppermute | solution.py:18
  7.9 0.0 collective-permute-start.3
  7.9 0.0 copy-done
  7.9 0.1 fusion.2
  8.0 0.0 copy-start.2
  8.0 2.5 %collective-permute-start.1 = (f32[4,1,4096]{2,1,0:T(1,128)S(1)}, f32[4,1,4096]{2,1,0:T(1,128)S(1)}, u32[]{:S(2)}, u32[]{:S(2)}) collective-permute-start(f32[4,1,4096]{2,1,0:T(1,128)S(1)} %get-tuple-element.14), channel_id=1, source_target_pairs={{0,6},{2,0},{4,2},{6,4},{1,7},{3,1},{5,3},{7,5},{8,14},{10,8},{12,... | collective-permute-start | bytes 196616 | tf_op jit(solution)/shard_map/ppermute | solution.py:18
  10.5 0.0 collective-permute-start
  10.5 0.0 copy-done.2
  10.5 0.1 broadcast_in_dim_tile.3.c_ref
  10.6 0.0 collective-permute-done.2.xh_ref
  10.6 2.4 %collective-permute-done.1.ya_ref = f32[4,1,4096]{2,1,0:T(1,128)S(1)} collective-permute-done((f32[4,1,4096]{2,1,0:T(1,128)S(1)}, f32[4,1,4096]{2,1,0:T(1,128)S(1)}, u32[]{:S(2)}, u32[]{:S(2)}) %collective-permute-start.1) | collective-permute-done | bytes 65568 | tf_op jit(solution)/shard_map/ppermute | solution.py:18
  13.0 2.7 %collective-permute-done.yb_ref = f32[4,1,4096]{2,1,0:T(1,128)S(1)} collective-permute-done((f32[4,1,4096]{2,1,0:T(1,128)S(1)}, f32[4,1,4096]{2,1,0:T(1,128)S(1)}, u32[]{:S(2)}, u32[]{:S(2)}) %collective-permute-start) | collective-permute-done | bytes 65568 | tf_op jit(solution)/shard_map/ppermute | solution.py:18
  15.7 0.0 copy-start.1
  15.7 1.2 %copy-done.1 = f32[4,16,4096]{2,1,0:T(8,128)S(1)} copy-done((f32[4,16,4096]{2,1,0:T(8,128)S(1)}, f32[4,16,4096]{2,1,0:T(8,128)}, u32[]{:S(2)}) %copy-start.1) | copy-done | bytes 1048600
  16.9 0.6 %shard_map.50 = (f32[4,16,4096]{2,1,0:T(8,128)S(1)}, f32[128,256]{1,0:T(8,128)S(1)}) custom-call(f32[4,16,4096]{2,1,0:T(8,128)S(1)} %copy-done, f32[4,16,4096]{2,1,0:T(8,128)S(1)} %copy-done.1, f32[1,128]{1,0:T(1,128)S(1)} %broadcast_in_dim_tile.3.c_ref, f32[4,1,4096]{2,1,0:T(1,128)S(1)} %collective-permute-done.yb_ref, ...), custom_call_target="tpu_custom_call" | custom-call | flops 16777216 | bytes 1048576 | tf_op jit(solution)/shard_map/pallas_call | solution.py:182
  17.5 0.0 collective-permute-done.4.za_ref
  17.5 3.1 %collective-permute-done.3.zb_ref = f32[1,16,4096]{2,1,0:T(8,128)S(1)} collective-permute-done((f32[1,16,4096]{2,1,0:T(8,128)S(1)}, f32[1,16,4096]{2,1,0:T(8,128)S(1)}, u32[]{:S(2)}, u32[]{:S(2)}) %collective-permute-start.3) | collective-permute-done | bytes 262176 | tf_op jit(solution)/shard_map/ppermute | solution.py:18
  20.6 0.4 %shard_map.51 = (f32[2,16,4096]{2,1,0:T(8,128)S(1)}, f32[32,128]{1,0:T(8,128)S(1)}) custom-call(f32[4,16,4096]{2,1,0:T(8,128)S(1)} %get-tuple-element.6.l_ref, f32[1,16,4096]{2,1,0:T(8,128)S(1)} %collective-permute-done.3.zb_ref, f32[1,16,4096]{2,1,0:T(8,128)S(1)} %collective-permute-done.4.za_ref, f32[128,256]{1,0:T(8,128)S(1)} %get-tuple-element.7.g_ref), custom_call_target="tpu_custom_call" | custom-call | flops 16777216 | bytes 1048576 | tf_op jit(solution)/shard_map/pallas_call | solution.py:192
  21.1 0.1 collective-permute-start.5
  21.1 1.2 %collective-permute-done.5 = f32[32,128]{1,0:T(8,128)S(1)} collective-permute-done((f32[32,128]{1,0:T(8,128)S(1)}, f32[32,128]{1,0:T(8,128)S(1)}, u32[]{:S(2)}, u32[]{:S(2)}) %collective-permute-start.5) | collective-permute-done | bytes 16416 | tf_op jit(solution)/shard_map/ppermute | solution.py:43
  22.3 2.4 %collective-permute-start.8 = (f32[32,128]{1,0:T(8,128)S(1)}, f32[32,128]{1,0:T(8,128)S(1)}, u32[]{:S(2)}, u32[]{:S(2)}) collective-permute-start(f32[32,128]{1,0:T(8,128)S(1)} %add.29), channel_id=1, source_target_pairs={{0,6},{1,7},{2,4},{3,5},{4,2},{5,3},{6,0},{7,1},{8,14},{9,15},{10,... | collective-permute-start | bytes 49160 | tf_op jit(solution)/shard_map/ppermute | solution.py:43
  24.8 0.0 collective-permute-start.7
  24.8 0.8 %collective-permute-start.6 = (f32[32,128]{1,0:T(8,128)S(1)}, f32[32,128]{1,0:T(8,128)S(1)}, u32[]{:S(2)}, u32[]{:S(2)}) collective-permute-start(f32[32,128]{1,0:T(8,128)S(1)} %add.29), channel_id=1, source_target_pairs={{0,3},{1,2},{2,1},{3,0},{4,7},{5,6},{6,5},{7,4},{8,11},{9,10},{10,... | collective-permute-start | bytes 49160 | tf_op jit(solution)/shard_map/ppermute | solution.py:43
  25.5 1.4 %collective-permute-done.8 = f32[32,128]{1,0:T(8,128)S(1)} collective-permute-done((f32[32,128]{1,0:T(8,128)S(1)}, f32[32,128]{1,0:T(8,128)S(1)}, u32[]{:S(2)}, u32[]{:S(2)}) %collective-permute-start.8) | collective-permute-done | bytes 16416 | tf_op jit(solution)/shard_map/ppermute | solution.py:43
  27.0 1.1 %collective-permute-done.7 = f32[32,128]{1,0:T(8,128)S(1)} collective-permute-done((f32[32,128]{1,0:T(8,128)S(1)}, f32[32,128]{1,0:T(8,128)S(1)}, u32[]{:S(2)}, u32[]{:S(2)}) %collective-permute-start.7) | collective-permute-done | bytes 16416 | tf_op jit(solution)/shard_map/ppermute | solution.py:43
  28.0 0.0 collective-permute-done.6
  28.1 1.8 %collective-permute-start.11 = (f32[32,128]{1,0:T(8,128)S(1)}, f32[32,128]{1,0:T(8,128)S(1)}, u32[]{:S(2)}, u32[]{:S(2)}) collective-permute-start(f32[32,128]{1,0:T(8,128)S(1)} %add_add_fusion.1), channel_id=1, source_target_pairs={{0,24},{1,25},{2,26},{3,27},{4,28},{5,29},{6,30},{7,31},{8,16},{9,... | collective-permute-start | bytes 49160 | tf_op jit(solution)/shard_map/ppermute | solution.py:43
  29.9 1.2 %collective-permute-start.10 = (f32[32,128]{1,0:T(8,128)S(1)}, f32[32,128]{1,0:T(8,128)S(1)}, u32[]{:S(2)}, u32[]{:S(2)}) collective-permute-start(f32[32,128]{1,0:T(8,128)S(1)} %add_add_fusion.1), channel_id=1, source_target_pairs={{0,17},{1,16},{2,19},{3,18},{4,21},{5,20},{6,23},{7,22},{8,25},{9,... | collective-permute-start | bytes 49160 | tf_op jit(solution)/shard_map/ppermute | solution.py:43
  31.0 1.2 %collective-permute-start.9 = (f32[32,128]{1,0:T(8,128)S(1)}, f32[32,128]{1,0:T(8,128)S(1)}, u32[]{:S(2)}, u32[]{:S(2)}) collective-permute-start(f32[32,128]{1,0:T(8,128)S(1)} %add_add_fusion.1), channel_id=1, source_target_pairs={{0,9},{1,8},{2,11},{3,10},{4,13},{5,12},{6,15},{7,14},{8,1},{9,0},... | collective-permute-start | bytes 49160 | tf_op jit(solution)/shard_map/ppermute | solution.py:43
  32.2 1.4 %collective-permute-done.11 = f32[32,128]{1,0:T(8,128)S(1)} collective-permute-done((f32[32,128]{1,0:T(8,128)S(1)}, f32[32,128]{1,0:T(8,128)S(1)}, u32[]{:S(2)}, u32[]{:S(2)}) %collective-permute-start.11) | collective-permute-done | bytes 16416 | tf_op jit(solution)/shard_map/ppermute | solution.py:43
  33.7 0.4 %collective-permute-done.10 = f32[32,128]{1,0:T(8,128)S(1)} collective-permute-done((f32[32,128]{1,0:T(8,128)S(1)}, f32[32,128]{1,0:T(8,128)S(1)}, u32[]{:S(2)}, u32[]{:S(2)}) %collective-permute-start.10) | collective-permute-done | bytes 16416 | tf_op jit(solution)/shard_map/ppermute | solution.py:43
  34.1 0.1 collective-permute-done.9
  34.2 1.1 %shard_map.52 = (f32[4,16,4096]{2,1,0:T(8,128)}, f32[64,64]{1,0:T(8,128)}) custom-call(f32[32,128]{1,0:T(8,128)S(1)} %add_add_fusion.p_ref, f32[4,16,4096]{2,1,0:T(8,128)S(1)} %get-tuple-element.6.l_ref, f32[2,16,4096]{2,1,0:T(8,128)S(1)} %get-tuple-element.9.r_ref), custom_call_target="tpu_custom_call" | custom-call | flops 4194304 | bytes 1048576 | tf_op jit(solution)/shard_map/pallas_call | solution.py:204
  (5 shorter events, 0.0 us)
Async XLA Ops:
  0.6 7.3 %copy-start = (f32[4,16,4096]{2,1,0:T(8,128)S(1)}, f32[4,16,4096]{2,1,0:T(8,128)}, u32[]{:S(2)}) copy-start(f32[4,16,4096]{2,1,0:T(8,128)} %g_ref.1) | copy-start | bytes 3145732
  1.7 8.9 %collective-permute-start.2 = (f32[4,16,128]{2,1,0:T(8,128)S(1)}, f32[4,16,128]{2,1,0:T(8,128)S(1)}, u32[]{:S(2)}, u32[]{:S(2)}) collective-permute-start(f32[4,16,128]{2,1,0:T(8,128)S(1)} %pad_maximum_fusion), channel_id=1, source_target_pairs={{0,1},{1,0},{2,3},{3,2},{4,5},{5,4},{6,7},{7,6},{8,9},{9,8},{10,11... | collective-permute-start | bytes 98312 | tf_op jit(solution)/shard_map/ppermute | solution.py:18
  3.2 14.3 %collective-permute-start.4 = (f32[1,16,4096]{2,1,0:T(8,128)S(1)}, f32[1,16,4096]{2,1,0:T(8,128)S(1)}, u32[]{:S(2)}, u32[]{:S(2)}) collective-permute-start(f32[1,16,4096]{2,1,0:T(8,128)S(1)} %get-tuple-element.10), channel_id=1, source_target_pairs={{0,24},{8,0},{16,8},{24,16},{1,25},{9,1},{17,9},{25,17},{2,26},{10... | collective-permute-start | bytes 786440 | tf_op jit(solution)/shard_map/ppermute | solution.py:18
  7.9 12.7 %collective-permute-start.3 = (f32[1,16,4096]{2,1,0:T(8,128)S(1)}, f32[1,16,4096]{2,1,0:T(8,128)S(1)}, u32[]{:S(2)}, u32[]{:S(2)}) collective-permute-start(f32[1,16,4096]{2,1,0:T(8,128)S(1)} %get-tuple-element.11), channel_id=1, source_target_pairs={{0,8},{8,16},{16,24},{24,0},{1,9},{9,17},{17,25},{25,1},{2,10},{10... | collective-permute-start | bytes 786440 | tf_op jit(solution)/shard_map/ppermute | solution.py:18
  8.0 2.5 %copy-start.2 = (f32[64]{0:T(128)S(1)}, f32[64]{0:T(128)}, u32[]{:S(2)}) copy-start(f32[64]{0:T(128)} %param.5) | copy-start | bytes 772
  8.0 5.0 %collective-permute-start.1 = (f32[4,1,4096]{2,1,0:T(1,128)S(1)}, f32[4,1,4096]{2,1,0:T(1,128)S(1)}, u32[]{:S(2)}, u32[]{:S(2)}) collective-permute-start(f32[4,1,4096]{2,1,0:T(1,128)S(1)} %get-tuple-element.14), channel_id=1, source_target_pairs={{0,6},{2,0},{4,2},{6,4},{1,7},{3,1},{5,3},{7,5},{8,14},{10,8},{12,... | collective-permute-start | bytes 196616 | tf_op jit(solution)/shard_map/ppermute | solution.py:18
  10.5 5.2 %collective-permute-start = (f32[4,1,4096]{2,1,0:T(1,128)S(1)}, f32[4,1,4096]{2,1,0:T(1,128)S(1)}, u32[]{:S(2)}, u32[]{:S(2)}) collective-permute-start(f32[4,1,4096]{2,1,0:T(1,128)S(1)} %get-tuple-element.15), channel_id=1, source_target_pairs={{0,2},{2,4},{4,6},{6,0},{1,3},{3,5},{5,7},{7,1},{8,10},{10,12},{12... | collective-permute-start | bytes 196616 | tf_op jit(solution)/shard_map/ppermute | solution.py:18
  15.7 1.2 %copy-start.1 = (f32[4,16,4096]{2,1,0:T(8,128)S(1)}, f32[4,16,4096]{2,1,0:T(8,128)}, u32[]{:S(2)}) copy-start(f32[4,16,4096]{2,1,0:T(8,128)} %b_ref.1) | copy-start | bytes 3145732
  21.1 1.2 %collective-permute-start.5 = (f32[32,128]{1,0:T(8,128)S(1)}, f32[32,128]{1,0:T(8,128)S(1)}, u32[]{:S(2)}, u32[]{:S(2)}) collective-permute-start(f32[32,128]{1,0:T(8,128)S(1)} %get-tuple-element.8), channel_id=1, source_target_pairs={{0,1},{1,0},{2,3},{3,2},{4,5},{5,4},{6,7},{7,6},{8,9},{9,8},{10,11... | collective-permute-start | bytes 49160 | tf_op jit(solution)/shard_map/ppermute | solution.py:43
  22.3 4.6 %collective-permute-start.8 = (f32[32,128]{1,0:T(8,128)S(1)}, f32[32,128]{1,0:T(8,128)S(1)}, u32[]{:S(2)}, u32[]{:S(2)}) collective-permute-start(f32[32,128]{1,0:T(8,128)S(1)} %add.29), channel_id=1, source_target_pairs={{0,6},{1,7},{2,4},{3,5},{4,2},{5,3},{6,0},{7,1},{8,14},{9,15},{10,... | collective-permute-start | bytes 49160 | tf_op jit(solution)/shard_map/ppermute | solution.py:43
  24.8 3.3 %collective-permute-start.7 = (f32[32,128]{1,0:T(8,128)S(1)}, f32[32,128]{1,0:T(8,128)S(1)}, u32[]{:S(2)}, u32[]{:S(2)}) collective-permute-start(f32[32,128]{1,0:T(8,128)S(1)} %add.29), channel_id=1, source_target_pairs={{0,5},{1,4},{2,7},{3,6},{4,1},{5,0},{6,3},{7,2},{8,13},{9,12},{10,... | collective-permute-start | bytes 49160 | tf_op jit(solution)/shard_map/ppermute | solution.py:43
  24.8 3.3 %collective-permute-start.6 = (f32[32,128]{1,0:T(8,128)S(1)}, f32[32,128]{1,0:T(8,128)S(1)}, u32[]{:S(2)}, u32[]{:S(2)}) collective-permute-start(f32[32,128]{1,0:T(8,128)S(1)} %add.29), channel_id=1, source_target_pairs={{0,3},{1,2},{2,1},{3,0},{4,7},{5,6},{6,5},{7,4},{8,11},{9,10},{10,... | collective-permute-start | bytes 49160 | tf_op jit(solution)/shard_map/ppermute | solution.py:43
  28.1 5.6 %collective-permute-start.11 = (f32[32,128]{1,0:T(8,128)S(1)}, f32[32,128]{1,0:T(8,128)S(1)}, u32[]{:S(2)}, u32[]{:S(2)}) collective-permute-start(f32[32,128]{1,0:T(8,128)S(1)} %add_add_fusion.1), channel_id=1, source_target_pairs={{0,24},{1,25},{2,26},{3,27},{4,28},{5,29},{6,30},{7,31},{8,16},{9,... | collective-permute-start | bytes 49160 | tf_op jit(solution)/shard_map/ppermute | solution.py:43
  29.9 4.2 %collective-permute-start.10 = (f32[32,128]{1,0:T(8,128)S(1)}, f32[32,128]{1,0:T(8,128)S(1)}, u32[]{:S(2)}, u32[]{:S(2)}) collective-permute-start(f32[32,128]{1,0:T(8,128)S(1)} %add_add_fusion.1), channel_id=1, source_target_pairs={{0,17},{1,16},{2,19},{3,18},{4,21},{5,20},{6,23},{7,22},{8,25},{9,... | collective-permute-start | bytes 49160 | tf_op jit(solution)/shard_map/ppermute | solution.py:43
  31.0 3.2 %collective-permute-start.9 = (f32[32,128]{1,0:T(8,128)S(1)}, f32[32,128]{1,0:T(8,128)S(1)}, u32[]{:S(2)}, u32[]{:S(2)}) collective-permute-start(f32[32,128]{1,0:T(8,128)S(1)} %add_add_fusion.1), channel_id=1, source_target_pairs={{0,9},{1,8},{2,11},{3,10},{4,13},{5,12},{6,15},{7,14},{8,1},{9,0},... | collective-permute-start | bytes 49160 | tf_op jit(solution)/shard_map/ppermute | solution.py:43

commit v4 on v3

v4 whole, which is shorter than its diff:
```python
import functools

import jax
import jax.numpy as jnp
from jax import lax
from jax.experimental import pallas as pl
from jax.experimental.pallas import tpu as pltpu
from jax.sharding import PartitionSpec as P


AXES = ("gz", "gy", "gx")
LANES = 128
VMEM = pl.BlockSpec(memory_space=pltpu.VMEM)
HBM = pl.BlockSpec(memory_space=pltpu.HBM)


def ring(array, axis, step):
    peers = lax.axis_size(axis)
    return lax.ppermute(array, axis, [(i, (i + step) % peers) for i in range(peers)])


def faces(array, dim, width):
    length = array.shape[dim]
    last = lax.slice_in_dim(array, length - width, length, axis=dim)
    initial = lax.slice_in_dim(array, 0, width, axis=dim)
    return last, initial


def stages_of(devices):
    bits = [1 << k for k in range(1, (devices - 1).bit_length())]
    stages = [(1,)]
    for low, high in zip(bits[0::2], bits[1::2]):
        stages.append((low | high, high | 1, low | 1))
    if len(bits) % 2:
        stages.append((bits[-1] | 1,))
    return stages


def sum_over_all(value):
    devices = lax.axis_size(AXES)
    for masks in stages_of(devices):
        got = []
        for mask in masks:
            got.append(lax.ppermute(value, AXES, [(i, i ^ mask) for i in range(devices)]))
        if len(got) == 1:
            value = value + got[0]
        else:
            far, second, first = got
            value = (value + first) + (second + far)
    return value


def half_roll(tile):
    return pltpu.roll(tile, LANES // 2, axis=1)


def split_gram(tiles):
    block = jnp.concatenate(tiles, axis=0)
    hi = block.astype(jnp.bfloat16)
    lo = (block - hi.astype(jnp.float32)).astype(jnp.bfloat16)
    both = lax.dot_general(
        hi,
        jnp.concatenate([hi, lo], axis=1),
        (((0,), (0,)), ((), ())),
        preferred_element_type=jnp.float32,
    )
    return both[:, :LANES] + 2.0 * both[:, LANES:]


def pack_gram(full):
    half, quarter = LANES // 2, LANES // 4
    low = lax.broadcasted_iota(jnp.int32, (quarter, LANES), 1) < half
    upper = jnp.where(low, full[:quarter], full[half + quarter :])
    lower = jnp.where(low, full[quarter:half], full[half : half + quarter])
    return upper + half_roll(lower)


def outer_planes(planes):
    even = lax.rem(lax.axis_index("gz"), 2) == 0
    first = jnp.where(even, planes - 1, 0)
    return first, planes - 1 - first


def inside(g_ref, b_ref, c_ref, l_ref):
    planes, rows, width = g_ref.shape
    chunks = width // LANES
    row = lax.broadcasted_iota(jnp.int32, (rows, LANES), 0)
    low = lax.broadcasted_iota(jnp.int32, (rows, LANES), 1) < LANES // 2
    centre = jnp.broadcast_to(c_ref[...], (rows, LANES))
    none = jnp.zeros((rows, LANES), jnp.float32)
    for z in range(planes):
        before, here = none, half_roll(g_ref[z, :, pl.ds(0, LANES)])
        for t in range(chunks):
            at = pl.ds(t * LANES, LANES)
            after = none
            if t + 1 < chunks:
                after = half_roll(g_ref[z, :, pl.ds((t + 1) * LANES, LANES)])
            x = g_ref[z, :, at]
            near = here + jnp.where(low, before, after)
            up = jnp.where(row == 0, 0.0, pltpu.roll(x, 1, axis=0))
            down = jnp.where(row == rows - 1, 0.0, pltpu.roll(x, rows - 1, axis=0))
            near = near + (up + down)
            if z > 0:
                near = near + g_ref[z - 1, :, at]
            if z < planes - 1:
                near = near + g_ref[z + 1, :, at]
            l_ref[z, :, at] = b_ref[z, :, at] - (centre * x - near)
            before, here = here, after


def edges(i_ref, yb_ref, ya_ref, xh_ref, l_ref, gram_ref):
    planes, rows, width = l_ref.shape
    chunks = width // LANES
    row = lax.broadcasted_iota(jnp.int32, (rows, LANES), 0)
    low = lax.broadcasted_iota(jnp.int32, (rows, LANES), 1) < LANES // 2
    gram = jnp.zeros((LANES, LANES), jnp.float32)
    for z in range(planes):
        tiles = []
        for t in range(chunks):
            at = pl.ds(t * LANES, LANES)
            add = jnp.where(row == 0, yb_ref[z, :, at], 0.0)
            add = jnp.where(row == rows - 1, ya_ref[z, :, at], add)
            value = i_ref[z, :, at] + add
            if t == 0:
                value = value + jnp.where(low, xh_ref[z], 0.0)
            if t == chunks - 1:
                value = value + jnp.where(low, 0.0, xh_ref[z])
            l_ref[z, :, at] = value
            tiles.append(value)
        if 0 < z < planes - 1:
            gram = gram + split_gram(tiles)
    gram_ref[...] = gram


def outer(which, l_ref, h_ref, g_ref, r_ref, o_ref):
    z = outer_planes(l_ref.shape[0])[which]
    tiles = []
    for t in range(l_ref.shape[2] // LANES):
        at = pl.ds(t * LANES, LANES)
        value = l_ref[z, :, at] + h_ref[0, :, at]
        r_ref[0, :, at] = value
        tiles.append(value)
    gram = g_ref[...] + split_gram(tiles)
    o_ref[...] = pack_gram(gram) if which else gram


def final(cells, p_ref, l_ref, first_ref, second_ref, n_ref, m_ref, buf, gram, sem):
    planes, rows, width = l_ref.shape
    half, quarter = LANES // 2, LANES // 4
    mean = p_ref[...] / jnp.float32(cells)
    row = lax.broadcasted_iota(jnp.int32, (quarter, LANES), 0)
    lane = lax.broadcasted_iota(jnp.int32, (quarter, LANES), 1)
    own = (lane == row) | (lane == row + half + quarter)
    diagonal = jnp.sum(jnp.where(own, mean, 0.0), axis=0, keepdims=True)
    diagonal = diagonal + half_roll(diagonal)
    scale = jnp.broadcast_to(lax.rsqrt(diagonal + 1e-06), (rows, LANES))
    first, second = outer_planes(planes)
    sources = [(z, l_ref.at[z]) for z in range(1, planes - 1)]
    sources += [(first, first_ref.at[0]), (second, second_ref.at[0])]
    copies = []
    for k, (z, source) in enumerate(sources):
        for t in range(width // LANES):
            at = pl.ds(t * LANES, LANES)
            buf[k, :, at] = source[:, at] * scale
        copies.append(pltpu.make_async_copy(buf.at[k], n_ref.at[z], sem.at[k]))
        copies[-1].start()
    square = jnp.concatenate([mean[:, :half], half_roll(mean)[:, :half]], axis=0)
    gram[...] = 0.5 * (square + square.T)
    copies.append(pltpu.make_async_copy(gram, m_ref, sem.at[planes]))
    copies[-1].start()
    for copy in copies:
        copy.wait()


def call(body, outs, cost, **kwargs):
    return pl.pallas_call(
        body,
        out_shape=outs,
        cost_estimate=pl.CostEstimate(flops=cost, bytes_accessed=1 << 20, transcendentals=0),
        compiler_params=pltpu.CompilerParams(vmem_limit_bytes=16 << 20),
        **kwargs,
    )


def pairs_along(array, offset):
    peers = lax.axis_size("gz")
    partner = {}
    for i in range(offset, peers + offset, 2):
        partner[i % peers], partner[(i + 1) % peers] = (i + 1) % peers, i % peers
    return lax.ppermute(array, "gz", sorted(partner.items()))


def local(rhs, guess, shifts):
    z_cells, y_cells, lane_count = guess.shape
    columns = shifts.shape[0]
    x_cells = lane_count // columns
    f32 = jnp.float32
    whole = jax.ShapeDtypeStruct(guess.shape, f32)
    face = jax.ShapeDtypeStruct((1, y_cells, lane_count), f32)
    square = jax.ShapeDtypeStruct((LANES, LANES), f32)
    packed = jax.ShapeDtypeStruct((columns // 2, LANES), f32)
    first, second = (
        lax.dynamic_slice_in_dim(guess, z, 1, 0) for z in outer_planes(z_cells)
    )
    first = pairs_along(first, 0)
    second = pairs_along(second, 1)
    last, initial = faces(guess, 1, 1)
    y_before = ring(last, "gy", 1)
    y_after = ring(initial, "gy", -1)
    last, initial = faces(guess, 2, columns)
    if lax.axis_size("gx") == 2:
        x_halos = ring(jnp.concatenate([last, initial], axis=2), "gx", 1)
    else:
        x_halos = jnp.concatenate(
            [ring(last, "gx", 1), ring(initial, "gx", -1)], axis=2
        )
    centre = jnp.tile(6.0 + shifts, LANES // columns)[None]
    left = call(inside, whole, 1 << 24, in_specs=[VMEM] * 3, out_specs=VMEM)(guess, rhs, centre)
    left, gram = call(
        edges,
        (whole, square),
        1 << 24,
        in_specs=[VMEM] * 4,
        out_specs=[VMEM] * 2,
        input_output_aliases={0: 0},
    )(left, y_before, y_after, x_halos)
    first, gram = call(
        functools.partial(outer, 0),
        (face, square),
        1 << 22,
        in_specs=[VMEM] * 3,
        out_specs=[VMEM] * 2,
    )(left, first, gram)
    second, total = call(
        functools.partial(outer, 1),
        (face, packed),
        1 << 22,
        in_specs=[VMEM] * 3,
        out_specs=[VMEM] * 2,
    )(left, second, gram)
    total = sum_over_all(total)
    total_cells = z_cells * y_cells * x_cells * lax.axis_size(AXES)
    return call(
        functools.partial(final, total_cells),
        (whole, jax.ShapeDtypeStruct((columns, columns), f32)),
        1 << 22,
        in_specs=[VMEM] * 4,
        out_specs=[HBM] * 2,
        scratch_shapes=[
            pltpu.VMEM(guess.shape, f32),
            pltpu.VMEM((columns, columns), f32),
            pltpu.SemaphoreType.DMA((z_cells + 1,)),
        ],
    )(total, left, first, second)


def solution(mesh):
    placed = (P("gz", "gy", "gx"), P("gz", "gy", "gx"), P())
    return jax.shard_map(
        local, mesh=mesh, in_specs=placed, out_specs=(P("gz", "gy", "gx"), P()), check_vma=False
    )
```

time: 35.5 us -> 38.5 us (1.085); the launches traced: 35.3 us -> 37.7 us
  waiting for transfers between devices: 13.8 us -> 15.7 us
  starting transfers between devices: 15.1 us -> 14.1 us
  local copies, waits for them, and re-layouts: 3.42 us -> 4.4 us
  Pallas kernels: 2.15 us -> 2.77 us
    ppermute x0 -> x2, waiting for transfers between devices: none -> 8.26 us  [pairs_along(): return lax.ppermute(array, 'gz', sorted(partner.items()))]
    ppermute x5 -> x3, waiting for transfers between devices: 8.18 us -> 0.01 us  [ring(): lax.ppermute(array, axis, [(i, (i + step) % peers) for i in range(peers)])]
    ppermute x0 -> x2, starting transfers between devices: none -> 4.08 us  [pairs_along(): return lax.ppermute(array, 'gz', sorted(partner.items()))]
    ppermute x5 -> x3, starting transfers between devices: 7.66 us -> 4.06 us  [ring(): lax.ppermute(array, axis, [(i, (i + step) % peers) for i in range(peers)])]
    ppermute x7, waiting for transfers between devices: 5.66 us -> 7.39 us  [sum_over_all(): lax.ppermute(value, AXES, [(i, i ^ mask) for i in range(devices)])]
    ppermute x7, starting transfers between devices: 7.45 us -> 5.95 us  [sum_over_all(): lax.ppermute(value, AXES, [(i, i ^ mask) for i in range(devices)])]
    dynamic_slice x0 -> x1, local copies, waits for them, and re-layouts: none -> 1.06 us  [local(): lax.dynamic_slice_in_dim(guess, z, 1, 0)]
    slice x1, local copies, waits for them, and re-layouts: 0.94 us -> 0.07 us  [faces(): last = lax.slice_in_dim(array, length - width, length, axis=dim)]
  transfers between devices with their start and end apart: 12 -> 12, of which waited for: 9 -> 7; matrix products, arithmetic and copies ran while one was open for 4% -> 3% of each run, Pallas kernels for 2% -> 4%
where the time goes in v4:
time: 38.5 us; the launch traced here: 37.7 us
  waiting for transfers between devices  15.7 us (41%)
  starting transfers between devices  14.1 us (37%)
  local copies, waits for them, and re-layouts  4.4 us (11%)
  Pallas kernels  2.77 us (7%)
  between operations  0.73 us (2%)
    ppermute x2, waiting for transfers between devices, pairs_along(): return lax.ppermute(array, 'gz', sorted(partner.items()))  8.26 us
    ppermute x7, waiting for transfers between devices, sum_over_all(): lax.ppermute(value, AXES, [(i, i ^ mask) for i in range(devices)])  7.39 us
    ppermute x7, starting transfers between devices, sum_over_all(): lax.ppermute(value, AXES, [(i, i ^ mask) for i in range(devices)])  5.95 us
    ppermute x2, starting transfers between devices, pairs_along(): return lax.ppermute(array, 'gz', sorted(partner.items()))  4.08 us
    ppermute x3, starting transfers between devices, ring(): lax.ppermute(array, axis, [(i, (i + step) % peers) for i in range(peers)])  4.06 us
    unnamed x6, local copies, waits for them, and re-layouts  1.79 us
    slice x1, local copies, waits for them, and re-layouts, faces(): initial = lax.slice_in_dim(array, 0, width, axis=dim)  1.38 us
    pallas_call x1, Pallas kernels, local(): call(functools.partial(final, total_cells), (whole, jax.ShapeDtypeStruct(...  1.12 us
  transfers between devices with their start and end apart: 12, of which 7 were waited for; matrix products, arithmetic and copies ran while one was open for 3% of the time, Pallas kernels for 4%

profile of v4, /device:TPU:0, one launch (start us, length us, event | category | flops | bytes accessed | tf_op | source)
XLA Modules:
  0.0 37.7 jit_solution(15481684446455576172)
XLA Ops:
  0.6 0.0 copy-start
  0.6 1.4 %fusion.1 = (f32[4,1,4096]{2,1,0:T(1,128)S(1)}, f32[4,1,4096]{2,1,0:T(1,128)S(1)}) fusion(f32[4,16,4096]{2,1,0:T(8,128)} %g_ref.1), kind=kLoop, calls=%fused_computation.7 | loop fusion | bytes 262144 | tf_op jit(solution)/shard_map/slice | solution.py:25
  2.0 3.0 %collective-permute-start = (f32[4,1,4096]{2,1,0:T(1,128)S(1)}, f32[4,1,4096]{2,1,0:T(1,128)S(1)}, u32[]{:S(2)}, u32[]{:S(2)}) collective-permute-start(f32[4,1,4096]{2,1,0:T(1,128)S(1)} %get-tuple-element.19), channel_id=1, source_target_pairs={{0,2},{2,4},{4,6},{6,0},{1,3},{3,5},{5,7},{7,1},{8,10},{10,12},{12... | collective-permute-start | bytes 196616 | tf_op jit(solution)/shard_map/ppermute | solution.py:19
  5.0 1.0 %collective-permute-start.1 = (f32[4,1,4096]{2,1,0:T(1,128)S(1)}, f32[4,1,4096]{2,1,0:T(1,128)S(1)}, u32[]{:S(2)}, u32[]{:S(2)}) collective-permute-start(f32[4,1,4096]{2,1,0:T(1,128)S(1)} %get-tuple-element.18), channel_id=1, source_target_pairs={{0,6},{2,0},{4,2},{6,4},{1,7},{3,1},{5,3},{7,5},{8,14},{10,8},{12,... | collective-permute-start | bytes 196616 | tf_op jit(solution)/shard_map/ppermute | solution.py:19
  6.1 1.1 %constant_dynamic-slice_fusion = (f32[1,16,4096]{2,1,0:T(8,128)S(1)}, f32[1,16,4096]{2,1,0:T(8,128)S(1)}) fusion(f32[4,16,4096]{2,1,0:T(8,128)} %g_ref.1, s32[]{:T(128)S(6)} %select_n.8, s32[]{:T(128)S(6)} %select_n.9), kind=kLoop, calls=%fused_computation.3 | loop fusion | bytes 1048584 | tf_op jit(solution)/shard_map/dynamic_slice | solution.py:203
  7.1 4.1 %collective-permute-start.3 = (f32[1,16,4096]{2,1,0:T(8,128)S(1)}, f32[1,16,4096]{2,1,0:T(8,128)S(1)}, u32[]{:S(2)}, u32[]{:S(2)}) collective-permute-start(f32[1,16,4096]{2,1,0:T(8,128)S(1)} %get-tuple-element.15), channel_id=1, source_target_pairs={{0,24},{8,16},{16,8},{24,0},{1,25},{9,17},{17,9},{25,1},{2,26},{10... | collective-permute-start | bytes 786440 | tf_op jit(solution)/shard_map/ppermute | solution.py:190
  11.2 0.0 collective-permute-start.4
  11.2 0.0 copy-done
  11.2 0.1 fusion
  11.3 0.0 copy-start.2
  11.3 0.1 pad_maximum_fusion
  11.4 0.0 collective-permute-start.2
  11.4 0.6 %copy-done.2 = f32[64]{0:T(128)S(1)} copy-done((f32[64]{0:T(128)S(1)}, f32[64]{0:T(128)}, u32[]{:S(2)}) %copy-start.2) | copy-done | bytes 280
  12.0 0.1 broadcast_in_dim_tile.3.c_ref
  12.0 0.0 copy-start.1
  12.1 1.2 %copy-done.1 = f32[4,16,4096]{2,1,0:T(8,128)S(1)} copy-done((f32[4,16,4096]{2,1,0:T(8,128)S(1)}, f32[4,16,4096]{2,1,0:T(8,128)}, u32[]{:S(2)}) %copy-start.1) | copy-done | bytes 1048600
  13.3 0.5 %shard_map.50.i_ref = f32[4,16,4096]{2,1,0:T(8,128)S(1)} custom-call(f32[4,16,4096]{2,1,0:T(8,128)S(1)} %copy-done, f32[4,16,4096]{2,1,0:T(8,128)S(1)} %copy-done.1, f32[1,128]{1,0:T(1,128)S(1)} %broadcast_in_dim_tile.3.c_ref), custom_call_target="tpu_custom_call" | custom-call | flops 16777216 | bytes 1048576 | tf_op jit(solution)/shard_map/pallas_call | solution.py:218
  13.8 0.0 collective-permute-done.2.xh_ref
  13.8 0.0 collective-permute-done.yb_ref
  13.8 0.0 collective-permute-done.1.ya_ref
  13.8 0.6 %shard_map.51 = (f32[4,16,4096]{2,1,0:T(8,128)S(1)}, f32[128,128]{1,0:T(8,128)S(1)}) custom-call(f32[4,16,4096]{2,1,0:T(8,128)S(1)} %shard_map.50.i_ref, f32[4,1,4096]{2,1,0:T(1,128)S(1)} %collective-permute-done.yb_ref, f32[4,1,4096]{2,1,0:T(1,128)S(1)} %collective-permute-done.1.ya_ref, ...), custom_call_target="tpu_custom_call", output_to_operand_aliasing={{0}: (0, {})} | custom-call | flops 16777216 | bytes 1048576 | tf_op jit(solution)/shard_map/pallas_call | solution.py:219
  14.4 8.3 %collective-permute-done.4.h_ref = f32[1,16,4096]{2,1,0:T(8,128)S(1)} collective-permute-done((f32[1,16,4096]{2,1,0:T(8,128)S(1)}, f32[1,16,4096]{2,1,0:T(8,128)S(1)}, u32[]{:S(2)}, u32[]{:S(2)}) %collective-permute-start.4) | collective-permute-done | bytes 262176 | tf_op jit(solution)/shard_map/ppermute | solution.py:190
  22.7 0.2 shard_map.52
  22.9 0.0 collective-permute-done.3.h_ref
  22.9 0.3 shard_map.53
  23.2 0.0 collective-permute-start.5
  23.3 1.2 %collective-permute-done.5 = f32[32,128]{1,0:T(8,128)S(1)} collective-permute-done((f32[32,128]{1,0:T(8,128)S(1)}, f32[32,128]{1,0:T(8,128)S(1)}, u32[]{:S(2)}, u32[]{:S(2)}) %collective-permute-start.5) | collective-permute-done | bytes 16416 | tf_op jit(solution)/shard_map/ppermute | solution.py:44
  24.5 1.3 %collective-permute-start.7 = (f32[32,128]{1,0:T(8,128)S(1)}, f32[32,128]{1,0:T(8,128)S(1)}, u32[]{:S(2)}, u32[]{:S(2)}) collective-permute-start(f32[32,128]{1,0:T(8,128)S(1)} %add.35), channel_id=1, source_target_pairs={{0,5},{1,4},{2,7},{3,6},{4,1},{5,0},{6,3},{7,2},{8,13},{9,12},{10,... | collective-permute-start | bytes 49160 | tf_op jit(solution)/shard_map/ppermute | solution.py:44
  25.7 0.5 %collective-permute-start.8 = (f32[32,128]{1,0:T(8,128)S(1)}, f32[32,128]{1,0:T(8,128)S(1)}, u32[]{:S(2)}, u32[]{:S(2)}) collective-permute-start(f32[32,128]{1,0:T(8,128)S(1)} %add.35), channel_id=1, source_target_pairs={{0,6},{1,7},{2,4},{3,5},{4,2},{5,3},{6,0},{7,1},{8,14},{9,15},{10,... | collective-permute-start | bytes 49160 | tf_op jit(solution)/shard_map/ppermute | solution.py:44
  26.3 1.1 %collective-permute-start.6 = (f32[32,128]{1,0:T(8,128)S(1)}, f32[32,128]{1,0:T(8,128)S(1)}, u32[]{:S(2)}, u32[]{:S(2)}) collective-permute-start(f32[32,128]{1,0:T(8,128)S(1)} %add.35), channel_id=1, source_target_pairs={{0,3},{1,2},{2,1},{3,0},{4,7},{5,6},{6,5},{7,4},{8,11},{9,10},{10,... | collective-permute-start | bytes 49160 | tf_op jit(solution)/shard_map/ppermute | solution.py:44
  27.4 0.2 collective-permute-done.7
  27.6 2.9 %collective-permute-done.8 = f32[32,128]{1,0:T(8,128)S(1)} collective-permute-done((f32[32,128]{1,0:T(8,128)S(1)}, f32[32,128]{1,0:T(8,128)S(1)}, u32[]{:S(2)}, u32[]{:S(2)}) %collective-permute-start.8) | collective-permute-done | bytes 16416 | tf_op jit(solution)/shard_map/ppermute | solution.py:44
  30.5 0.0 collective-permute-done.6
  30.5 0.1 collective-permute-start.10
  30.6 2.8 %collective-permute-start.11 = (f32[32,128]{1,0:T(8,128)S(1)}, f32[32,128]{1,0:T(8,128)S(1)}, u32[]{:S(2)}, u32[]{:S(2)}) collective-permute-start(f32[32,128]{1,0:T(8,128)S(1)} %add_add_fusion.1), channel_id=1, source_target_pairs={{0,24},{1,25},{2,26},{3,27},{4,28},{5,29},{6,30},{7,31},{8,16},{9,... | collective-permute-start | bytes 49160 | tf_op jit(solution)/shard_map/ppermute | solution.py:44
  33.5 0.1 collective-permute-start.9
  33.5 1.1 %collective-permute-done.10 = f32[32,128]{1,0:T(8,128)S(1)} collective-permute-done((f32[32,128]{1,0:T(8,128)S(1)}, f32[32,128]{1,0:T(8,128)S(1)}, u32[]{:S(2)}, u32[]{:S(2)}) %collective-permute-start.10) | collective-permute-done | bytes 16416 | tf_op jit(solution)/shard_map/ppermute | solution.py:44
  34.7 1.6 %collective-permute-done.11 = f32[32,128]{1,0:T(8,128)S(1)} collective-permute-done((f32[32,128]{1,0:T(8,128)S(1)}, f32[32,128]{1,0:T(8,128)S(1)}, u32[]{:S(2)}, u32[]{:S(2)}) %collective-permute-start.11) | collective-permute-done | bytes 16416 | tf_op jit(solution)/shard_map/ppermute | solution.py:44
  36.2 0.4 %collective-permute-done.9 = f32[32,128]{1,0:T(8,128)S(1)} collective-permute-done((f32[32,128]{1,0:T(8,128)S(1)}, f32[32,128]{1,0:T(8,128)S(1)}, u32[]{:S(2)}, u32[]{:S(2)}) %collective-permute-start.9) | collective-permute-done | bytes 16416 | tf_op jit(solution)/shard_map/ppermute | solution.py:44
  36.6 1.1 %shard_map.54 = (f32[4,16,4096]{2,1,0:T(8,128)}, f32[64,64]{1,0:T(8,128)}) custom-call(f32[32,128]{1,0:T(8,128)S(1)} %add_add_fusion.p_ref, f32[4,16,4096]{2,1,0:T(8,128)S(1)} %get-tuple-element.8.l_ref, f32[1,16,4096]{2,1,0:T(8,128)S(1)} %get-tuple-element.12.first_ref, f32[1,16,4096]{2,1,0:T(8,128)S(1)} %get-tuple-element.13.second_ref), custom_call_target="tpu_custom_call" | custom-call | flops 4194304 | bytes 1048576 | tf_op jit(solution)/shard_map/pallas_call | solution.py:243
  (5 shorter events, 0.0 us)
Async XLA Ops:
  0.6 10.6 %copy-start = (f32[4,16,4096]{2,1,0:T(8,128)S(1)}, f32[4,16,4096]{2,1,0:T(8,128)}, u32[]{:S(2)}) copy-start(f32[4,16,4096]{2,1,0:T(8,128)} %g_ref.1) | copy-start | bytes 3145732
  2.0 11.7 %collective-permute-start = (f32[4,1,4096]{2,1,0:T(1,128)S(1)}, f32[4,1,4096]{2,1,0:T(1,128)S(1)}, u32[]{:S(2)}, u32[]{:S(2)}) collective-permute-start(f32[4,1,4096]{2,1,0:T(1,128)S(1)} %get-tuple-element.19), channel_id=1, source_target_pairs={{0,2},{2,4},{4,6},{6,0},{1,3},{3,5},{5,7},{7,1},{8,10},{10,12},{12... | collective-permute-start | bytes 196616 | tf_op jit(solution)/shard_map/ppermute | solution.py:19
  5.0 8.7 %collective-permute-start.1 = (f32[4,1,4096]{2,1,0:T(1,128)S(1)}, f32[4,1,4096]{2,1,0:T(1,128)S(1)}, u32[]{:S(2)}, u32[]{:S(2)}) collective-permute-start(f32[4,1,4096]{2,1,0:T(1,128)S(1)} %get-tuple-element.18), channel_id=1, source_target_pairs={{0,6},{2,0},{4,2},{6,4},{1,7},{3,1},{5,3},{7,5},{8,14},{10,8},{12,... | collective-permute-start | bytes 196616 | tf_op jit(solution)/shard_map/ppermute | solution.py:19
  7.1 15.8 %collective-permute-start.3 = (f32[1,16,4096]{2,1,0:T(8,128)S(1)}, f32[1,16,4096]{2,1,0:T(8,128)S(1)}, u32[]{:S(2)}, u32[]{:S(2)}) collective-permute-start(f32[1,16,4096]{2,1,0:T(8,128)S(1)} %get-tuple-element.15), channel_id=1, source_target_pairs={{0,24},{8,16},{16,8},{24,0},{1,25},{9,17},{17,9},{25,1},{2,26},{10... | collective-permute-start | bytes 786440 | tf_op jit(solution)/shard_map/ppermute | solution.py:190
  11.2 11.5 %collective-permute-start.4 = (f32[1,16,4096]{2,1,0:T(8,128)S(1)}, f32[1,16,4096]{2,1,0:T(8,128)S(1)}, u32[]{:S(2)}, u32[]{:S(2)}) collective-permute-start(f32[1,16,4096]{2,1,0:T(8,128)S(1)} %get-tuple-element.14), channel_id=1, source_target_pairs={{0,8},{8,0},{16,24},{24,16},{1,9},{9,1},{17,25},{25,17},{2,10},{10... | collective-permute-start | bytes 786440 | tf_op jit(solution)/shard_map/ppermute | solution.py:190
  11.3 0.7 %copy-start.2 = (f32[64]{0:T(128)S(1)}, f32[64]{0:T(128)}, u32[]{:S(2)}) copy-start(f32[64]{0:T(128)} %param.5) | copy-start | bytes 772
  11.4 2.4 %collective-permute-start.2 = (f32[4,16,128]{2,1,0:T(8,128)S(1)}, f32[4,16,128]{2,1,0:T(8,128)S(1)}, u32[]{:S(2)}, u32[]{:S(2)}) collective-permute-start(f32[4,16,128]{2,1,0:T(8,128)S(1)} %pad_maximum_fusion), channel_id=1, source_target_pairs={{0,1},{1,0},{2,3},{3,2},{4,5},{5,4},{6,7},{7,6},{8,9},{9,8},{10,11... | collective-permute-start | bytes 98312 | tf_op jit(solution)/shard_map/ppermute | solution.py:19
  12.0 1.2 %copy-start.1 = (f32[4,16,4096]{2,1,0:T(8,128)S(1)}, f32[4,16,4096]{2,1,0:T(8,128)}, u32[]{:S(2)}) copy-start(f32[4,16,4096]{2,1,0:T(8,128)} %b_ref.1) | copy-start | bytes 3145732
  23.2 1.2 %collective-permute-start.5 = (f32[32,128]{1,0:T(8,128)S(1)}, f32[32,128]{1,0:T(8,128)S(1)}, u32[]{:S(2)}, u32[]{:S(2)}) collective-permute-start(f32[32,128]{1,0:T(8,128)S(1)} %get-tuple-element.11), channel_id=1, source_target_pairs={{0,1},{1,0},{2,3},{3,2},{4,5},{5,4},{6,7},{7,6},{8,9},{9,8},{10,11... | collective-permute-start | bytes 49160 | tf_op jit(solution)/shard_map/ppermute | solution.py:44
  24.5 3.2 %collective-permute-start.7 = (f32[32,128]{1,0:T(8,128)S(1)}, f32[32,128]{1,0:T(8,128)S(1)}, u32[]{:S(2)}, u32[]{:S(2)}) collective-permute-start(f32[32,128]{1,0:T(8,128)S(1)} %add.35), channel_id=1, source_target_pairs={{0,5},{1,4},{2,7},{3,6},{4,1},{5,0},{6,3},{7,2},{8,13},{9,12},{10,... | collective-permute-start | bytes 49160 | tf_op jit(solution)/shard_map/ppermute | solution.py:44
  25.7 4.8 %collective-permute-start.8 = (f32[32,128]{1,0:T(8,128)S(1)}, f32[32,128]{1,0:T(8,128)S(1)}, u32[]{:S(2)}, u32[]{:S(2)}) collective-permute-start(f32[32,128]{1,0:T(8,128)S(1)} %add.35), channel_id=1, source_target_pairs={{0,6},{1,7},{2,4},{3,5},{4,2},{5,3},{6,0},{7,1},{8,14},{9,15},{10,... | collective-permute-start | bytes 49160 | tf_op jit(solution)/shard_map/ppermute | solution.py:44
  26.3 4.3 %collective-permute-start.6 = (f32[32,128]{1,0:T(8,128)S(1)}, f32[32,128]{1,0:T(8,128)S(1)}, u32[]{:S(2)}, u32[]{:S(2)}) collective-permute-start(f32[32,128]{1,0:T(8,128)S(1)} %add.35), channel_id=1, source_target_pairs={{0,3},{1,2},{2,1},{3,0},{4,7},{5,6},{6,5},{7,4},{8,11},{9,10},{10,... | collective-permute-start | bytes 49160 | tf_op jit(solution)/shard_map/ppermute | solution.py:44
  30.5 4.1 %collective-permute-start.10 = (f32[32,128]{1,0:T(8,128)S(1)}, f32[32,128]{1,0:T(8,128)S(1)}, u32[]{:S(2)}, u32[]{:S(2)}) collective-permute-start(f32[32,128]{1,0:T(8,128)S(1)} %add_add_fusion.1), channel_id=1, source_target_pairs={{0,17},{1,16},{2,19},{3,18},{4,21},{5,20},{6,23},{7,22},{8,25},{9,... | collective-permute-start | bytes 49160 | tf_op jit(solution)/shard_map/ppermute | solution.py:44
  30.6 5.6 %collective-permute-start.11 = (f32[32,128]{1,0:T(8,128)S(1)}, f32[32,128]{1,0:T(8,128)S(1)}, u32[]{:S(2)}, u32[]{:S(2)}) collective-permute-start(f32[32,128]{1,0:T(8,128)S(1)} %add_add_fusion.1), channel_id=1, source_target_pairs={{0,24},{1,25},{2,26},{3,27},{4,28},{5,29},{6,30},{7,31},{8,16},{9,... | collective-permute-start | bytes 49160 | tf_op jit(solution)/shard_map/ppermute | solution.py:44
  33.5 3.2 %collective-permute-start.9 = (f32[32,128]{1,0:T(8,128)S(1)}, f32[32,128]{1,0:T(8,128)S(1)}, u32[]{:S(2)}, u32[]{:S(2)}) collective-permute-start(f32[32,128]{1,0:T(8,128)S(1)} %add_add_fusion.1), channel_id=1, source_target_pairs={{0,9},{1,8},{2,11},{3,10},{4,13},{5,12},{6,15},{7,14},{8,1},{9,0},... | collective-permute-start | bytes 49160 | tf_op jit(solution)/shard_map/ppermute | solution.py:44

commit v5 on v4

--- a/solution.py
+++ b/solution.py
@@ -76,9 +76,21 @@
 
 
 def outer_planes(planes):
-    even = lax.rem(lax.axis_index("gz"), 2) == 0
-    first = jnp.where(even, planes - 1, 0)
+    same = lax.rem(lax.axis_index("gz") + lax.axis_index("gx"), 2) == 1
+    first = jnp.where(same, planes - 1, 0)
     return first, planes - 1 - first
+
+
+def z_faces(g_ref, first_ref, second_ref, sem):
+    planes = outer_planes(g_ref.shape[0])
+    copies = [
+        pltpu.make_async_copy(g_ref.at[z], ref.at[0], sem.at[k])
+        for k, (z, ref) in enumerate(zip(planes, (first_ref, second_ref)))
+    ]
+    for copy in copies:
+        copy.start()
+    for copy in copies:
+        copy.wait()
 
 
 def inside(g_ref, b_ref, c_ref, l_ref):
@@ -172,22 +184,24 @@
         copy.wait()
 
 
-def call(body, outs, cost, **kwargs):
+def call(body, outs, cost, limit=16 << 20, **kwargs):
     return pl.pallas_call(
         body,
         out_shape=outs,
         cost_estimate=pl.CostEstimate(flops=cost, bytes_accessed=1 << 20, transcendentals=0),
-        compiler_params=pltpu.CompilerParams(vmem_limit_bytes=16 << 20),
+        compiler_params=pltpu.CompilerParams(vmem_limit_bytes=limit),
         **kwargs,
     )
 
 
-def pairs_along(array, offset):
-    peers = lax.axis_size("gz")
-    partner = {}
-    for i in range(offset, peers + offset, 2):
-        partner[i % peers], partner[(i + 1) % peers] = (i + 1) % peers, i % peers
-    return lax.ppermute(array, "gz", sorted(partner.items()))
+def z_exchange(array, turn):
+    peers, cores = lax.axis_size("gz"), lax.axis_size("gx")
+    moves = []
+    for z in range(peers):
+        for core in range(cores):
+            up = (z + core + turn) % 2 == 1
+            moves.append((z * cores + core, (z + (1 if up else -1)) % peers * cores + core))
+    return lax.ppermute(array, ("gz", "gx"), moves)
 
 
 def local(rhs, guess, shifts):
@@ -199,11 +213,18 @@
     face = jax.ShapeDtypeStruct((1, y_cells, lane_count), f32)
     square = jax.ShapeDtypeStruct((LANES, LANES), f32)
     packed = jax.ShapeDtypeStruct((columns // 2, LANES), f32)
-    first, second = (
-        lax.dynamic_slice_in_dim(guess, z, 1, 0) for z in outer_planes(z_cells)
-    )
-    first = pairs_along(first, 0)
-    second = pairs_along(second, 1)
+    in_vmem = pltpu.VMEM((1, y_cells, lane_count), f32)
+    first, second = call(
+        z_faces,
+        (in_vmem, in_vmem),
+        1 << 20,
+        limit=60 << 20,
+        in_specs=[HBM],
+        out_specs=[VMEM] * 2,
+        scratch_shapes=[pltpu.SemaphoreType.DMA((2,))],
+    )(guess)
+    first = z_exchange(first, 0)
+    second = z_exchange(second, 1)
     last, initial = faces(guess, 1, 1)
     y_before = ring(last, "gy", 1)
     y_after = ring(initial, "gy", -1)

time: 38.5 us -> 35.9 us (0.932); the launches traced: 37.7 us -> 35.7 us
  waiting for transfers between devices: 15.7 us -> 11.7 us
  starting transfers between devices: 14.1 us -> 17 us
  local copies, waits for them, and re-layouts: 4.4 us -> 2.36 us
  Pallas kernels: 2.77 us -> 3.82 us
    ppermute x2, waiting for transfers between devices: 8.26 us -> 2.05 us  [z_exchange(): return lax.ppermute(array, ('gz', 'gx'), moves)]
    ppermute x7, starting transfers between devices: 5.95 us -> 8.87 us  [sum_over_all(): lax.ppermute(value, AXES, [(i, i ^ mask) for i in range(devices)])]
    ppermute x3, waiting for transfers between devices: 0.01 us -> 1.99 us  [ring(): lax.ppermute(array, axis, [(i, (i + step) % peers) for i in range(peers)])]
    slice x1, local copies, waits for them, and re-layouts: 1.38 us -> 0.09 us  [faces(): initial = lax.slice_in_dim(array, 0, width, axis=dim)]
    dynamic_slice x1 -> x0, local copies, waits for them, and re-layouts: 1.06 us -> none  [local(): lax.dynamic_slice_in_dim(guess, z, 1, 0)]
    pallas_call x0 -> x1, Pallas kernels: none -> 1.04 us  [local(): call(z_faces, (in_vmem, in_vmem), 1 << 20, limit=60 << 20, in_specs=[HBM]...]
    slice x1, local copies, waits for them, and re-layouts: 0.07 us -> 0.94 us  [faces(): last = lax.slice_in_dim(array, length - width, length, axis=dim)]
    ppermute x2, starting transfers between devices: 4.08 us -> 4.68 us  [z_exchange(): return lax.ppermute(array, ('gz', 'gx'), moves)]
  transfers between devices with their start and end apart: 12 -> 12, of which waited for: 7 -> 9; matrix products, arithmetic and copies ran while one was open for 3% -> 1% of each run, Pallas kernels for 4% -> 7%
where the time goes in v5:
time: 35.9 us; the launch traced here: 35.7 us
  starting transfers between devices  17 us (47%)
  waiting for transfers between devices  11.7 us (33%)
  Pallas kernels  3.82 us (11%)
  local copies, waits for them, and re-layouts  2.36 us (7%)
  between operations  0.71 us (2%)
    ppermute x7, starting transfers between devices, sum_over_all(): lax.ppermute(value, AXES, [(i, i ^ mask) for i in range(devices)])  8.87 us
    ppermute x7, waiting for transfers between devices, sum_over_all(): lax.ppermute(value, AXES, [(i, i ^ mask) for i in range(devices)])  7.66 us
    ppermute x2, starting transfers between devices, z_exchange(): return lax.ppermute(array, ('gz', 'gx'), moves)  4.68 us
    ppermute x3, starting transfers between devices, ring(): lax.ppermute(array, axis, [(i, (i + step) % peers) for i in range(peers)])  3.48 us
    ppermute x2, waiting for transfers between devices, z_exchange(): return lax.ppermute(array, ('gz', 'gx'), moves)  2.05 us
    ppermute x3, waiting for transfers between devices, ring(): lax.ppermute(array, axis, [(i, (i + step) % peers) for i in range(peers)])  1.99 us
    unnamed x6, local copies, waits for them, and re-layouts  1.24 us
    pallas_call x1, Pallas kernels, local(): call(functools.partial(final, total_cells), (whole, jax.ShapeDtypeStruct(...  1.12 us
  transfers between devices with their start and end apart: 12, of which 9 were waited for; matrix products, arithmetic and copies ran while one was open for 1% of the time, Pallas kernels for 7%

profile of v5, /device:TPU:0, one launch (start us, length us, event | category | flops | bytes accessed | tf_op | source)
XLA Modules:
  0.0 35.7 jit_solution(1834203299204782253)
XLA Ops:
  0.6 0.0 copy-start
  0.6 0.9 %fusion = (f32[4,16,64]{2,1,0:T(8,128)S(1)}, f32[4,16,64]{2,1,0:T(8,128)S(1)}) fusion(f32[4,16,4096]{2,1,0:T(8,128)} %g_ref.3), kind=kLoop, calls=%fused_computation.4 | loop fusion | bytes 65536 | tf_op jit(solution)/shard_map/slice | solution.py:24
  1.6 0.1 pad_maximum_fusion
  1.7 0.5 %collective-permute-start.2 = (f32[4,16,128]{2,1,0:T(8,128)S(1)}, f32[4,16,128]{2,1,0:T(8,128)S(1)}, u32[]{:S(2)}, u32[]{:S(2)}) collective-permute-start(f32[4,16,128]{2,1,0:T(8,128)S(1)} %pad_maximum_fusion), channel_id=1, source_target_pairs={{0,1},{1,0},{2,3},{3,2},{4,5},{5,4},{6,7},{7,6},{8,9},{9,8},{10,11... | collective-permute-start | bytes 98312 | tf_op jit(solution)/shard_map/ppermute | solution.py:19
  2.2 1.0 %shard_map.52 = (f32[1,16,4096]{2,1,0:T(8,128)S(1)}, f32[1,16,4096]{2,1,0:T(8,128)S(1)}) custom-call(f32[4,16,4096]{2,1,0:T(8,128)} %g_ref.3), custom_call_target="tpu_custom_call" | custom-call | flops 1048576 | bytes 1048576 | tf_op jit(solution)/shard_map/pallas_call | solution.py:217
  3.2 4.7 %collective-permute-start.4 = (f32[1,16,4096]{2,1,0:T(8,128)S(1)}, f32[1,16,4096]{2,1,0:T(8,128)S(1)}, u32[]{:S(2)}, u32[]{:S(2)}) collective-permute-start(f32[1,16,4096]{2,1,0:T(8,128)S(1)} %get-tuple-element.12), channel_id=1, source_target_pairs={{0,24},{1,9},{8,16},{9,1},{16,8},{17,25},{24,0},{25,17},{2,26},{3,... | collective-permute-start | bytes 786440 | tf_op jit(solution)/shard_map/ppermute | solution.py:204
  7.9 0.0 collective-permute-start.3
  7.9 0.0 copy-done
  7.9 0.1 fusion.1
  8.0 0.0 copy-start.2
  8.0 1.5 %collective-permute-start = (f32[4,1,4096]{2,1,0:T(1,128)S(1)}, f32[4,1,4096]{2,1,0:T(1,128)S(1)}, u32[]{:S(2)}, u32[]{:S(2)}) collective-permute-start(f32[4,1,4096]{2,1,0:T(1,128)S(1)} %get-tuple-element.21), channel_id=1, source_target_pairs={{0,2},{2,4},{4,6},{6,0},{1,3},{3,5},{5,7},{7,1},{8,10},{10,12},{12... | collective-permute-start | bytes 196616 | tf_op jit(solution)/shard_map/ppermute | solution.py:19
  9.6 1.4 %collective-permute-start.1 = (f32[4,1,4096]{2,1,0:T(1,128)S(1)}, f32[4,1,4096]{2,1,0:T(1,128)S(1)}, u32[]{:S(2)}, u32[]{:S(2)}) collective-permute-start(f32[4,1,4096]{2,1,0:T(1,128)S(1)} %get-tuple-element.20), channel_id=1, source_target_pairs={{0,6},{2,0},{4,2},{6,4},{1,7},{3,1},{5,3},{7,5},{8,14},{10,8},{12,... | collective-permute-start | bytes 196616 | tf_op jit(solution)/shard_map/ppermute | solution.py:19
  11.0 0.0 copy-done.2
  11.0 0.1 broadcast_in_dim_tile.3.c_ref
  11.1 0.0 copy-start.1
  11.1 1.2 %copy-done.1 = f32[4,16,4096]{2,1,0:T(8,128)S(1)} copy-done((f32[4,16,4096]{2,1,0:T(8,128)S(1)}, f32[4,16,4096]{2,1,0:T(8,128)}, u32[]{:S(2)}) %copy-start.1) | copy-done | bytes 1048600
  12.3 0.5 %shard_map.50.i_ref = f32[4,16,4096]{2,1,0:T(8,128)S(1)} custom-call(f32[4,16,4096]{2,1,0:T(8,128)S(1)} %copy-done, f32[4,16,4096]{2,1,0:T(8,128)S(1)} %copy-done.1, f32[1,128]{1,0:T(1,128)S(1)} %broadcast_in_dim_tile.3.c_ref), custom_call_target="tpu_custom_call" | custom-call | flops 16777216 | bytes 1048576 | tf_op jit(solution)/shard_map/pallas_call | solution.py:239
  12.8 0.0 collective-permute-done.2.xh_ref
  12.8 0.7 %collective-permute-done.yb_ref = f32[4,1,4096]{2,1,0:T(1,128)S(1)} collective-permute-done((f32[4,1,4096]{2,1,0:T(1,128)S(1)}, f32[4,1,4096]{2,1,0:T(1,128)S(1)}, u32[]{:S(2)}, u32[]{:S(2)}) %collective-permute-start) | collective-permute-done | bytes 65568 | tf_op jit(solution)/shard_map/ppermute | solution.py:19
  13.5 1.3 %collective-permute-done.1.ya_ref = f32[4,1,4096]{2,1,0:T(1,128)S(1)} collective-permute-done((f32[4,1,4096]{2,1,0:T(1,128)S(1)}, f32[4,1,4096]{2,1,0:T(1,128)S(1)}, u32[]{:S(2)}, u32[]{:S(2)}) %collective-permute-start.1) | collective-permute-done | bytes 65568 | tf_op jit(solution)/shard_map/ppermute | solution.py:19
  14.8 0.6 %shard_map.51 = (f32[4,16,4096]{2,1,0:T(8,128)S(1)}, f32[128,128]{1,0:T(8,128)S(1)}) custom-call(f32[4,16,4096]{2,1,0:T(8,128)S(1)} %shard_map.50.i_ref, f32[4,1,4096]{2,1,0:T(1,128)S(1)} %collective-permute-done.yb_ref, f32[4,1,4096]{2,1,0:T(1,128)S(1)} %collective-permute-done.1.ya_ref, ...), custom_call_target="tpu_custom_call", output_to_operand_aliasing={{0}: (0, {})} | custom-call | flops 16777216 | bytes 1048576 | tf_op jit(solution)/shard_map/pallas_call | solution.py:240
  15.4 0.0 collective-permute-done.4.h_ref
  15.4 0.3 shard_map.53
  15.7 2.0 %collective-permute-done.3.h_ref = f32[1,16,4096]{2,1,0:T(8,128)S(1)} collective-permute-done((f32[1,16,4096]{2,1,0:T(8,128)S(1)}, f32[1,16,4096]{2,1,0:T(8,128)S(1)}, u32[]{:S(2)}, u32[]{:S(2)}) %collective-permute-start.3) | collective-permute-done | bytes 262176 | tf_op jit(solution)/shard_map/ppermute | solution.py:204
  17.7 0.3 shard_map.54
  18.0 2.7 %collective-permute-start.5 = (f32[32,128]{1,0:T(8,128)S(1)}, f32[32,128]{1,0:T(8,128)S(1)}, u32[]{:S(2)}, u32[]{:S(2)}) collective-permute-start(f32[32,128]{1,0:T(8,128)S(1)} %get-tuple-element.15), channel_id=1, source_target_pairs={{0,1},{1,0},{2,3},{3,2},{4,5},{5,4},{6,7},{7,6},{8,9},{9,8},{10,11... | collective-permute-start | bytes 49160 | tf_op jit(solution)/shard_map/ppermute | solution.py:44
  20.7 0.8 %collective-permute-done.5 = f32[32,128]{1,0:T(8,128)S(1)} collective-permute-done((f32[32,128]{1,0:T(8,128)S(1)}, f32[32,128]{1,0:T(8,128)S(1)}, u32[]{:S(2)}, u32[]{:S(2)}) %collective-permute-start.5) | collective-permute-done | bytes 16416 | tf_op jit(solution)/shard_map/ppermute | solution.py:44
  21.6 1.2 %collective-permute-start.6 = (f32[32,128]{1,0:T(8,128)S(1)}, f32[32,128]{1,0:T(8,128)S(1)}, u32[]{:S(2)}, u32[]{:S(2)}) collective-permute-start(f32[32,128]{1,0:T(8,128)S(1)} %add.29), channel_id=1, source_target_pairs={{0,3},{1,2},{2,1},{3,0},{4,7},{5,6},{6,5},{7,4},{8,11},{9,10},{10,... | collective-permute-start | bytes 49160 | tf_op jit(solution)/shard_map/ppermute | solution.py:44
  22.8 1.3 %collective-permute-start.7 = (f32[32,128]{1,0:T(8,128)S(1)}, f32[32,128]{1,0:T(8,128)S(1)}, u32[]{:S(2)}, u32[]{:S(2)}) collective-permute-start(f32[32,128]{1,0:T(8,128)S(1)} %add.29), channel_id=1, source_target_pairs={{0,5},{1,4},{2,7},{3,6},{4,1},{5,0},{6,3},{7,2},{8,13},{9,12},{10,... | collective-permute-start | bytes 49160 | tf_op jit(solution)/shard_map/ppermute | solution.py:44
  24.1 0.7 %collective-permute-start.8 = (f32[32,128]{1,0:T(8,128)S(1)}, f32[32,128]{1,0:T(8,128)S(1)}, u32[]{:S(2)}, u32[]{:S(2)}) collective-permute-start(f32[32,128]{1,0:T(8,128)S(1)} %add.29), channel_id=1, source_target_pairs={{0,6},{1,7},{2,4},{3,5},{4,2},{5,3},{6,0},{7,1},{8,14},{9,15},{10,... | collective-permute-start | bytes 49160 | tf_op jit(solution)/shard_map/ppermute | solution.py:44
  24.8 0.0 collective-permute-done.6
  24.8 1.2 %collective-permute-done.7 = f32[32,128]{1,0:T(8,128)S(1)} collective-permute-done((f32[32,128]{1,0:T(8,128)S(1)}, f32[32,128]{1,0:T(8,128)S(1)}, u32[]{:S(2)}, u32[]{:S(2)}) %collective-permute-start.7) | collective-permute-done | bytes 16416 | tf_op jit(solution)/shard_map/ppermute | solution.py:44
  26.0 2.8 %collective-permute-done.8 = f32[32,128]{1,0:T(8,128)S(1)} collective-permute-done((f32[32,128]{1,0:T(8,128)S(1)}, f32[32,128]{1,0:T(8,128)S(1)}, u32[]{:S(2)}, u32[]{:S(2)}) %collective-permute-start.8) | collective-permute-done | bytes 16416 | tf_op jit(solution)/shard_map/ppermute | solution.py:44
  28.7 0.2 collective-permute-start.10
  28.9 2.3 %collective-permute-start.11 = (f32[32,128]{1,0:T(8,128)S(1)}, f32[32,128]{1,0:T(8,128)S(1)}, u32[]{:S(2)}, u32[]{:S(2)}) collective-permute-start(f32[32,128]{1,0:T(8,128)S(1)} %add_add_fusion.1), channel_id=1, source_target_pairs={{0,24},{1,25},{2,26},{3,27},{4,28},{5,29},{6,30},{7,31},{8,16},{9,... | collective-permute-start | bytes 49160 | tf_op jit(solution)/shard_map/ppermute | solution.py:44
  31.2 0.5 %collective-permute-start.9 = (f32[32,128]{1,0:T(8,128)S(1)}, f32[32,128]{1,0:T(8,128)S(1)}, u32[]{:S(2)}, u32[]{:S(2)}) collective-permute-start(f32[32,128]{1,0:T(8,128)S(1)} %add_add_fusion.1), channel_id=1, source_target_pairs={{0,9},{1,8},{2,11},{3,10},{4,13},{5,12},{6,15},{7,14},{8,1},{9,0},... | collective-permute-start | bytes 49160 | tf_op jit(solution)/shard_map/ppermute | solution.py:44
  31.7 1.3 %collective-permute-done.10 = f32[32,128]{1,0:T(8,128)S(1)} collective-permute-done((f32[32,128]{1,0:T(8,128)S(1)}, f32[32,128]{1,0:T(8,128)S(1)}, u32[]{:S(2)}, u32[]{:S(2)}) %collective-permute-start.10) | collective-permute-done | bytes 16416 | tf_op jit(solution)/shard_map/ppermute | solution.py:44
  33.0 1.5 %collective-permute-done.11 = f32[32,128]{1,0:T(8,128)S(1)} collective-permute-done((f32[32,128]{1,0:T(8,128)S(1)}, f32[32,128]{1,0:T(8,128)S(1)}, u32[]{:S(2)}, u32[]{:S(2)}) %collective-permute-start.11) | collective-permute-done | bytes 16416 | tf_op jit(solution)/shard_map/ppermute | solution.py:44
  34.5 0.1 collective-permute-done.9
  34.6 1.1 %shard_map.55 = (f32[4,16,4096]{2,1,0:T(8,128)}, f32[64,64]{1,0:T(8,128)}) custom-call(f32[32,128]{1,0:T(8,128)S(1)} %add_add_fusion.p_ref, f32[4,16,4096]{2,1,0:T(8,128)S(1)} %get-tuple-element.10.l_ref, f32[1,16,4096]{2,1,0:T(8,128)S(1)} %get-tuple-element.16.first_ref, f32[1,16,4096]{2,1,0:T(8,128)S(1)} %get-tuple-element.17.second_ref), custom_call_target="tpu_custom_call" | custom-call | flops 4194304 | bytes 1048576 | tf_op jit(solution)/shard_map/pallas_call | solution.py:264
  (5 shorter events, 0.0 us)
Async XLA Ops:
  0.6 7.3 %copy-start = (f32[4,16,4096]{2,1,0:T(8,128)S(1)}, f32[4,16,4096]{2,1,0:T(8,128)}, u32[]{:S(2)}) copy-start(f32[4,16,4096]{2,1,0:T(8,128)} %g_ref.3) | copy-start | bytes 3145732
  1.7 11.1 %collective-permute-start.2 = (f32[4,16,128]{2,1,0:T(8,128)S(1)}, f32[4,16,128]{2,1,0:T(8,128)S(1)}, u32[]{:S(2)}, u32[]{:S(2)}) collective-permute-start(f32[4,16,128]{2,1,0:T(8,128)S(1)} %pad_maximum_fusion), channel_id=1, source_target_pairs={{0,1},{1,0},{2,3},{3,2},{4,5},{5,4},{6,7},{7,6},{8,9},{9,8},{10,11... | collective-permute-start | bytes 98312 | tf_op jit(solution)/shard_map/ppermute | solution.py:19
  3.2 12.2 %collective-permute-start.4 = (f32[1,16,4096]{2,1,0:T(8,128)S(1)}, f32[1,16,4096]{2,1,0:T(8,128)S(1)}, u32[]{:S(2)}, u32[]{:S(2)}) collective-permute-start(f32[1,16,4096]{2,1,0:T(8,128)S(1)} %get-tuple-element.12), channel_id=1, source_target_pairs={{0,24},{1,9},{8,16},{9,1},{16,8},{17,25},{24,0},{25,17},{2,26},{3,... | collective-permute-start | bytes 786440 | tf_op jit(solution)/shard_map/ppermute | solution.py:204
  7.9 9.8 %collective-permute-start.3 = (f32[1,16,4096]{2,1,0:T(8,128)S(1)}, f32[1,16,4096]{2,1,0:T(8,128)S(1)}, u32[]{:S(2)}, u32[]{:S(2)}) collective-permute-start(f32[1,16,4096]{2,1,0:T(8,128)S(1)} %get-tuple-element.11), channel_id=1, source_target_pairs={{0,8},{1,25},{8,0},{9,17},{16,24},{17,9},{24,16},{25,1},{2,10},{3,... | collective-permute-start | bytes 786440 | tf_op jit(solution)/shard_map/ppermute | solution.py:204
  8.0 3.0 %copy-start.2 = (f32[64]{0:T(128)S(1)}, f32[64]{0:T(128)}, u32[]{:S(2)}) copy-start(f32[64]{0:T(128)} %param.5) | copy-start | bytes 772
  8.0 5.4 %collective-permute-start = (f32[4,1,4096]{2,1,0:T(1,128)S(1)}, f32[4,1,4096]{2,1,0:T(1,128)S(1)}, u32[]{:S(2)}, u32[]{:S(2)}) collective-permute-start(f32[4,1,4096]{2,1,0:T(1,128)S(1)} %get-tuple-element.21), channel_id=1, source_target_pairs={{0,2},{2,4},{4,6},{6,0},{1,3},{3,5},{5,7},{7,1},{8,10},{10,12},{12... | collective-permute-start | bytes 196616 | tf_op jit(solution)/shard_map/ppermute | solution.py:19
  9.6 5.2 %collective-permute-start.1 = (f32[4,1,4096]{2,1,0:T(1,128)S(1)}, f32[4,1,4096]{2,1,0:T(1,128)S(1)}, u32[]{:S(2)}, u32[]{:S(2)}) collective-permute-start(f32[4,1,4096]{2,1,0:T(1,128)S(1)} %get-tuple-element.20), channel_id=1, source_target_pairs={{0,6},{2,0},{4,2},{6,4},{1,7},{3,1},{5,3},{7,5},{8,14},{10,8},{12,... | collective-permute-start | bytes 196616 | tf_op jit(solution)/shard_map/ppermute | solution.py:19
  11.1 1.2 %copy-start.1 = (f32[4,16,4096]{2,1,0:T(8,128)S(1)}, f32[4,16,4096]{2,1,0:T(8,128)}, u32[]{:S(2)}) copy-start(f32[4,16,4096]{2,1,0:T(8,128)} %b_ref.1) | copy-start | bytes 3145732
  18.0 3.5 %collective-permute-start.5 = (f32[32,128]{1,0:T(8,128)S(1)}, f32[32,128]{1,0:T(8,128)S(1)}, u32[]{:S(2)}, u32[]{:S(2)}) collective-permute-start(f32[32,128]{1,0:T(8,128)S(1)} %get-tuple-element.15), channel_id=1, source_target_pairs={{0,1},{1,0},{2,3},{3,2},{4,5},{5,4},{6,7},{7,6},{8,9},{9,8},{10,11... | collective-permute-start | bytes 49160 | tf_op jit(solution)/shard_map/ppermute | solution.py:44
  21.6 3.2 %collective-permute-start.6 = (f32[32,128]{1,0:T(8,128)S(1)}, f32[32,128]{1,0:T(8,128)S(1)}, u32[]{:S(2)}, u32[]{:S(2)}) collective-permute-start(f32[32,128]{1,0:T(8,128)S(1)} %add.29), channel_id=1, source_target_pairs={{0,3},{1,2},{2,1},{3,0},{4,7},{5,6},{6,5},{7,4},{8,11},{9,10},{10,... | collective-permute-start | bytes 49160 | tf_op jit(solution)/shard_map/ppermute | solution.py:44
  22.8 3.2 %collective-permute-start.7 = (f32[32,128]{1,0:T(8,128)S(1)}, f32[32,128]{1,0:T(8,128)S(1)}, u32[]{:S(2)}, u32[]{:S(2)}) collective-permute-start(f32[32,128]{1,0:T(8,128)S(1)} %add.29), channel_id=1, source_target_pairs={{0,5},{1,4},{2,7},{3,6},{4,1},{5,0},{6,3},{7,2},{8,13},{9,12},{10,... | collective-permute-start | bytes 49160 | tf_op jit(solution)/shard_map/ppermute | solution.py:44
  24.1 4.6 %collective-permute-start.8 = (f32[32,128]{1,0:T(8,128)S(1)}, f32[32,128]{1,0:T(8,128)S(1)}, u32[]{:S(2)}, u32[]{:S(2)}) collective-permute-start(f32[32,128]{1,0:T(8,128)S(1)} %add.29), channel_id=1, source_target_pairs={{0,6},{1,7},{2,4},{3,5},{4,2},{5,3},{6,0},{7,1},{8,14},{9,15},{10,... | collective-permute-start | bytes 49160 | tf_op jit(solution)/shard_map/ppermute | solution.py:44
  28.7 4.3 %collective-permute-start.10 = (f32[32,128]{1,0:T(8,128)S(1)}, f32[32,128]{1,0:T(8,128)S(1)}, u32[]{:S(2)}, u32[]{:S(2)}) collective-permute-start(f32[32,128]{1,0:T(8,128)S(1)} %add_add_fusion.1), channel_id=1, source_target_pairs={{0,17},{1,16},{2,19},{3,18},{4,21},{5,20},{6,23},{7,22},{8,25},{9,... | collective-permute-start | bytes 49160 | tf_op jit(solution)/shard_map/ppermute | solution.py:44
  28.9 5.6 %collective-permute-start.11 = (f32[32,128]{1,0:T(8,128)S(1)}, f32[32,128]{1,0:T(8,128)S(1)}, u32[]{:S(2)}, u32[]{:S(2)}) collective-permute-start(f32[32,128]{1,0:T(8,128)S(1)} %add_add_fusion.1), channel_id=1, source_target_pairs={{0,24},{1,25},{2,26},{3,27},{4,28},{5,29},{6,30},{7,31},{8,16},{9,... | collective-permute-start | bytes 49160 | tf_op jit(solution)/shard_map/ppermute | solution.py:44
  31.2 3.4 %collective-permute-start.9 = (f32[32,128]{1,0:T(8,128)S(1)}, f32[32,128]{1,0:T(8,128)S(1)}, u32[]{:S(2)}, u32[]{:S(2)}) collective-permute-start(f32[32,128]{1,0:T(8,128)S(1)} %add_add_fusion.1), channel_id=1, source_target_pairs={{0,9},{1,8},{2,11},{3,10},{4,13},{5,12},{6,15},{7,14},{8,1},{9,0},... | collective-permute-start | bytes 49160 | tf_op jit(solution)/shard_map/ppermute | solution.py:44

commit v6 on v5

--- a/solution.py
+++ b/solution.py
@@ -81,16 +81,24 @@
     return first, planes - 1 - first
 
 
-def z_faces(g_ref, first_ref, second_ref, sem):
-    planes = outer_planes(g_ref.shape[0])
+def run_copies(pairs, sem):
     copies = [
-        pltpu.make_async_copy(g_ref.at[z], ref.at[0], sem.at[k])
-        for k, (z, ref) in enumerate(zip(planes, (first_ref, second_ref)))
+        pltpu.make_async_copy(source, target, sem.at[k])
+        for k, (source, target) in enumerate(pairs)
     ]
     for copy in copies:
         copy.start()
     for copy in copies:
         copy.wait()
+
+
+def z_faces(g_ref, first_ref, second_ref, sem):
+    first, second = outer_planes(g_ref.shape[0])
+    run_copies(((g_ref.at[first], first_ref.at[0]), (g_ref.at[second], second_ref.at[0])), sem)
+
+
+def load(g_ref, b_ref, g_out, b_out, sem):
+    run_copies(((g_ref, g_out), (b_ref, b_out)), sem)
 
 
 def inside(g_ref, b_ref, c_ref, l_ref):
@@ -225,6 +233,16 @@
     )(guess)
     first = z_exchange(first, 0)
     second = z_exchange(second, 1)
+    in_vmem = pltpu.VMEM(guess.shape, f32)
+    guess, rhs = call(
+        load,
+        (in_vmem, in_vmem),
+        1 << 20,
+        limit=60 << 20,
+        in_specs=[HBM] * 2,
+        out_specs=[VMEM] * 2,
+        scratch_shapes=[pltpu.SemaphoreType.DMA((2,))],
+    )(guess, rhs)
     last, initial = faces(guess, 1, 1)
     y_before = ring(last, "gy", 1)
     y_after = ring(initial, "gy", -1)

time: 35.9 us -> 38.2 us (1.064)
  waiting for transfers between devices: 11.7 us -> 16.3 us
  starting transfers between devices: 17 us -> 14.7 us
  Pallas kernels: 3.82 us -> 5.38 us
  local copies, waits for them, and re-layouts: 2.36 us -> 0.82 us
    ppermute x2, waiting for transfers between devices: 2.05 us -> 8.94 us  [z_exchange(): return lax.ppermute(array, ('gz', 'gx'), moves)]
    ppermute x7, starting transfers between devices: 8.87 us -> 6.12 us  [sum_over_all(): lax.ppermute(value, AXES, [(i, i ^ mask) for i in range(devices)])]
    ppermute x3, waiting for transfers between devices: 1.99 us -> 0.07 us  [ring(): lax.ppermute(array, axis, [(i, (i + step) % peers) for i in range(peers)])]
    pallas_call x0 -> x1, Pallas kernels: none -> 1.56 us  [local(): call(load, (in_vmem, in_vmem), 1 << 20, limit=60 << 20, in_specs=[HBM] *...]
    slice x1, local copies, waits for them, and re-layouts: 0.94 us -> 0.07 us  [faces(): last = lax.slice_in_dim(array, length - width, length, axis=dim)]
    unnamed x6 -> x2, local copies, waits for them, and re-layouts: 1.24 us -> 0.56 us
    ppermute x3, starting transfers between devices: 3.48 us -> 4.05 us  [ring(): lax.ppermute(array, axis, [(i, (i + step) % peers) for i in range(peers)])]
  transfers between devices with their start and end apart: 12 -> 12, of which waited for: 9 -> 8; matrix products, arithmetic and copies ran while one was open for 1% -> 1% of each run, Pallas kernels for 7% -> 6%
where the time goes in v6:
time: 38.2 us; the launch traced here: 38 us
  waiting for transfers between devices  16.3 us (43%)
  starting transfers between devices  14.7 us (38%)
  Pallas kernels  5.38 us (14%)
  local copies, waits for them, and re-layouts  0.82 us (2%)
  between operations  0.72 us (2%)
    ppermute x2, waiting for transfers between devices, z_exchange(): return lax.ppermute(array, ('gz', 'gx'), moves)  8.94 us
    ppermute x7, waiting for transfers between devices, sum_over_all(): lax.ppermute(value, AXES, [(i, i ^ mask) for i in range(devices)])  7.28 us
    ppermute x7, starting transfers between devices, sum_over_all(): lax.ppermute(value, AXES, [(i, i ^ mask) for i in range(devices)])  6.12 us
    ppermute x2, starting transfers between devices, z_exchange(): return lax.ppermute(array, ('gz', 'gx'), moves)  4.53 us
    ppermute x3, starting transfers between devices, ring(): lax.ppermute(array, axis, [(i, (i + step) % peers) for i in range(peers)])  4.05 us
    pallas_call x1, Pallas kernels, local(): call(load, (in_vmem, in_vmem), 1 << 20, limit=60 << 20, in_specs=[HBM] *...  1.56 us
    pallas_call x1, Pallas kernels, local(): call(functools.partial(final, total_cells), (whole, jax.ShapeDtypeStruct(...  1.12 us
    pallas_call x1, Pallas kernels, local(): call(z_faces, (in_vmem, in_vmem), 1 << 20, limit=60 << 20, in_specs=[HBM]...  1.04 us
  transfers between devices with their start and end apart: 12, of which 8 were waited for; matrix products, arithmetic and copies ran while one was open for 1% of the time, Pallas kernels for 6%

profile of v6, /device:TPU:0, one launch (start us, length us, event | category | flops | bytes accessed | tf_op | source)
XLA Modules:
  0.0 38.0 jit_solution(18260737910148995157)
XLA Ops:
  0.6 1.6 %shard_map.50 = (f32[4,16,4096]{2,1,0:T(8,128)S(1)}, f32[4,16,4096]{2,1,0:T(8,128)S(1)}) custom-call(f32[4,16,4096]{2,1,0:T(8,128)} %g_ref.3, f32[4,16,4096]{2,1,0:T(8,128)} %b_ref.1), custom_call_target="tpu_custom_call" | custom-call | flops 1048576 | bytes 1048576 | tf_op jit(solution)/shard_map/pallas_call | solution.py:237
  2.2 0.1 fusion.1
  2.3 3.0 %collective-permute-start = (f32[4,1,4096]{2,1,0:T(1,128)S(1)}, f32[4,1,4096]{2,1,0:T(1,128)S(1)}, u32[]{:S(2)}, u32[]{:S(2)}) collective-permute-start(f32[4,1,4096]{2,1,0:T(1,128)S(1)} %get-tuple-element.25), channel_id=1, source_target_pairs={{0,2},{2,4},{4,6},{6,0},{1,3},{3,5},{5,7},{7,1},{8,10},{10,12},{12... | collective-permute-start | bytes 196616 | tf_op jit(solution)/shard_map/ppermute | solution.py:19
  5.3 1.0 %collective-permute-start.1 = (f32[4,1,4096]{2,1,0:T(1,128)S(1)}, f32[4,1,4096]{2,1,0:T(1,128)S(1)}, u32[]{:S(2)}, u32[]{:S(2)}) collective-permute-start(f32[4,1,4096]{2,1,0:T(1,128)S(1)} %get-tuple-element.24), channel_id=1, source_target_pairs={{0,6},{2,0},{4,2},{6,4},{1,7},{3,1},{5,3},{7,5},{8,14},{10,8},{12,... | collective-permute-start | bytes 196616 | tf_op jit(solution)/shard_map/ppermute | solution.py:19
  6.3 1.0 %shard_map.53 = (f32[1,16,4096]{2,1,0:T(8,128)S(1)}, f32[1,16,4096]{2,1,0:T(8,128)S(1)}) custom-call(f32[4,16,4096]{2,1,0:T(8,128)} %g_ref.3), custom_call_target="tpu_custom_call" | custom-call | flops 1048576 | bytes 1048576 | tf_op jit(solution)/shard_map/pallas_call | solution.py:225
  7.4 2.1 %collective-permute-start.3 = (f32[1,16,4096]{2,1,0:T(8,128)S(1)}, f32[1,16,4096]{2,1,0:T(8,128)S(1)}, u32[]{:S(2)}, u32[]{:S(2)}) collective-permute-start(f32[1,16,4096]{2,1,0:T(8,128)S(1)} %get-tuple-element.15), channel_id=1, source_target_pairs={{0,8},{1,25},{8,0},{9,17},{16,24},{17,9},{24,16},{25,1},{2,10},{3,... | collective-permute-start | bytes 786440 | tf_op jit(solution)/shard_map/ppermute | solution.py:212
  9.4 2.5 %collective-permute-start.4 = (f32[1,16,4096]{2,1,0:T(8,128)S(1)}, f32[1,16,4096]{2,1,0:T(8,128)S(1)}, u32[]{:S(2)}, u32[]{:S(2)}) collective-permute-start(f32[1,16,4096]{2,1,0:T(8,128)S(1)} %get-tuple-element.16), channel_id=1, source_target_pairs={{0,24},{1,9},{8,16},{9,1},{16,8},{17,25},{24,0},{25,17},{2,26},{3,... | collective-permute-start | bytes 786440 | tf_op jit(solution)/shard_map/ppermute | solution.py:212
  11.9 0.1 fusion
  12.0 0.0 copy-start
  12.0 0.1 pad_maximum_fusion
  12.1 0.0 collective-permute-start.2
  12.1 0.6 %copy-done = f32[64]{0:T(128)S(1)} copy-done((f32[64]{0:T(128)S(1)}, f32[64]{0:T(128)}, u32[]{:S(2)}) %copy-start) | copy-done | bytes 280
  12.7 0.1 broadcast_in_dim_tile.3.c_ref
  12.8 0.5 %shard_map.51.i_ref = f32[4,16,4096]{2,1,0:T(8,128)S(1)} custom-call(f32[4,16,4096]{2,1,0:T(8,128)S(1)} %get-tuple-element.12.g_ref, f32[4,16,4096]{2,1,0:T(8,128)S(1)} %get-tuple-element.13.b_ref, f32[1,128]{1,0:T(1,128)S(1)} %broadcast_in_dim_tile.3.c_ref), custom_call_target="tpu_custom_call" | custom-call | flops 16777216 | bytes 1048576 | tf_op jit(solution)/shard_map/pallas_call | solution.py:257
  13.2 0.1 collective-permute-done.2.xh_ref
  13.3 0.0 collective-permute-done.yb_ref
  13.3 0.0 collective-permute-done.1.ya_ref
  13.3 0.6 %shard_map.52 = (f32[4,16,4096]{2,1,0:T(8,128)S(1)}, f32[128,128]{1,0:T(8,128)S(1)}) custom-call(f32[4,16,4096]{2,1,0:T(8,128)S(1)} %shard_map.51.i_ref, f32[4,1,4096]{2,1,0:T(1,128)S(1)} %collective-permute-done.yb_ref, f32[4,1,4096]{2,1,0:T(1,128)S(1)} %collective-permute-done.1.ya_ref, ...), custom_call_target="tpu_custom_call", output_to_operand_aliasing={{0}: (0, {})} | custom-call | flops 16777216 | bytes 1048576 | tf_op jit(solution)/shard_map/pallas_call | solution.py:258
  13.9 8.9 %collective-permute-done.4.h_ref = f32[1,16,4096]{2,1,0:T(8,128)S(1)} collective-permute-done((f32[1,16,4096]{2,1,0:T(8,128)S(1)}, f32[1,16,4096]{2,1,0:T(8,128)S(1)}, u32[]{:S(2)}, u32[]{:S(2)}) %collective-permute-start.4) | collective-permute-done | bytes 262176 | tf_op jit(solution)/shard_map/ppermute | solution.py:212
  22.9 0.2 shard_map.54
  23.1 0.0 collective-permute-done.3.h_ref
  23.1 0.3 shard_map.55
  23.5 0.0 collective-permute-start.5
  23.5 1.2 %collective-permute-done.5 = f32[32,128]{1,0:T(8,128)S(1)} collective-permute-done((f32[32,128]{1,0:T(8,128)S(1)}, f32[32,128]{1,0:T(8,128)S(1)}, u32[]{:S(2)}, u32[]{:S(2)}) %collective-permute-start.5) | collective-permute-done | bytes 16416 | tf_op jit(solution)/shard_map/ppermute | solution.py:44
  24.7 1.3 %collective-permute-start.7 = (f32[32,128]{1,0:T(8,128)S(1)}, f32[32,128]{1,0:T(8,128)S(1)}, u32[]{:S(2)}, u32[]{:S(2)}) collective-permute-start(f32[32,128]{1,0:T(8,128)S(1)} %add.29), channel_id=1, source_target_pairs={{0,5},{1,4},{2,7},{3,6},{4,1},{5,0},{6,3},{7,2},{8,13},{9,12},{10,... | collective-permute-start | bytes 49160 | tf_op jit(solution)/shard_map/ppermute | solution.py:44
  25.9 0.5 %collective-permute-start.8 = (f32[32,128]{1,0:T(8,128)S(1)}, f32[32,128]{1,0:T(8,128)S(1)}, u32[]{:S(2)}, u32[]{:S(2)}) collective-permute-start(f32[32,128]{1,0:T(8,128)S(1)} %add.29), channel_id=1, source_target_pairs={{0,6},{1,7},{2,4},{3,5},{4,2},{5,3},{6,0},{7,1},{8,14},{9,15},{10,... | collective-permute-start | bytes 49160 | tf_op jit(solution)/shard_map/ppermute | solution.py:44
  26.5 1.1 %collective-permute-start.6 = (f32[32,128]{1,0:T(8,128)S(1)}, f32[32,128]{1,0:T(8,128)S(1)}, u32[]{:S(2)}, u32[]{:S(2)}) collective-permute-start(f32[32,128]{1,0:T(8,128)S(1)} %add.29), channel_id=1, source_target_pairs={{0,3},{1,2},{2,1},{3,0},{4,7},{5,6},{6,5},{7,4},{8,11},{9,10},{10,... | collective-permute-start | bytes 49160 | tf_op jit(solution)/shard_map/ppermute | solution.py:44
  27.6 0.2 collective-permute-done.7
  27.8 2.9 %collective-permute-done.8 = f32[32,128]{1,0:T(8,128)S(1)} collective-permute-done((f32[32,128]{1,0:T(8,128)S(1)}, f32[32,128]{1,0:T(8,128)S(1)}, u32[]{:S(2)}, u32[]{:S(2)}) %collective-permute-start.8) | collective-permute-done | bytes 16416 | tf_op jit(solution)/shard_map/ppermute | solution.py:44
  30.7 0.0 collective-permute-done.6
  30.8 0.1 collective-permute-start.10
  30.8 2.9 %collective-permute-start.11 = (f32[32,128]{1,0:T(8,128)S(1)}, f32[32,128]{1,0:T(8,128)S(1)}, u32[]{:S(2)}, u32[]{:S(2)}) collective-permute-start(f32[32,128]{1,0:T(8,128)S(1)} %add_add_fusion.1), channel_id=1, source_target_pairs={{0,24},{1,25},{2,26},{3,27},{4,28},{5,29},{6,30},{7,31},{8,16},{9,... | collective-permute-start | bytes 49160 | tf_op jit(solution)/shard_map/ppermute | solution.py:44
  33.7 0.2 collective-permute-start.9
  33.9 0.9 %collective-permute-done.10 = f32[32,128]{1,0:T(8,128)S(1)} collective-permute-done((f32[32,128]{1,0:T(8,128)S(1)}, f32[32,128]{1,0:T(8,128)S(1)}, u32[]{:S(2)}, u32[]{:S(2)}) %collective-permute-start.10) | collective-permute-done | bytes 16416 | tf_op jit(solution)/shard_map/ppermute | solution.py:44
  34.9 1.6 %collective-permute-done.11 = f32[32,128]{1,0:T(8,128)S(1)} collective-permute-done((f32[32,128]{1,0:T(8,128)S(1)}, f32[32,128]{1,0:T(8,128)S(1)}, u32[]{:S(2)}, u32[]{:S(2)}) %collective-permute-start.11) | collective-permute-done | bytes 16416 | tf_op jit(solution)/shard_map/ppermute | solution.py:44
  36.4 0.4 %collective-permute-done.9 = f32[32,128]{1,0:T(8,128)S(1)} collective-permute-done((f32[32,128]{1,0:T(8,128)S(1)}, f32[32,128]{1,0:T(8,128)S(1)}, u32[]{:S(2)}, u32[]{:S(2)}) %collective-permute-start.9) | collective-permute-done | bytes 16416 | tf_op jit(solution)/shard_map/ppermute | solution.py:44
  36.9 1.1 %shard_map.56 = (f32[4,16,4096]{2,1,0:T(8,128)}, f32[64,64]{1,0:T(8,128)}) custom-call(f32[32,128]{1,0:T(8,128)S(1)} %add_add_fusion.p_ref, f32[4,16,4096]{2,1,0:T(8,128)S(1)} %get-tuple-element.14.l_ref, f32[1,16,4096]{2,1,0:T(8,128)S(1)} %get-tuple-element.20.first_ref, f32[1,16,4096]{2,1,0:T(8,128)S(1)} %get-tuple-element.21.second_ref), custom_call_target="tpu_custom_call" | custom-call | flops 4194304 | bytes 1048576 | tf_op jit(solution)/shard_map/pallas_call | solution.py:282
  (5 shorter events, 0.0 us)
Async XLA Ops:
  2.3 11.0 %collective-permute-start = (f32[4,1,4096]{2,1,0:T(1,128)S(1)}, f32[4,1,4096]{2,1,0:T(1,128)S(1)}, u32[]{:S(2)}, u32[]{:S(2)}) collective-permute-start(f32[4,1,4096]{2,1,0:T(1,128)S(1)} %get-tuple-element.25), channel_id=1, source_target_pairs={{0,2},{2,4},{4,6},{6,0},{1,3},{3,5},{5,7},{7,1},{8,10},{10,12},{12... | collective-permute-start | bytes 196616 | tf_op jit(solution)/shard_map/ppermute | solution.py:19
  5.3 8.0 %collective-permute-start.1 = (f32[4,1,4096]{2,1,0:T(1,128)S(1)}, f32[4,1,4096]{2,1,0:T(1,128)S(1)}, u32[]{:S(2)}, u32[]{:S(2)}) collective-permute-start(f32[4,1,4096]{2,1,0:T(1,128)S(1)} %get-tuple-element.24), channel_id=1, source_target_pairs={{0,6},{2,0},{4,2},{6,4},{1,7},{3,1},{5,3},{7,5},{8,14},{10,8},{12,... | collective-permute-start | bytes 196616 | tf_op jit(solution)/shard_map/ppermute | solution.py:19
  7.4 15.7 %collective-permute-start.3 = (f32[1,16,4096]{2,1,0:T(8,128)S(1)}, f32[1,16,4096]{2,1,0:T(8,128)S(1)}, u32[]{:S(2)}, u32[]{:S(2)}) collective-permute-start(f32[1,16,4096]{2,1,0:T(8,128)S(1)} %get-tuple-element.15), channel_id=1, source_target_pairs={{0,8},{1,25},{8,0},{9,17},{16,24},{17,9},{24,16},{25,1},{2,10},{3,... | collective-permute-start | bytes 786440 | tf_op jit(solution)/shard_map/ppermute | solution.py:212
  9.4 13.4 %collective-permute-start.4 = (f32[1,16,4096]{2,1,0:T(8,128)S(1)}, f32[1,16,4096]{2,1,0:T(8,128)S(1)}, u32[]{:S(2)}, u32[]{:S(2)}) collective-permute-start(f32[1,16,4096]{2,1,0:T(8,128)S(1)} %get-tuple-element.16), channel_id=1, source_target_pairs={{0,24},{1,9},{8,16},{9,1},{16,8},{17,25},{24,0},{25,17},{2,26},{3,... | collective-permute-start | bytes 786440 | tf_op jit(solution)/shard_map/ppermute | solution.py:212
  12.0 0.7 %copy-start = (f32[64]{0:T(128)S(1)}, f32[64]{0:T(128)}, u32[]{:S(2)}) copy-start(f32[64]{0:T(128)} %param.5) | copy-start | bytes 772
  12.1 1.2 %collective-permute-start.2 = (f32[4,16,128]{2,1,0:T(8,128)S(1)}, f32[4,16,128]{2,1,0:T(8,128)S(1)}, u32[]{:S(2)}, u32[]{:S(2)}) collective-permute-start(f32[4,16,128]{2,1,0:T(8,128)S(1)} %pad_maximum_fusion), channel_id=1, source_target_pairs={{0,1},{1,0},{2,3},{3,2},{4,5},{5,4},{6,7},{7,6},{8,9},{9,8},{10,11... | collective-permute-start | bytes 98312 | tf_op jit(solution)/shard_map/ppermute | solution.py:19
  23.5 1.2 %collective-permute-start.5 = (f32[32,128]{1,0:T(8,128)S(1)}, f32[32,128]{1,0:T(8,128)S(1)}, u32[]{:S(2)}, u32[]{:S(2)}) collective-permute-start(f32[32,128]{1,0:T(8,128)S(1)} %get-tuple-element.19), channel_id=1, source_target_pairs={{0,1},{1,0},{2,3},{3,2},{4,5},{5,4},{6,7},{7,6},{8,9},{9,8},{10,11... | collective-permute-start | bytes 49160 | tf_op jit(solution)/shard_map/ppermute | solution.py:44
  24.7 3.2 %collective-permute-start.7 = (f32[32,128]{1,0:T(8,128)S(1)}, f32[32,128]{1,0:T(8,128)S(1)}, u32[]{:S(2)}, u32[]{:S(2)}) collective-permute-start(f32[32,128]{1,0:T(8,128)S(1)} %add.29), channel_id=1, source_target_pairs={{0,5},{1,4},{2,7},{3,6},{4,1},{5,0},{6,3},{7,2},{8,13},{9,12},{10,... | collective-permute-start | bytes 49160 | tf_op jit(solution)/shard_map/ppermute | solution.py:44
  25.9 4.8 %collective-permute-start.8 = (f32[32,128]{1,0:T(8,128)S(1)}, f32[32,128]{1,0:T(8,128)S(1)}, u32[]{:S(2)}, u32[]{:S(2)}) collective-permute-start(f32[32,128]{1,0:T(8,128)S(1)} %add.29), channel_id=1, source_target_pairs={{0,6},{1,7},{2,4},{3,5},{4,2},{5,3},{6,0},{7,1},{8,14},{9,15},{10,... | collective-permute-start | bytes 49160 | tf_op jit(solution)/shard_map/ppermute | solution.py:44
  26.5 4.3 %collective-permute-start.6 = (f32[32,128]{1,0:T(8,128)S(1)}, f32[32,128]{1,0:T(8,128)S(1)}, u32[]{:S(2)}, u32[]{:S(2)}) collective-permute-start(f32[32,128]{1,0:T(8,128)S(1)} %add.29), channel_id=1, source_target_pairs={{0,3},{1,2},{2,1},{3,0},{4,7},{5,6},{6,5},{7,4},{8,11},{9,10},{10,... | collective-permute-start | bytes 49160 | tf_op jit(solution)/shard_map/ppermute | solution.py:44
  30.8 4.1 %collective-permute-start.10 = (f32[32,128]{1,0:T(8,128)S(1)}, f32[32,128]{1,0:T(8,128)S(1)}, u32[]{:S(2)}, u32[]{:S(2)}) collective-permute-start(f32[32,128]{1,0:T(8,128)S(1)} %add_add_fusion.1), channel_id=1, source_target_pairs={{0,17},{1,16},{2,19},{3,18},{4,21},{5,20},{6,23},{7,22},{8,25},{9,... | collective-permute-start | bytes 49160 | tf_op jit(solution)/shard_map/ppermute | solution.py:44
  30.8 5.6 %collective-permute-start.11 = (f32[32,128]{1,0:T(8,128)S(1)}, f32[32,128]{1,0:T(8,128)S(1)}, u32[]{:S(2)}, u32[]{:S(2)}) collective-permute-start(f32[32,128]{1,0:T(8,128)S(1)} %add_add_fusion.1), channel_id=1, source_target_pairs={{0,24},{1,25},{2,26},{3,27},{4,28},{5,29},{6,30},{7,31},{8,16},{9,... | collective-permute-start | bytes 49160 | tf_op jit(solution)/shard_map/ppermute | solution.py:44
  33.7 3.2 %collective-permute-start.9 = (f32[32,128]{1,0:T(8,128)S(1)}, f32[32,128]{1,0:T(8,128)S(1)}, u32[]{:S(2)}, u32[]{:S(2)}) collective-permute-start(f32[32,128]{1,0:T(8,128)S(1)} %add_add_fusion.1), channel_id=1, source_target_pairs={{0,9},{1,8},{2,11},{3,10},{4,13},{5,12},{6,15},{7,14},{8,1},{9,0},... | collective-permute-start | bytes 49160 | tf_op jit(solution)/shard_map/ppermute | solution.py:44

commit v7 on v6

--- a/solution.py
+++ b/solution.py
@@ -10,6 +10,7 @@
 
 AXES = ("gz", "gy", "gx")
 LANES = 128
+HOLD = 800
 VMEM = pl.BlockSpec(memory_space=pltpu.VMEM)
 HBM = pl.BlockSpec(memory_space=pltpu.HBM)
 
@@ -30,10 +31,10 @@
     bits = [1 << k for k in range(1, (devices - 1).bit_length())]
     stages = [(1,)]
     for low, high in zip(bits[0::2], bits[1::2]):
-        stages.append((low | high, high | 1, low | 1))
+        stages.append((low | high, high, low))
     if len(bits) % 2:
-        stages.append((bits[-1] | 1,))
-    return stages
+        stages.append((bits[-1],))
+    return stages[::-1]
 
 
 def sum_over_all(value):
@@ -76,8 +77,8 @@
 
 
 def outer_planes(planes):
-    same = lax.rem(lax.axis_index("gz") + lax.axis_index("gx"), 2) == 1
-    first = jnp.where(same, planes - 1, 0)
+    even = lax.rem(lax.axis_index("gz"), 2) == 0
+    first = jnp.where(even, planes - 1, 0)
     return first, planes - 1 - first
 
 
@@ -92,8 +93,10 @@
         copy.wait()
 
 
-def z_faces(g_ref, first_ref, second_ref, sem):
+def z_faces(g_ref, first_ref, second_ref, sem, spent):
     first, second = outer_planes(g_ref.shape[0])
+    odd = lax.rem(lax.axis_index("gx"), 2)
+    spent[0] = lax.fori_loop(0, odd * HOLD, lambda _, x: x * 1664525 + 1013904223, odd)
     run_copies(((g_ref.at[first], first_ref.at[0]), (g_ref.at[second], second_ref.at[0])), sem)
 
 
@@ -203,13 +206,9 @@
 
 
 def z_exchange(array, turn):
-    peers, cores = lax.axis_size("gz"), lax.axis_size("gx")
-    moves = []
-    for z in range(peers):
-        for core in range(cores):
-            up = (z + core + turn) % 2 == 1
-            moves.append((z * cores + core, (z + (1 if up else -1)) % peers * cores + core))
-    return lax.ppermute(array, ("gz", "gx"), moves)
+    peers = lax.axis_size("gz")
+    moves = [(z, (z + (1 if (z + turn) % 2 == 0 else -1)) % peers) for z in range(peers)]
+    return lax.ppermute(array, "gz", moves)
 
 
 def local(rhs, guess, shifts):
@@ -229,7 +228,7 @@
         limit=60 << 20,
         in_specs=[HBM],
         out_specs=[VMEM] * 2,
-        scratch_shapes=[pltpu.SemaphoreType.DMA((2,))],
+        scratch_shapes=[pltpu.SemaphoreType.DMA((2,)), pltpu.SMEM((1,), jnp.int32)],
     )(guess)
     first = z_exchange(first, 0)
     second = z_exchange(second, 1)

time: 38.2 us -> 41.5 us (1.086)
  starting transfers between devices: 14.7 us -> 16.8 us
  waiting for transfers between devices: 16.3 us -> 18.1 us
  local copies, waits for them, and re-layouts: 0.82 us -> 0.26 us
    ppermute x7, starting transfers between devices: 6.12 us -> 7.73 us  [sum_over_all(): lax.ppermute(value, AXES, [(i, i ^ mask) for i in range(devices)])]
    ppermute x2, waiting for transfers between devices: 8.94 us -> 10.3 us  [z_exchange(): return lax.ppermute(array, 'gz', moves)]
    ppermute x3, starting transfers between devices: 4.05 us -> 4.98 us  [ring(): lax.ppermute(array, axis, [(i, (i + step) % peers) for i in range(peers)])]
    unnamed x2, local copies, waits for them, and re-layouts: 0.56 us -> 0.01 us
    ppermute x2, starting transfers between devices: 4.53 us -> 4.08 us  [z_exchange(): return lax.ppermute(array, 'gz', moves)]
where the time goes in v7:
time: 41.5 us; the launch traced here: 41.4 us
  waiting for transfers between devices  18.1 us (44%)
  starting transfers between devices  16.8 us (40%)
  Pallas kernels  5.38 us (13%)
  between operations  0.71 us (2%)
    ppermute x2, waiting for transfers between devices, z_exchange(): return lax.ppermute(array, 'gz', moves)  10.3 us
    ppermute x7, starting transfers between devices, sum_over_all(): lax.ppermute(value, AXES, [(i, i ^ mask) for i in range(devices)])  7.73 us
    ppermute x7, waiting for transfers between devices, sum_over_all(): lax.ppermute(value, AXES, [(i, i ^ mask) for i in range(devices)])  7.57 us
    ppermute x3, starting transfers between devices, ring(): lax.ppermute(array, axis, [(i, (i + step) % peers) for i in range(peers)])  4.98 us
    ppermute x2, starting transfers between devices, z_exchange(): return lax.ppermute(array, 'gz', moves)  4.08 us
    pallas_call x1, Pallas kernels, local(): call(load, (in_vmem, in_vmem), 1 << 20, limit=60 << 20, in_specs=[HBM] *...  1.56 us
    pallas_call x1, Pallas kernels, local(): call(functools.partial(final, total_cells), (whole, jax.ShapeDtypeStruct(...  1.12 us
    pallas_call x1, Pallas kernels, local(): call(z_faces, (in_vmem, in_vmem), 1 << 20, limit=60 << 20, in_specs=[HBM]...  1.04 us
  transfers between devices with their start and end apart: 12, of which 8 were waited for; matrix products, arithmetic and copies ran while one was open for 1% of the time, Pallas kernels for 6%

profile of v7, /device:TPU:0, one launch (start us, length us, event | category | flops | bytes accessed | tf_op | source)
XLA Modules:
  0.0 41.4 jit_solution(3518330953914255338)
XLA Ops:
  0.6 1.6 %shard_map.50 = (f32[4,16,4096]{2,1,0:T(8,128)S(1)}, f32[4,16,4096]{2,1,0:T(8,128)S(1)}) custom-call(f32[4,16,4096]{2,1,0:T(8,128)} %g_ref.3, f32[4,16,4096]{2,1,0:T(8,128)} %b_ref.1), custom_call_target="tpu_custom_call" | custom-call | flops 1048576 | bytes 1048576 | tf_op jit(solution)/shard_map/pallas_call | solution.py:236
  2.2 0.1 fusion.1
  2.3 3.0 %collective-permute-start = (f32[4,1,4096]{2,1,0:T(1,128)S(1)}, f32[4,1,4096]{2,1,0:T(1,128)S(1)}, u32[]{:S(2)}, u32[]{:S(2)}) collective-permute-start(f32[4,1,4096]{2,1,0:T(1,128)S(1)} %get-tuple-element.25), channel_id=1, source_target_pairs={{0,2},{2,4},{4,6},{6,0},{1,3},{3,5},{5,7},{7,1},{8,10},{10,12},{12... | collective-permute-start | bytes 196616 | tf_op jit(solution)/shard_map/ppermute | solution.py:20
  5.3 1.0 %collective-permute-start.1 = (f32[4,1,4096]{2,1,0:T(1,128)S(1)}, f32[4,1,4096]{2,1,0:T(1,128)S(1)}, u32[]{:S(2)}, u32[]{:S(2)}) collective-permute-start(f32[4,1,4096]{2,1,0:T(1,128)S(1)} %get-tuple-element.24), channel_id=1, source_target_pairs={{0,6},{2,0},{4,2},{6,4},{1,7},{3,1},{5,3},{7,5},{8,14},{10,8},{12,... | collective-permute-start | bytes 196616 | tf_op jit(solution)/shard_map/ppermute | solution.py:20
  6.3 1.0 %shard_map.53 = (f32[1,16,4096]{2,1,0:T(8,128)S(1)}, f32[1,16,4096]{2,1,0:T(8,128)S(1)}) custom-call(f32[4,16,4096]{2,1,0:T(8,128)} %g_ref.3), custom_call_target="tpu_custom_call" | custom-call | flops 1048576 | bytes 1048576 | tf_op jit(solution)/shard_map/pallas_call | solution.py:224
  7.4 4.1 %collective-permute-start.3 = (f32[1,16,4096]{2,1,0:T(8,128)S(1)}, f32[1,16,4096]{2,1,0:T(8,128)S(1)}, u32[]{:S(2)}, u32[]{:S(2)}) collective-permute-start(f32[1,16,4096]{2,1,0:T(8,128)S(1)} %get-tuple-element.15), channel_id=1, source_target_pairs={{0,24},{8,16},{16,8},{24,0},{1,25},{9,17},{17,9},{25,1},{2,26},{10... | collective-permute-start | bytes 786440 | tf_op jit(solution)/shard_map/ppermute | solution.py:211
  11.5 0.0 collective-permute-start.4
  11.5 0.1 fusion
  11.6 0.0 copy-start
  11.6 0.1 pad_maximum_fusion
  11.6 0.9 %collective-permute-start.2 = (f32[4,16,128]{2,1,0:T(8,128)S(1)}, f32[4,16,128]{2,1,0:T(8,128)S(1)}, u32[]{:S(2)}, u32[]{:S(2)}) collective-permute-start(f32[4,16,128]{2,1,0:T(8,128)S(1)} %pad_maximum_fusion), channel_id=1, source_target_pairs={{0,1},{1,0},{2,3},{3,2},{4,5},{5,4},{6,7},{7,6},{8,9},{9,8},{10,11... | collective-permute-start | bytes 98312 | tf_op jit(solution)/shard_map/ppermute | solution.py:20
  12.6 0.0 copy-done
  12.6 0.1 broadcast_in_dim_tile.3.c_ref
  12.7 0.5 %shard_map.51.i_ref = f32[4,16,4096]{2,1,0:T(8,128)S(1)} custom-call(f32[4,16,4096]{2,1,0:T(8,128)S(1)} %get-tuple-element.12.g_ref, f32[4,16,4096]{2,1,0:T(8,128)S(1)} %get-tuple-element.13.b_ref, f32[1,128]{1,0:T(1,128)S(1)} %broadcast_in_dim_tile.3.c_ref), custom_call_target="tpu_custom_call" | custom-call | flops 16777216 | bytes 1048576 | tf_op jit(solution)/shard_map/pallas_call | solution.py:256
  13.2 0.3 collective-permute-done.2.xh_ref
  13.4 0.0 collective-permute-done.yb_ref
  13.4 0.0 collective-permute-done.1.ya_ref
  13.4 0.6 %shard_map.52 = (f32[4,16,4096]{2,1,0:T(8,128)S(1)}, f32[128,128]{1,0:T(8,128)S(1)}) custom-call(f32[4,16,4096]{2,1,0:T(8,128)S(1)} %shard_map.51.i_ref, f32[4,1,4096]{2,1,0:T(1,128)S(1)} %collective-permute-done.yb_ref, f32[4,1,4096]{2,1,0:T(1,128)S(1)} %collective-permute-done.1.ya_ref, ...), custom_call_target="tpu_custom_call", output_to_operand_aliasing={{0}: (0, {})} | custom-call | flops 16777216 | bytes 1048576 | tf_op jit(solution)/shard_map/pallas_call | solution.py:257
  14.1 10.3 %collective-permute-done.4.h_ref = f32[1,16,4096]{2,1,0:T(8,128)S(1)} collective-permute-done((f32[1,16,4096]{2,1,0:T(8,128)S(1)}, f32[1,16,4096]{2,1,0:T(8,128)S(1)}, u32[]{:S(2)}, u32[]{:S(2)}) %collective-permute-start.4) | collective-permute-done | bytes 262176 | tf_op jit(solution)/shard_map/ppermute | solution.py:211
  24.3 0.2 shard_map.54
  24.6 0.0 collective-permute-done.3.h_ref
  24.6 0.3 shard_map.55
  24.9 0.4 %collective-permute-start.6 = (f32[32,128]{1,0:T(8,128)S(1)}, f32[32,128]{1,0:T(8,128)S(1)}, u32[]{:S(2)}, u32[]{:S(2)}) collective-permute-start(f32[32,128]{1,0:T(8,128)S(1)} %get-tuple-element.19), channel_id=1, source_target_pairs={{0,16},{1,17},{2,18},{3,19},{4,20},{5,21},{6,22},{7,23},{8,24},{9,... | collective-permute-start | bytes 49160 | tf_op jit(solution)/shard_map/ppermute | solution.py:45
  25.3 3.7 %collective-permute-start.7 = (f32[32,128]{1,0:T(8,128)S(1)}, f32[32,128]{1,0:T(8,128)S(1)}, u32[]{:S(2)}, u32[]{:S(2)}) collective-permute-start(f32[32,128]{1,0:T(8,128)S(1)} %get-tuple-element.19), channel_id=1, source_target_pairs={{0,24},{1,25},{2,26},{3,27},{4,28},{5,29},{6,30},{7,31},{8,16},{9,... | collective-permute-start | bytes 49160 | tf_op jit(solution)/shard_map/ppermute | solution.py:45
  29.0 0.0 collective-permute-start.5
  29.0 0.5 %collective-permute-done.6 = f32[32,128]{1,0:T(8,128)S(1)} collective-permute-done((f32[32,128]{1,0:T(8,128)S(1)}, f32[32,128]{1,0:T(8,128)S(1)}, u32[]{:S(2)}, u32[]{:S(2)}) %collective-permute-start.6) | collective-permute-done | bytes 16416 | tf_op jit(solution)/shard_map/ppermute | solution.py:45
  29.6 1.3 %collective-permute-done.7 = f32[32,128]{1,0:T(8,128)S(1)} collective-permute-done((f32[32,128]{1,0:T(8,128)S(1)}, f32[32,128]{1,0:T(8,128)S(1)}, u32[]{:S(2)}, u32[]{:S(2)}) %collective-permute-start.7) | collective-permute-done | bytes 16416 | tf_op jit(solution)/shard_map/ppermute | solution.py:45
  30.9 1.9 %collective-permute-done.5 = f32[32,128]{1,0:T(8,128)S(1)} collective-permute-done((f32[32,128]{1,0:T(8,128)S(1)}, f32[32,128]{1,0:T(8,128)S(1)}, u32[]{:S(2)}, u32[]{:S(2)}) %collective-permute-start.5) | collective-permute-done | bytes 16416 | tf_op jit(solution)/shard_map/ppermute | solution.py:45
  32.8 1.6 %collective-permute-start.9 = (f32[32,128]{1,0:T(8,128)S(1)}, f32[32,128]{1,0:T(8,128)S(1)}, u32[]{:S(2)}, u32[]{:S(2)}) collective-permute-start(f32[32,128]{1,0:T(8,128)S(1)} %add_add_fusion.1), channel_id=1, source_target_pairs={{0,4},{1,5},{2,6},{3,7},{4,0},{5,1},{6,2},{7,3},{8,12},{9,13},{10,... | collective-permute-start | bytes 49160 | tf_op jit(solution)/shard_map/ppermute | solution.py:45
  34.3 0.0 collective-permute-start.10
  34.4 2.0 %collective-permute-start.8 = (f32[32,128]{1,0:T(8,128)S(1)}, f32[32,128]{1,0:T(8,128)S(1)}, u32[]{:S(2)}, u32[]{:S(2)}) collective-permute-start(f32[32,128]{1,0:T(8,128)S(1)} %add_add_fusion.1), channel_id=1, source_target_pairs={{0,2},{1,3},{2,0},{3,1},{4,6},{5,7},{6,4},{7,5},{8,10},{9,11},{10,... | collective-permute-start | bytes 49160 | tf_op jit(solution)/shard_map/ppermute | solution.py:45
  36.3 0.2 collective-permute-done.9
  36.6 2.4 %collective-permute-done.10 = f32[32,128]{1,0:T(8,128)S(1)} collective-permute-done((f32[32,128]{1,0:T(8,128)S(1)}, f32[32,128]{1,0:T(8,128)S(1)}, u32[]{:S(2)}, u32[]{:S(2)}) %collective-permute-start.10) | collective-permute-done | bytes 16416 | tf_op jit(solution)/shard_map/ppermute | solution.py:45
  39.0 0.0 collective-permute-done.8
  39.0 0.1 collective-permute-start.11
  39.1 1.2 %collective-permute-done.11 = f32[32,128]{1,0:T(8,128)S(1)} collective-permute-done((f32[32,128]{1,0:T(8,128)S(1)}, f32[32,128]{1,0:T(8,128)S(1)}, u32[]{:S(2)}, u32[]{:S(2)}) %collective-permute-start.11) | collective-permute-done | bytes 16416 | tf_op jit(solution)/shard_map/ppermute | solution.py:45
  40.3 1.1 %shard_map.56 = (f32[4,16,4096]{2,1,0:T(8,128)}, f32[64,64]{1,0:T(8,128)}) custom-call(f32[32,128]{1,0:T(8,128)S(1)} %add.35.p_ref, f32[4,16,4096]{2,1,0:T(8,128)S(1)} %get-tuple-element.14.l_ref, f32[1,16,4096]{2,1,0:T(8,128)S(1)} %get-tuple-element.20.first_ref, f32[1,16,4096]{2,1,0:T(8,128)S(1)} %get-tuple-element.21.second_ref), custom_call_target="tpu_custom_call" | custom-call | flops 4194304 | bytes 1048576 | tf_op jit(solution)/shard_map/pallas_call | solution.py:281
  (5 shorter events, 0.0 us)
Async XLA Ops:
  2.3 11.1 %collective-permute-start = (f32[4,1,4096]{2,1,0:T(1,128)S(1)}, f32[4,1,4096]{2,1,0:T(1,128)S(1)}, u32[]{:S(2)}, u32[]{:S(2)}) collective-permute-start(f32[4,1,4096]{2,1,0:T(1,128)S(1)} %get-tuple-element.25), channel_id=1, source_target_pairs={{0,2},{2,4},{4,6},{6,0},{1,3},{3,5},{5,7},{7,1},{8,10},{10,12},{12... | collective-permute-start | bytes 196616 | tf_op jit(solution)/shard_map/ppermute | solution.py:20
  5.3 8.1 %collective-permute-start.1 = (f32[4,1,4096]{2,1,0:T(1,128)S(1)}, f32[4,1,4096]{2,1,0:T(1,128)S(1)}, u32[]{:S(2)}, u32[]{:S(2)}) collective-permute-start(f32[4,1,4096]{2,1,0:T(1,128)S(1)} %get-tuple-element.24), channel_id=1, source_target_pairs={{0,6},{2,0},{4,2},{6,4},{1,7},{3,1},{5,3},{7,5},{8,14},{10,8},{12,... | collective-permute-start | bytes 196616 | tf_op jit(solution)/shard_map/ppermute | solution.py:20
  7.4 17.2 %collective-permute-start.3 = (f32[1,16,4096]{2,1,0:T(8,128)S(1)}, f32[1,16,4096]{2,1,0:T(8,128)S(1)}, u32[]{:S(2)}, u32[]{:S(2)}) collective-permute-start(f32[1,16,4096]{2,1,0:T(8,128)S(1)} %get-tuple-element.15), channel_id=1, source_target_pairs={{0,24},{8,16},{16,8},{24,0},{1,25},{9,17},{17,9},{25,1},{2,26},{10... | collective-permute-start | bytes 786440 | tf_op jit(solution)/shard_map/ppermute | solution.py:211
  11.5 12.9 %collective-permute-start.4 = (f32[1,16,4096]{2,1,0:T(8,128)S(1)}, f32[1,16,4096]{2,1,0:T(8,128)S(1)}, u32[]{:S(2)}, u32[]{:S(2)}) collective-permute-start(f32[1,16,4096]{2,1,0:T(8,128)S(1)} %get-tuple-element.16), channel_id=1, source_target_pairs={{0,8},{8,0},{16,24},{24,16},{1,9},{9,1},{17,25},{25,17},{2,10},{10... | collective-permute-start | bytes 786440 | tf_op jit(solution)/shard_map/ppermute | solution.py:211
  11.6 1.0 %copy-start = (f32[64]{0:T(128)S(1)}, f32[64]{0:T(128)}, u32[]{:S(2)}) copy-start(f32[64]{0:T(128)} %param.5) | copy-start | bytes 772
  11.6 1.8 %collective-permute-start.2 = (f32[4,16,128]{2,1,0:T(8,128)S(1)}, f32[4,16,128]{2,1,0:T(8,128)S(1)}, u32[]{:S(2)}, u32[]{:S(2)}) collective-permute-start(f32[4,16,128]{2,1,0:T(8,128)S(1)} %pad_maximum_fusion), channel_id=1, source_target_pairs={{0,1},{1,0},{2,3},{3,2},{4,5},{5,4},{6,7},{7,6},{8,9},{9,8},{10,11... | collective-permute-start | bytes 98312 | tf_op jit(solution)/shard_map/ppermute | solution.py:20
  24.9 4.7 %collective-permute-start.6 = (f32[32,128]{1,0:T(8,128)S(1)}, f32[32,128]{1,0:T(8,128)S(1)}, u32[]{:S(2)}, u32[]{:S(2)}) collective-permute-start(f32[32,128]{1,0:T(8,128)S(1)} %get-tuple-element.19), channel_id=1, source_target_pairs={{0,16},{1,17},{2,18},{3,19},{4,20},{5,21},{6,22},{7,23},{8,24},{9,... | collective-permute-start | bytes 49160 | tf_op jit(solution)/shard_map/ppermute | solution.py:45
  25.3 5.6 %collective-permute-start.7 = (f32[32,128]{1,0:T(8,128)S(1)}, f32[32,128]{1,0:T(8,128)S(1)}, u32[]{:S(2)}, u32[]{:S(2)}) collective-permute-start(f32[32,128]{1,0:T(8,128)S(1)} %get-tuple-element.19), channel_id=1, source_target_pairs={{0,24},{1,25},{2,26},{3,27},{4,28},{5,29},{6,30},{7,31},{8,16},{9,... | collective-permute-start | bytes 49160 | tf_op jit(solution)/shard_map/ppermute | solution.py:45
  29.0 3.7 %collective-permute-start.5 = (f32[32,128]{1,0:T(8,128)S(1)}, f32[32,128]{1,0:T(8,128)S(1)}, u32[]{:S(2)}, u32[]{:S(2)}) collective-permute-start(f32[32,128]{1,0:T(8,128)S(1)} %get-tuple-element.19), channel_id=1, source_target_pairs={{0,8},{1,9},{2,10},{3,11},{4,12},{5,13},{6,14},{7,15},{8,0},{9,1},... | collective-permute-start | bytes 49160 | tf_op jit(solution)/shard_map/ppermute | solution.py:45
  32.8 3.8 %collective-permute-start.9 = (f32[32,128]{1,0:T(8,128)S(1)}, f32[32,128]{1,0:T(8,128)S(1)}, u32[]{:S(2)}, u32[]{:S(2)}) collective-permute-start(f32[32,128]{1,0:T(8,128)S(1)} %add_add_fusion.1), channel_id=1, source_target_pairs={{0,4},{1,5},{2,6},{3,7},{4,0},{5,1},{6,2},{7,3},{8,12},{9,13},{10,... | collective-permute-start | bytes 49160 | tf_op jit(solution)/shard_map/ppermute | solution.py:45
  34.3 4.6 %collective-permute-start.10 = (f32[32,128]{1,0:T(8,128)S(1)}, f32[32,128]{1,0:T(8,128)S(1)}, u32[]{:S(2)}, u32[]{:S(2)}) collective-permute-start(f32[32,128]{1,0:T(8,128)S(1)} %add_add_fusion.1), channel_id=1, source_target_pairs={{0,6},{1,7},{2,4},{3,5},{4,2},{5,3},{6,0},{7,1},{8,14},{9,15},{10,... | collective-permute-start | bytes 49160 | tf_op jit(solution)/shard_map/ppermute | solution.py:45
  34.4 4.6 %collective-permute-start.8 = (f32[32,128]{1,0:T(8,128)S(1)}, f32[32,128]{1,0:T(8,128)S(1)}, u32[]{:S(2)}, u32[]{:S(2)}) collective-permute-start(f32[32,128]{1,0:T(8,128)S(1)} %add_add_fusion.1), channel_id=1, source_target_pairs={{0,2},{1,3},{2,0},{3,1},{4,6},{5,7},{6,4},{7,5},{8,10},{9,11},{10,... | collective-permute-start | bytes 49160 | tf_op jit(solution)/shard_map/ppermute | solution.py:45
  39.0 1.2 %collective-permute-start.11 = (f32[32,128]{1,0:T(8,128)S(1)}, f32[32,128]{1,0:T(8,128)S(1)}, u32[]{:S(2)}, u32[]{:S(2)}) collective-permute-start(f32[32,128]{1,0:T(8,128)S(1)} %add_add_fusion), channel_id=1, source_target_pairs={{0,1},{1,0},{2,3},{3,2},{4,5},{5,4},{6,7},{7,6},{8,9},{9,8},{10,11... | collective-permute-start | bytes 49160 | tf_op jit(solution)/shard_map/ppermute | solution.py:45

commit v8 on v7

--- a/solution.py
+++ b/solution.py
@@ -10,7 +10,7 @@
 
 AXES = ("gz", "gy", "gx")
 LANES = 128
-HOLD = 800
+HOLD = 950
 VMEM = pl.BlockSpec(memory_space=pltpu.VMEM)
 HBM = pl.BlockSpec(memory_space=pltpu.HBM)
 
@@ -82,6 +82,10 @@
     return first, planes - 1 - first
 
 
+def is_odd_core():
+    return lax.rem(lax.axis_index("gx"), 2) == 1
+
+
 def run_copies(pairs, sem):
     copies = [
         pltpu.make_async_copy(source, target, sem.at[k])
@@ -93,23 +97,13 @@
         copy.wait()
 
 
-def z_faces(g_ref, first_ref, second_ref, sem, spent):
-    first, second = outer_planes(g_ref.shape[0])
-    odd = lax.rem(lax.axis_index("gx"), 2)
-    spent[0] = lax.fori_loop(0, odd * HOLD, lambda _, x: x * 1664525 + 1013904223, odd)
-    run_copies(((g_ref.at[first], first_ref.at[0]), (g_ref.at[second], second_ref.at[0])), sem)
-
-
-def load(g_ref, b_ref, g_out, b_out, sem):
-    run_copies(((g_ref, g_out), (b_ref, b_out)), sem)
-
-
-def inside(g_ref, b_ref, c_ref, l_ref):
+def inside(g_ref, b_ref, s_ref, l_ref):
     planes, rows, width = g_ref.shape
     chunks = width // LANES
     row = lax.broadcasted_iota(jnp.int32, (rows, LANES), 0)
     low = lax.broadcasted_iota(jnp.int32, (rows, LANES), 1) < LANES // 2
-    centre = jnp.broadcast_to(c_ref[...], (rows, LANES))
+    centre = 6.0 + s_ref[...]
+    centre = jnp.broadcast_to(jnp.concatenate([centre, centre], axis=1), (rows, LANES))
     none = jnp.zeros((rows, LANES), jnp.float32)
     for z in range(planes):
         before, here = none, half_roll(g_ref[z, :, pl.ds(0, LANES)])
@@ -129,6 +123,36 @@
                 near = near + g_ref[z + 1, :, at]
             l_ref[z, :, at] = b_ref[z, :, at] - (centre * x - near)
             before, here = here, after
+
+
+def head(g_ref, b_ref, s_ref, first_ref, second_ref, g_out, l_out, b_buf, s_buf, spent, sem):
+    first, second = outer_planes(g_ref.shape[0])
+    faces = ((g_ref.at[first], first_ref.at[0]), (g_ref.at[second], second_ref.at[0]))
+    odd = is_odd_core()
+
+    @pl.when(odd)
+    def _():
+        run_copies(faces + ((g_ref, g_out), (b_ref, b_buf), (s_ref, s_buf)), sem)
+        inside(g_out, b_buf, s_buf, l_out)
+        spent[0] = lax.fori_loop(0, HOLD, lambda _, x: x * 1664525 + 1013904223, 1)
+
+    @pl.when(jnp.logical_not(odd))
+    def _():
+        run_copies(faces, sem)
+
+
+def rest(g_ref, b_ref, s_ref, g_in, l_in, g_out, l_out, b_buf, s_buf, sem):
+    odd = is_odd_core()
+
+    @pl.when(odd)
+    def _():
+        g_out[...] = g_in[...]
+        l_out[...] = l_in[...]
+
+    @pl.when(jnp.logical_not(odd))
+    def _():
+        run_copies(((g_ref, g_out), (b_ref, b_buf), (s_ref, s_buf)), sem)
+        inside(g_out, b_buf, s_buf, l_out)
 
 
 def edges(i_ref, yb_ref, ya_ref, xh_ref, l_ref, gram_ref):
@@ -220,28 +244,32 @@
     face = jax.ShapeDtypeStruct((1, y_cells, lane_count), f32)
     square = jax.ShapeDtypeStruct((LANES, LANES), f32)
     packed = jax.ShapeDtypeStruct((columns // 2, LANES), f32)
-    in_vmem = pltpu.VMEM((1, y_cells, lane_count), f32)
-    first, second = call(
-        z_faces,
-        (in_vmem, in_vmem),
+    face_in_vmem = pltpu.VMEM((1, y_cells, lane_count), f32)
+    whole_in_vmem = pltpu.VMEM(guess.shape, f32)
+    small = shifts[None]
+    scratch = [whole_in_vmem, pltpu.VMEM((1, columns), f32)]
+    first, second, held, left = call(
+        head,
+        (face_in_vmem,) * 2 + (whole_in_vmem,) * 2,
         1 << 20,
         limit=60 << 20,
-        in_specs=[HBM],
-        out_specs=[VMEM] * 2,
-        scratch_shapes=[pltpu.SemaphoreType.DMA((2,)), pltpu.SMEM((1,), jnp.int32)],
-    )(guess)
+        in_specs=[HBM] * 3,
+        out_specs=[VMEM] * 4,
+        scratch_shapes=scratch
+        + [pltpu.SMEM((1,), jnp.int32), pltpu.SemaphoreType.DMA((5,))],
+    )(guess, rhs, small)
     first = z_exchange(first, 0)
     second = z_exchange(second, 1)
-    in_vmem = pltpu.VMEM(guess.shape, f32)
-    guess, rhs = call(
-        load,
-        (in_vmem, in_vmem),
+    guess, left = call(
+        rest,
+        (whole_in_vmem,) * 2,
         1 << 20,
         limit=60 << 20,
-        in_specs=[HBM] * 2,
+        in_specs=[HBM] * 3 + [VMEM] * 2,
         out_specs=[VMEM] * 2,
-        scratch_shapes=[pltpu.SemaphoreType.DMA((2,))],
-    )(guess, rhs)
+        scratch_shapes=scratch + [pltpu.SemaphoreType.DMA((3,))],
+        input_output_aliases={3: 0, 4: 1},
+    )(guess, rhs, small, held, left)
     last, initial = faces(guess, 1, 1)
     y_before = ring(last, "gy", 1)
     y_after = ring(initial, "gy", -1)
@@ -252,8 +280,6 @@
         x_halos = jnp.concatenate(
             [ring(last, "gx", 1), ring(initial, "gx", -1)], axis=2
         )
-    centre = jnp.tile(6.0 + shifts, LANES // columns)[None]
-    left = call(inside, whole, 1 << 24, in_specs=[VMEM] * 3, out_specs=VMEM)(guess, rhs, centre)
     left, gram = call(
         edges,
         (whole, square),

time: 41.5 us -> 40.5 us (0.976)
  waiting for transfers between devices: 18.1 us -> 14.6 us
  starting transfers between devices: 16.8 us -> 19.4 us
    ppermute x2, waiting for transfers between devices: 10.3 us -> 6.9 us  [z_exchange(): return lax.ppermute(array, 'gz', moves)]
    ppermute x3, starting transfers between devices: 4.98 us -> 7.66 us  [ring(): lax.ppermute(array, axis, [(i, (i + step) % peers) for i in range(peers)])]
    ppermute x7, waiting for transfers between devices: 7.57 us -> 6.79 us  [sum_over_all(): lax.ppermute(value, AXES, [(i, i ^ mask) for i in range(devices)])]
    ppermute x3, waiting for transfers between devices: 0.29 us -> 0.87 us  [ring(): lax.ppermute(array, axis, [(i, (i + step) % peers) for i in range(peers)])]
    ppermute x2, starting transfers between devices: 4.08 us -> 3.6 us  [z_exchange(): return lax.ppermute(array, 'gz', moves)]
    pallas_call x3 -> x2, Pallas kernels: 3.08 us -> 3.17 us  [the longest x1 2.08 us: local(): call(rest, (whole_in_vmem,) * 2, 1 << 20, limit=60 << 20, in_specs=[HBM]...]
  transfers between devices with their start and end apart: 12 -> 12, of which waited for: 8 -> 8; matrix products, arithmetic and copies ran while one was open for 1% -> 0% of each run, Pallas kernels for 6% -> 2%
where the time goes in v8:
time: 40.5 us; the launch traced here: 40.4 us
  starting transfers between devices  19.4 us (48%)
  waiting for transfers between devices  14.6 us (36%)
  Pallas kernels  5.46 us (13%)
  between operations  0.7 us (2%)
    ppermute x7, starting transfers between devices, sum_over_all(): lax.ppermute(value, AXES, [(i, i ^ mask) for i in range(devices)])  8.13 us
    ppermute x3, starting transfers between devices, ring(): lax.ppermute(array, axis, [(i, (i + step) % peers) for i in range(peers)])  7.66 us
    ppermute x2, waiting for transfers between devices, z_exchange(): return lax.ppermute(array, 'gz', moves)  6.9 us
    ppermute x7, waiting for transfers between devices, sum_over_all(): lax.ppermute(value, AXES, [(i, i ^ mask) for i in range(devices)])  6.79 us
    ppermute x2, starting transfers between devices, z_exchange(): return lax.ppermute(array, 'gz', moves)  3.6 us
    pallas_call x1, Pallas kernels, local(): call(rest, (whole_in_vmem,) * 2, 1 << 20, limit=60 << 20, in_specs=[HBM]...  2.08 us
    pallas_call x1, Pallas kernels, local(): call(functools.partial(final, total_cells), (whole, jax.ShapeDtypeStruct(...  1.12 us
    pallas_call x1, Pallas kernels, local(): call(head, (face_in_vmem,) * 2 + (whole_in_vmem,) * 2, 1 << 20, limit=60...  1.09 us
  transfers between devices with their start and end apart: 12, of which 8 were waited for; matrix products, arithmetic and copies ran while one was open for 0% of the time, Pallas kernels for 2%

profile of v8, /device:TPU:0, one launch (start us, length us, event | category | flops | bytes accessed | tf_op | source)
XLA Modules:
  0.0 40.4 jit_solution(15585735332597793107)
XLA Ops:
  0.6 1.1 %shard_map.50 = (f32[1,16,4096]{2,1,0:T(8,128)S(1)}, f32[1,16,4096]{2,1,0:T(8,128)S(1)}, f32[4,16,4096]{2,1,0:T(8,128)S(1)}, f32[4,16,4096]{2,1,0:T(8,128)S(1)}) custom-call(f32[4,16,4096]{2,1,0:T(8,128)} %g_ref.3, f32[4,16,4096]{2,1,0:T(8,128)} %b_ref.3, f32[1,64]{1,0:T(1,128)} %bitcast.1), custom_call_target="tpu_custom_call" | custom-call | flops 1048576 | bytes 1048576 | tf_op jit(solution)/shard_map/pallas_call | solution.py:251
  1.7 2.1 %shard_map.51 = (f32[4,16,4096]{2,1,0:T(8,128)S(1)}, f32[4,16,4096]{2,1,0:T(8,128)S(1)}) custom-call(f32[4,16,4096]{2,1,0:T(8,128)} %g_ref.3, f32[4,16,4096]{2,1,0:T(8,128)} %b_ref.3, f32[1,64]{1,0:T(1,128)} %bitcast.2, f32[4,16,4096]{2,1,0:T(8,128)S(1)} %get-tuple-element.14.g_in, ...), custom_call_target="tpu_custom_call", output_to_operand_aliasing={{0}: (3, {}), {1}: (4, {})} | custom-call | flops 1048576 | bytes 1048576 | tf_op jit(solution)/shard_map/pallas_call | solution.py:263
  3.8 0.1 fusion.1
  3.9 4.0 %collective-permute-start.1 = (f32[4,1,4096]{2,1,0:T(1,128)S(1)}, f32[4,1,4096]{2,1,0:T(1,128)S(1)}, u32[]{:S(2)}, u32[]{:S(2)}) collective-permute-start(f32[4,1,4096]{2,1,0:T(1,128)S(1)} %get-tuple-element.28), channel_id=1, source_target_pairs={{0,6},{2,0},{4,2},{6,4},{1,7},{3,1},{5,3},{7,5},{8,14},{10,8},{12,... | collective-permute-start | bytes 196616 | tf_op jit(solution)/shard_map/ppermute | solution.py:20
  7.9 0.0 collective-permute-start
  7.9 3.6 %collective-permute-start.3 = (f32[1,16,4096]{2,1,0:T(8,128)S(1)}, f32[1,16,4096]{2,1,0:T(8,128)S(1)}, u32[]{:S(2)}, u32[]{:S(2)}) collective-permute-start(f32[1,16,4096]{2,1,0:T(8,128)S(1)} %get-tuple-element.19), channel_id=1, source_target_pairs={{0,24},{8,16},{16,8},{24,0},{1,25},{9,17},{17,9},{25,1},{2,26},{10... | collective-permute-start | bytes 786440 | tf_op jit(solution)/shard_map/ppermute | solution.py:235
  11.5 0.0 collective-permute-start.4
  11.5 0.1 fusion
  11.6 0.1 pad_maximum_fusion
  11.7 3.7 %collective-permute-start.2 = (f32[4,16,128]{2,1,0:T(8,128)S(1)}, f32[4,16,128]{2,1,0:T(8,128)S(1)}, u32[]{:S(2)}, u32[]{:S(2)}) collective-permute-start(f32[4,16,128]{2,1,0:T(8,128)S(1)} %pad_maximum_fusion), channel_id=1, source_target_pairs={{0,1},{1,0},{2,3},{3,2},{4,5},{5,4},{6,7},{7,6},{8,9},{9,8},{10,11... | collective-permute-start | bytes 98312 | tf_op jit(solution)/shard_map/ppermute | solution.py:20
  15.3 0.9 %collective-permute-done.2.xh_ref = f32[4,16,128]{2,1,0:T(8,128)S(1)} collective-permute-done((f32[4,16,128]{2,1,0:T(8,128)S(1)}, f32[4,16,128]{2,1,0:T(8,128)S(1)}, u32[]{:S(2)}, u32[]{:S(2)}) %collective-permute-start.2) | collective-permute-done | bytes 32800 | tf_op jit(solution)/shard_map/ppermute | solution.py:20
  16.2 0.0 collective-permute-done.1.ya_ref
  16.2 0.0 collective-permute-done.yb_ref
  16.2 0.6 %shard_map.52 = (f32[4,16,4096]{2,1,0:T(8,128)S(1)}, f32[128,128]{1,0:T(8,128)S(1)}) custom-call(f32[4,16,4096]{2,1,0:T(8,128)S(1)} %get-tuple-element.16.i_ref, f32[4,1,4096]{2,1,0:T(1,128)S(1)} %collective-permute-done.yb_ref, f32[4,1,4096]{2,1,0:T(1,128)S(1)} %collective-permute-done.1.ya_ref, ...), custom_call_target="tpu_custom_call", output_to_operand_aliasing={{0}: (0, {})} | custom-call | flops 16777216 | bytes 1048576 | tf_op jit(solution)/shard_map/pallas_call | solution.py:283
  16.8 6.9 %collective-permute-done.4.h_ref = f32[1,16,4096]{2,1,0:T(8,128)S(1)} collective-permute-done((f32[1,16,4096]{2,1,0:T(8,128)S(1)}, f32[1,16,4096]{2,1,0:T(8,128)S(1)}, u32[]{:S(2)}, u32[]{:S(2)}) %collective-permute-start.4) | collective-permute-done | bytes 262176 | tf_op jit(solution)/shard_map/ppermute | solution.py:235
  23.7 0.2 shard_map.53
  24.0 0.0 collective-permute-done.3.h_ref
  24.0 0.3 shard_map.54
  24.3 0.5 %collective-permute-start.7 = (f32[32,128]{1,0:T(8,128)S(1)}, f32[32,128]{1,0:T(8,128)S(1)}, u32[]{:S(2)}, u32[]{:S(2)}) collective-permute-start(f32[32,128]{1,0:T(8,128)S(1)} %get-tuple-element.23), channel_id=1, source_target_pairs={{0,24},{1,25},{2,26},{3,27},{4,28},{5,29},{6,30},{7,31},{8,16},{9,... | collective-permute-start | bytes 49160 | tf_op jit(solution)/shard_map/ppermute | solution.py:45
  24.8 0.6 %collective-permute-start.6 = (f32[32,128]{1,0:T(8,128)S(1)}, f32[32,128]{1,0:T(8,128)S(1)}, u32[]{:S(2)}, u32[]{:S(2)}) collective-permute-start(f32[32,128]{1,0:T(8,128)S(1)} %get-tuple-element.23), channel_id=1, source_target_pairs={{0,16},{1,17},{2,18},{3,19},{4,20},{5,21},{6,22},{7,23},{8,24},{9,... | collective-permute-start | bytes 49160 | tf_op jit(solution)/shard_map/ppermute | solution.py:45
  25.4 3.3 %collective-permute-start.5 = (f32[32,128]{1,0:T(8,128)S(1)}, f32[32,128]{1,0:T(8,128)S(1)}, u32[]{:S(2)}, u32[]{:S(2)}) collective-permute-start(f32[32,128]{1,0:T(8,128)S(1)} %get-tuple-element.23), channel_id=1, source_target_pairs={{0,8},{1,9},{2,10},{3,11},{4,12},{5,13},{6,14},{7,15},{8,0},{9,1},... | collective-permute-start | bytes 49160 | tf_op jit(solution)/shard_map/ppermute | solution.py:45
  28.7 1.2 %collective-permute-done.7 = f32[32,128]{1,0:T(8,128)S(1)} collective-permute-done((f32[32,128]{1,0:T(8,128)S(1)}, f32[32,128]{1,0:T(8,128)S(1)}, u32[]{:S(2)}, u32[]{:S(2)}) %collective-permute-start.7) | collective-permute-done | bytes 16416 | tf_op jit(solution)/shard_map/ppermute | solution.py:45
  29.9 0.0 collective-permute-done.6
  29.9 0.8 %collective-permute-done.5 = f32[32,128]{1,0:T(8,128)S(1)} collective-permute-done((f32[32,128]{1,0:T(8,128)S(1)}, f32[32,128]{1,0:T(8,128)S(1)}, u32[]{:S(2)}, u32[]{:S(2)}) %collective-permute-start.5) | collective-permute-done | bytes 16416 | tf_op jit(solution)/shard_map/ppermute | solution.py:45
  30.7 3.0 %collective-permute-start.10 = (f32[32,128]{1,0:T(8,128)S(1)}, f32[32,128]{1,0:T(8,128)S(1)}, u32[]{:S(2)}, u32[]{:S(2)}) collective-permute-start(f32[32,128]{1,0:T(8,128)S(1)} %add_add_fusion.1), channel_id=1, source_target_pairs={{0,6},{1,7},{2,4},{3,5},{4,2},{5,3},{6,0},{7,1},{8,14},{9,15},{10,... | collective-permute-start | bytes 49160 | tf_op jit(solution)/shard_map/ppermute | solution.py:45
  33.7 0.5 %collective-permute-start.9 = (f32[32,128]{1,0:T(8,128)S(1)}, f32[32,128]{1,0:T(8,128)S(1)}, u32[]{:S(2)}, u32[]{:S(2)}) collective-permute-start(f32[32,128]{1,0:T(8,128)S(1)} %add_add_fusion.1), channel_id=1, source_target_pairs={{0,4},{1,5},{2,6},{3,7},{4,0},{5,1},{6,2},{7,3},{8,12},{9,13},{10,... | collective-permute-start | bytes 49160 | tf_op jit(solution)/shard_map/ppermute | solution.py:45
  34.3 0.1 collective-permute-start.8
  34.4 1.1 %collective-permute-done.10 = f32[32,128]{1,0:T(8,128)S(1)} collective-permute-done((f32[32,128]{1,0:T(8,128)S(1)}, f32[32,128]{1,0:T(8,128)S(1)}, u32[]{:S(2)}, u32[]{:S(2)}) %collective-permute-start.10) | collective-permute-done | bytes 16416 | tf_op jit(solution)/shard_map/ppermute | solution.py:45
  35.5 2.0 %collective-permute-done.9 = f32[32,128]{1,0:T(8,128)S(1)} collective-permute-done((f32[32,128]{1,0:T(8,128)S(1)}, f32[32,128]{1,0:T(8,128)S(1)}, u32[]{:S(2)}, u32[]{:S(2)}) %collective-permute-start.9) | collective-permute-done | bytes 16416 | tf_op jit(solution)/shard_map/ppermute | solution.py:45
  37.5 0.5 %collective-permute-done.8 = f32[32,128]{1,0:T(8,128)S(1)} collective-permute-done((f32[32,128]{1,0:T(8,128)S(1)}, f32[32,128]{1,0:T(8,128)S(1)}, u32[]{:S(2)}, u32[]{:S(2)}) %collective-permute-start.8) | collective-permute-done | bytes 16416 | tf_op jit(solution)/shard_map/ppermute | solution.py:45
  38.0 0.1 collective-permute-start.11
  38.1 1.2 %collective-permute-done.11 = f32[32,128]{1,0:T(8,128)S(1)} collective-permute-done((f32[32,128]{1,0:T(8,128)S(1)}, f32[32,128]{1,0:T(8,128)S(1)}, u32[]{:S(2)}, u32[]{:S(2)}) %collective-permute-start.11) | collective-permute-done | bytes 16416 | tf_op jit(solution)/shard_map/ppermute | solution.py:45
  39.3 1.1 %shard_map.55 = (f32[4,16,4096]{2,1,0:T(8,128)}, f32[64,64]{1,0:T(8,128)}) custom-call(f32[32,128]{1,0:T(8,128)S(1)} %add.27.p_ref, f32[4,16,4096]{2,1,0:T(8,128)S(1)} %get-tuple-element.18.l_ref, f32[1,16,4096]{2,1,0:T(8,128)S(1)} %get-tuple-element.24.first_ref, f32[1,16,4096]{2,1,0:T(8,128)S(1)} %get-tuple-element.25.second_ref), custom_call_target="tpu_custom_call" | custom-call | flops 4194304 | bytes 1048576 | tf_op jit(solution)/shard_map/pallas_call | solution.py:307
  (3 shorter events, 0.0 us)
Async XLA Ops:
  3.9 12.3 %collective-permute-start.1 = (f32[4,1,4096]{2,1,0:T(1,128)S(1)}, f32[4,1,4096]{2,1,0:T(1,128)S(1)}, u32[]{:S(2)}, u32[]{:S(2)}) collective-permute-start(f32[4,1,4096]{2,1,0:T(1,128)S(1)} %get-tuple-element.28), channel_id=1, source_target_pairs={{0,6},{2,0},{4,2},{6,4},{1,7},{3,1},{5,3},{7,5},{8,14},{10,8},{12,... | collective-permute-start | bytes 196616 | tf_op jit(solution)/shard_map/ppermute | solution.py:20
  7.9 8.3 %collective-permute-start = (f32[4,1,4096]{2,1,0:T(1,128)S(1)}, f32[4,1,4096]{2,1,0:T(1,128)S(1)}, u32[]{:S(2)}, u32[]{:S(2)}) collective-permute-start(f32[4,1,4096]{2,1,0:T(1,128)S(1)} %get-tuple-element.29), channel_id=1, source_target_pairs={{0,2},{2,4},{4,6},{6,0},{1,3},{3,5},{5,7},{7,1},{8,10},{10,12},{12... | collective-permute-start | bytes 196616 | tf_op jit(solution)/shard_map/ppermute | solution.py:20
  7.9 16.1 %collective-permute-start.3 = (f32[1,16,4096]{2,1,0:T(8,128)S(1)}, f32[1,16,4096]{2,1,0:T(8,128)S(1)}, u32[]{:S(2)}, u32[]{:S(2)}) collective-permute-start(f32[1,16,4096]{2,1,0:T(8,128)S(1)} %get-tuple-element.19), channel_id=1, source_target_pairs={{0,24},{8,16},{16,8},{24,0},{1,25},{9,17},{17,9},{25,1},{2,26},{10... | collective-permute-start | bytes 786440 | tf_op jit(solution)/shard_map/ppermute | solution.py:235
  11.5 12.2 %collective-permute-start.4 = (f32[1,16,4096]{2,1,0:T(8,128)S(1)}, f32[1,16,4096]{2,1,0:T(8,128)S(1)}, u32[]{:S(2)}, u32[]{:S(2)}) collective-permute-start(f32[1,16,4096]{2,1,0:T(8,128)S(1)} %get-tuple-element.20), channel_id=1, source_target_pairs={{0,8},{8,0},{16,24},{24,16},{1,9},{9,1},{17,25},{25,17},{2,10},{10... | collective-permute-start | bytes 786440 | tf_op jit(solution)/shard_map/ppermute | solution.py:235
  11.7 4.5 %collective-permute-start.2 = (f32[4,16,128]{2,1,0:T(8,128)S(1)}, f32[4,16,128]{2,1,0:T(8,128)S(1)}, u32[]{:S(2)}, u32[]{:S(2)}) collective-permute-start(f32[4,16,128]{2,1,0:T(8,128)S(1)} %pad_maximum_fusion), channel_id=1, source_target_pairs={{0,1},{1,0},{2,3},{3,2},{4,5},{5,4},{6,7},{7,6},{8,9},{9,8},{10,11... | collective-permute-start | bytes 98312 | tf_op jit(solution)/shard_map/ppermute | solution.py:20
  24.3 5.6 %collective-permute-start.7 = (f32[32,128]{1,0:T(8,128)S(1)}, f32[32,128]{1,0:T(8,128)S(1)}, u32[]{:S(2)}, u32[]{:S(2)}) collective-permute-start(f32[32,128]{1,0:T(8,128)S(1)} %get-tuple-element.23), channel_id=1, source_target_pairs={{0,24},{1,25},{2,26},{3,27},{4,28},{5,29},{6,30},{7,31},{8,16},{9,... | collective-permute-start | bytes 49160 | tf_op jit(solution)/shard_map/ppermute | solution.py:45
  24.8 5.1 %collective-permute-start.6 = (f32[32,128]{1,0:T(8,128)S(1)}, f32[32,128]{1,0:T(8,128)S(1)}, u32[]{:S(2)}, u32[]{:S(2)}) collective-permute-start(f32[32,128]{1,0:T(8,128)S(1)} %get-tuple-element.23), channel_id=1, source_target_pairs={{0,16},{1,17},{2,18},{3,19},{4,20},{5,21},{6,22},{7,23},{8,24},{9,... | collective-permute-start | bytes 49160 | tf_op jit(solution)/shard_map/ppermute | solution.py:45
  25.4 5.3 %collective-permute-start.5 = (f32[32,128]{1,0:T(8,128)S(1)}, f32[32,128]{1,0:T(8,128)S(1)}, u32[]{:S(2)}, u32[]{:S(2)}) collective-permute-start(f32[32,128]{1,0:T(8,128)S(1)} %get-tuple-element.23), channel_id=1, source_target_pairs={{0,8},{1,9},{2,10},{3,11},{4,12},{5,13},{6,14},{7,15},{8,0},{9,1},... | collective-permute-start | bytes 49160 | tf_op jit(solution)/shard_map/ppermute | solution.py:45
  30.7 4.7 %collective-permute-start.10 = (f32[32,128]{1,0:T(8,128)S(1)}, f32[32,128]{1,0:T(8,128)S(1)}, u32[]{:S(2)}, u32[]{:S(2)}) collective-permute-start(f32[32,128]{1,0:T(8,128)S(1)} %add_add_fusion.1), channel_id=1, source_target_pairs={{0,6},{1,7},{2,4},{3,5},{4,2},{5,3},{6,0},{7,1},{8,14},{9,15},{10,... | collective-permute-start | bytes 49160 | tf_op jit(solution)/shard_map/ppermute | solution.py:45
  33.7 3.7 %collective-permute-start.9 = (f32[32,128]{1,0:T(8,128)S(1)}, f32[32,128]{1,0:T(8,128)S(1)}, u32[]{:S(2)}, u32[]{:S(2)}) collective-permute-start(f32[32,128]{1,0:T(8,128)S(1)} %add_add_fusion.1), channel_id=1, source_target_pairs={{0,4},{1,5},{2,6},{3,7},{4,0},{5,1},{6,2},{7,3},{8,12},{9,13},{10,... | collective-permute-start | bytes 49160 | tf_op jit(solution)/shard_map/ppermute | solution.py:45
  34.3 3.7 %collective-permute-start.8 = (f32[32,128]{1,0:T(8,128)S(1)}, f32[32,128]{1,0:T(8,128)S(1)}, u32[]{:S(2)}, u32[]{:S(2)}) collective-permute-start(f32[32,128]{1,0:T(8,128)S(1)} %add_add_fusion.1), channel_id=1, source_target_pairs={{0,2},{1,3},{2,0},{3,1},{4,6},{5,7},{6,4},{7,5},{8,10},{9,11},{10,... | collective-permute-start | bytes 49160 | tf_op jit(solution)/shard_map/ppermute | solution.py:45
  38.0 1.2 %collective-permute-start.11 = (f32[32,128]{1,0:T(8,128)S(1)}, f32[32,128]{1,0:T(8,128)S(1)}, u32[]{:S(2)}, u32[]{:S(2)}) collective-permute-start(f32[32,128]{1,0:T(8,128)S(1)} %add_add_fusion), channel_id=1, source_target_pairs={{0,1},{1,0},{2,3},{3,2},{4,5},{5,4},{6,7},{7,6},{8,9},{9,8},{10,11... | collective-permute-start | bytes 49160 | tf_op jit(solution)/shard_map/ppermute | solution.py:45

commit v9 on v7

--- a/solution.py
+++ b/solution.py
@@ -29,20 +29,18 @@
 
 def stages_of(devices):
     bits = [1 << k for k in range(1, (devices - 1).bit_length())]
-    stages = [(1,)]
-    for low, high in zip(bits[0::2], bits[1::2]):
-        stages.append((low | high, high, low))
-    if len(bits) % 2:
-        stages.append((bits[-1],))
-    return stages[::-1]
+    triples = [(low | high, high, low) for low, high in zip(bits[0::2], bits[1::2])]
+    single = [(bits[-1],)] * (len(bits) % 2)
+    return list(zip(triples + single + [(1,)], triples[::-1] + single + [(1,)]))
 
 
 def sum_over_all(value):
     devices = lax.axis_size(AXES)
-    for masks in stages_of(devices):
+    for odd, even in stages_of(devices):
         got = []
-        for mask in masks:
-            got.append(lax.ppermute(value, AXES, [(i, i ^ mask) for i in range(devices)]))
+        for k in range(len(odd)):
+            moves = [(i, i ^ (odd if i % 2 else even)[k]) for i in range(devices)]
+            got.append(lax.ppermute(value, AXES, moves))
         if len(got) == 1:
             value = value + got[0]
         else:

time: 41.5 us -> 41.5 us (level)
  no operation moved by 1% of the time
where the time goes in v9:
time: 41.5 us; the launch traced here: 41.4 us
  waiting for transfers between devices  18.1 us (44%)
  starting transfers between devices  16.8 us (40%)
  Pallas kernels  5.38 us (13%)
  between operations  0.71 us (2%)
    ppermute x2, waiting for transfers between devices, z_exchange(): return lax.ppermute(array, 'gz', moves)  10.3 us
    ppermute x7, starting transfers between devices, sum_over_all(): got.append(lax.ppermute(value, AXES, moves))  7.73 us
    ppermute x7, waiting for transfers between devices, sum_over_all(): got.append(lax.ppermute(value, AXES, moves))  7.57 us
    ppermute x3, starting transfers between devices, ring(): lax.ppermute(array, axis, [(i, (i + step) % peers) for i in range(peers)])  4.98 us
    ppermute x2, starting transfers between devices, z_exchange(): return lax.ppermute(array, 'gz', moves)  4.08 us
    pallas_call x1, Pallas kernels, local(): call(load, (in_vmem, in_vmem), 1 << 20, limit=60 << 20, in_specs=[HBM] *...  1.56 us
    pallas_call x1, Pallas kernels, local(): call(functools.partial(final, total_cells), (whole, jax.ShapeDtypeStruct(...  1.12 us
    pallas_call x1, Pallas kernels, local(): call(z_faces, (in_vmem, in_vmem), 1 << 20, limit=60 << 20, in_specs=[HBM]...  1.04 us
  transfers between devices with their start and end apart: 12, of which 8 were waited for; matrix products, arithmetic and copies ran while one was open for 1% of the time, Pallas kernels for 6%

profile of v9, /device:TPU:0, one launch (start us, length us, event | category | flops | bytes accessed | tf_op | source)
XLA Modules:
  0.0 41.4 jit_solution(10491812164420898814)
XLA Ops:
  0.6 1.6 %shard_map.50 = (f32[4,16,4096]{2,1,0:T(8,128)S(1)}, f32[4,16,4096]{2,1,0:T(8,128)S(1)}) custom-call(f32[4,16,4096]{2,1,0:T(8,128)} %g_ref.3, f32[4,16,4096]{2,1,0:T(8,128)} %b_ref.1), custom_call_target="tpu_custom_call" | custom-call | flops 1048576 | bytes 1048576 | tf_op jit(solution)/shard_map/pallas_call | solution.py:234
  2.2 0.1 fusion.1
  2.3 3.0 %collective-permute-start = (f32[4,1,4096]{2,1,0:T(1,128)S(1)}, f32[4,1,4096]{2,1,0:T(1,128)S(1)}, u32[]{:S(2)}, u32[]{:S(2)}) collective-permute-start(f32[4,1,4096]{2,1,0:T(1,128)S(1)} %get-tuple-element.25), channel_id=1, source_target_pairs={{0,2},{2,4},{4,6},{6,0},{1,3},{3,5},{5,7},{7,1},{8,10},{10,12},{12... | collective-permute-start | bytes 196616 | tf_op jit(solution)/shard_map/ppermute | solution.py:20
  5.3 1.0 %collective-permute-start.1 = (f32[4,1,4096]{2,1,0:T(1,128)S(1)}, f32[4,1,4096]{2,1,0:T(1,128)S(1)}, u32[]{:S(2)}, u32[]{:S(2)}) collective-permute-start(f32[4,1,4096]{2,1,0:T(1,128)S(1)} %get-tuple-element.24), channel_id=1, source_target_pairs={{0,6},{2,0},{4,2},{6,4},{1,7},{3,1},{5,3},{7,5},{8,14},{10,8},{12,... | collective-permute-start | bytes 196616 | tf_op jit(solution)/shard_map/ppermute | solution.py:20
  6.3 1.0 %shard_map.53 = (f32[1,16,4096]{2,1,0:T(8,128)S(1)}, f32[1,16,4096]{2,1,0:T(8,128)S(1)}) custom-call(f32[4,16,4096]{2,1,0:T(8,128)} %g_ref.3), custom_call_target="tpu_custom_call" | custom-call | flops 1048576 | bytes 1048576 | tf_op jit(solution)/shard_map/pallas_call | solution.py:222
  7.4 4.1 %collective-permute-start.3 = (f32[1,16,4096]{2,1,0:T(8,128)S(1)}, f32[1,16,4096]{2,1,0:T(8,128)S(1)}, u32[]{:S(2)}, u32[]{:S(2)}) collective-permute-start(f32[1,16,4096]{2,1,0:T(8,128)S(1)} %get-tuple-element.15), channel_id=1, source_target_pairs={{0,24},{8,16},{16,8},{24,0},{1,25},{9,17},{17,9},{25,1},{2,26},{10... | collective-permute-start | bytes 786440 | tf_op jit(solution)/shard_map/ppermute | solution.py:209
  11.5 0.0 collective-permute-start.4
  11.5 0.1 fusion
  11.6 0.0 copy-start
  11.6 0.1 pad_maximum_fusion
  11.6 0.9 %collective-permute-start.2 = (f32[4,16,128]{2,1,0:T(8,128)S(1)}, f32[4,16,128]{2,1,0:T(8,128)S(1)}, u32[]{:S(2)}, u32[]{:S(2)}) collective-permute-start(f32[4,16,128]{2,1,0:T(8,128)S(1)} %pad_maximum_fusion), channel_id=1, source_target_pairs={{0,1},{1,0},{2,3},{3,2},{4,5},{5,4},{6,7},{7,6},{8,9},{9,8},{10,11... | collective-permute-start | bytes 98312 | tf_op jit(solution)/shard_map/ppermute | solution.py:20
  12.6 0.0 copy-done
  12.6 0.1 broadcast_in_dim_tile.3.c_ref
  12.7 0.5 %shard_map.51.i_ref = f32[4,16,4096]{2,1,0:T(8,128)S(1)} custom-call(f32[4,16,4096]{2,1,0:T(8,128)S(1)} %get-tuple-element.12.g_ref, f32[4,16,4096]{2,1,0:T(8,128)S(1)} %get-tuple-element.13.b_ref, f32[1,128]{1,0:T(1,128)S(1)} %broadcast_in_dim_tile.3.c_ref), custom_call_target="tpu_custom_call" | custom-call | flops 16777216 | bytes 1048576 | tf_op jit(solution)/shard_map/pallas_call | solution.py:254
  13.2 0.3 collective-permute-done.2.xh_ref
  13.4 0.0 collective-permute-done.yb_ref
  13.4 0.0 collective-permute-done.1.ya_ref
  13.4 0.6 %shard_map.52 = (f32[4,16,4096]{2,1,0:T(8,128)S(1)}, f32[128,128]{1,0:T(8,128)S(1)}) custom-call(f32[4,16,4096]{2,1,0:T(8,128)S(1)} %shard_map.51.i_ref, f32[4,1,4096]{2,1,0:T(1,128)S(1)} %collective-permute-done.yb_ref, f32[4,1,4096]{2,1,0:T(1,128)S(1)} %collective-permute-done.1.ya_ref, ...), custom_call_target="tpu_custom_call", output_to_operand_aliasing={{0}: (0, {})} | custom-call | flops 16777216 | bytes 1048576 | tf_op jit(solution)/shard_map/pallas_call | solution.py:255
  14.1 10.3 %collective-permute-done.4.h_ref = f32[1,16,4096]{2,1,0:T(8,128)S(1)} collective-permute-done((f32[1,16,4096]{2,1,0:T(8,128)S(1)}, f32[1,16,4096]{2,1,0:T(8,128)S(1)}, u32[]{:S(2)}, u32[]{:S(2)}) %collective-permute-start.4) | collective-permute-done | bytes 262176 | tf_op jit(solution)/shard_map/ppermute | solution.py:209
  24.3 0.2 shard_map.54
  24.6 0.0 collective-permute-done.3.h_ref
  24.6 0.3 shard_map.55
  24.9 0.4 %collective-permute-start.6 = (f32[32,128]{1,0:T(8,128)S(1)}, f32[32,128]{1,0:T(8,128)S(1)}, u32[]{:S(2)}, u32[]{:S(2)}) collective-permute-start(f32[32,128]{1,0:T(8,128)S(1)} %get-tuple-element.19), channel_id=1, source_target_pairs={{0,16},{1,5},{2,18},{3,7},{4,20},{5,1},{6,22},{7,3},{8,24},{9,13},... | collective-permute-start | bytes 49160 | tf_op jit(solution)/shard_map/ppermute | solution.py:43
  25.3 3.7 %collective-permute-start.7 = (f32[32,128]{1,0:T(8,128)S(1)}, f32[32,128]{1,0:T(8,128)S(1)}, u32[]{:S(2)}, u32[]{:S(2)}) collective-permute-start(f32[32,128]{1,0:T(8,128)S(1)} %get-tuple-element.19), channel_id=1, source_target_pairs={{0,24},{1,7},{2,26},{3,5},{4,28},{5,3},{6,30},{7,1},{8,16},{9,15},... | collective-permute-start | bytes 49160 | tf_op jit(solution)/shard_map/ppermute | solution.py:43
  29.0 0.0 collective-permute-start.5
  29.0 0.5 %collective-permute-done.6 = f32[32,128]{1,0:T(8,128)S(1)} collective-permute-done((f32[32,128]{1,0:T(8,128)S(1)}, f32[32,128]{1,0:T(8,128)S(1)}, u32[]{:S(2)}, u32[]{:S(2)}) %collective-permute-start.6) | collective-permute-done | bytes 16416 | tf_op jit(solution)/shard_map/ppermute | solution.py:43
  29.6 1.3 %collective-permute-done.7 = f32[32,128]{1,0:T(8,128)S(1)} collective-permute-done((f32[32,128]{1,0:T(8,128)S(1)}, f32[32,128]{1,0:T(8,128)S(1)}, u32[]{:S(2)}, u32[]{:S(2)}) %collective-permute-start.7) | collective-permute-done | bytes 16416 | tf_op jit(solution)/shard_map/ppermute | solution.py:43
  30.9 1.9 %collective-permute-done.5 = f32[32,128]{1,0:T(8,128)S(1)} collective-permute-done((f32[32,128]{1,0:T(8,128)S(1)}, f32[32,128]{1,0:T(8,128)S(1)}, u32[]{:S(2)}, u32[]{:S(2)}) %collective-permute-start.5) | collective-permute-done | bytes 16416 | tf_op jit(solution)/shard_map/ppermute | solution.py:43
  32.8 1.6 %collective-permute-start.9 = (f32[32,128]{1,0:T(8,128)S(1)}, f32[32,128]{1,0:T(8,128)S(1)}, u32[]{:S(2)}, u32[]{:S(2)}) collective-permute-start(f32[32,128]{1,0:T(8,128)S(1)} %add_add_fusion.1), channel_id=1, source_target_pairs={{0,4},{1,17},{2,6},{3,19},{4,0},{5,21},{6,2},{7,23},{8,12},{9,25},... | collective-permute-start | bytes 49160 | tf_op jit(solution)/shard_map/ppermute | solution.py:43
  34.3 0.0 collective-permute-start.10
  34.4 2.0 %collective-permute-start.8 = (f32[32,128]{1,0:T(8,128)S(1)}, f32[32,128]{1,0:T(8,128)S(1)}, u32[]{:S(2)}, u32[]{:S(2)}) collective-permute-start(f32[32,128]{1,0:T(8,128)S(1)} %add_add_fusion.1), channel_id=1, source_target_pairs={{0,2},{1,9},{2,0},{3,11},{4,6},{5,13},{6,4},{7,15},{8,10},{9,1},{1... | collective-permute-start | bytes 49160 | tf_op jit(solution)/shard_map/ppermute | solution.py:43
  36.3 0.2 collective-permute-done.9
  36.6 2.4 %collective-permute-done.10 = f32[32,128]{1,0:T(8,128)S(1)} collective-permute-done((f32[32,128]{1,0:T(8,128)S(1)}, f32[32,128]{1,0:T(8,128)S(1)}, u32[]{:S(2)}, u32[]{:S(2)}) %collective-permute-start.10) | collective-permute-done | bytes 16416 | tf_op jit(solution)/shard_map/ppermute | solution.py:43
  39.0 0.0 collective-permute-done.8
  39.0 0.1 collective-permute-start.11
  39.1 1.2 %collective-permute-done.11 = f32[32,128]{1,0:T(8,128)S(1)} collective-permute-done((f32[32,128]{1,0:T(8,128)S(1)}, f32[32,128]{1,0:T(8,128)S(1)}, u32[]{:S(2)}, u32[]{:S(2)}) %collective-permute-start.11) | collective-permute-done | bytes 16416 | tf_op jit(solution)/shard_map/ppermute | solution.py:43
  40.3 1.1 %shard_map.56 = (f32[4,16,4096]{2,1,0:T(8,128)}, f32[64,64]{1,0:T(8,128)}) custom-call(f32[32,128]{1,0:T(8,128)S(1)} %add.35.p_ref, f32[4,16,4096]{2,1,0:T(8,128)S(1)} %get-tuple-element.14.l_ref, f32[1,16,4096]{2,1,0:T(8,128)S(1)} %get-tuple-element.20.first_ref, f32[1,16,4096]{2,1,0:T(8,128)S(1)} %get-tuple-element.21.second_ref), custom_call_target="tpu_custom_call" | custom-call | flops 4194304 | bytes 1048576 | tf_op jit(solution)/shard_map/pallas_call | solution.py:279
  (5 shorter events, 0.0 us)
Async XLA Ops:
  2.3 11.1 %collective-permute-start = (f32[4,1,4096]{2,1,0:T(1,128)S(1)}, f32[4,1,4096]{2,1,0:T(1,128)S(1)}, u32[]{:S(2)}, u32[]{:S(2)}) collective-permute-start(f32[4,1,4096]{2,1,0:T(1,128)S(1)} %get-tuple-element.25), channel_id=1, source_target_pairs={{0,2},{2,4},{4,6},{6,0},{1,3},{3,5},{5,7},{7,1},{8,10},{10,12},{12... | collective-permute-start | bytes 196616 | tf_op jit(solution)/shard_map/ppermute | solution.py:20
  5.3 8.1 %collective-permute-start.1 = (f32[4,1,4096]{2,1,0:T(1,128)S(1)}, f32[4,1,4096]{2,1,0:T(1,128)S(1)}, u32[]{:S(2)}, u32[]{:S(2)}) collective-permute-start(f32[4,1,4096]{2,1,0:T(1,128)S(1)} %get-tuple-element.24), channel_id=1, source_target_pairs={{0,6},{2,0},{4,2},{6,4},{1,7},{3,1},{5,3},{7,5},{8,14},{10,8},{12,... | collective-permute-start | bytes 196616 | tf_op jit(solution)/shard_map/ppermute | solution.py:20
  7.4 17.2 %collective-permute-start.3 = (f32[1,16,4096]{2,1,0:T(8,128)S(1)}, f32[1,16,4096]{2,1,0:T(8,128)S(1)}, u32[]{:S(2)}, u32[]{:S(2)}) collective-permute-start(f32[1,16,4096]{2,1,0:T(8,128)S(1)} %get-tuple-element.15), channel_id=1, source_target_pairs={{0,24},{8,16},{16,8},{24,0},{1,25},{9,17},{17,9},{25,1},{2,26},{10... | collective-permute-start | bytes 786440 | tf_op jit(solution)/shard_map/ppermute | solution.py:209
  11.5 12.9 %collective-permute-start.4 = (f32[1,16,4096]{2,1,0:T(8,128)S(1)}, f32[1,16,4096]{2,1,0:T(8,128)S(1)}, u32[]{:S(2)}, u32[]{:S(2)}) collective-permute-start(f32[1,16,4096]{2,1,0:T(8,128)S(1)} %get-tuple-element.16), channel_id=1, source_target_pairs={{0,8},{8,0},{16,24},{24,16},{1,9},{9,1},{17,25},{25,17},{2,10},{10... | collective-permute-start | bytes 786440 | tf_op jit(solution)/shard_map/ppermute | solution.py:209
  11.6 1.0 %copy-start = (f32[64]{0:T(128)S(1)}, f32[64]{0:T(128)}, u32[]{:S(2)}) copy-start(f32[64]{0:T(128)} %param.5) | copy-start | bytes 772
  11.6 1.8 %collective-permute-start.2 = (f32[4,16,128]{2,1,0:T(8,128)S(1)}, f32[4,16,128]{2,1,0:T(8,128)S(1)}, u32[]{:S(2)}, u32[]{:S(2)}) collective-permute-start(f32[4,16,128]{2,1,0:T(8,128)S(1)} %pad_maximum_fusion), channel_id=1, source_target_pairs={{0,1},{1,0},{2,3},{3,2},{4,5},{5,4},{6,7},{7,6},{8,9},{9,8},{10,11... | collective-permute-start | bytes 98312 | tf_op jit(solution)/shard_map/ppermute | solution.py:20
  24.9 4.7 %collective-permute-start.6 = (f32[32,128]{1,0:T(8,128)S(1)}, f32[32,128]{1,0:T(8,128)S(1)}, u32[]{:S(2)}, u32[]{:S(2)}) collective-permute-start(f32[32,128]{1,0:T(8,128)S(1)} %get-tuple-element.19), channel_id=1, source_target_pairs={{0,16},{1,5},{2,18},{3,7},{4,20},{5,1},{6,22},{7,3},{8,24},{9,13},... | collective-permute-start | bytes 49160 | tf_op jit(solution)/shard_map/ppermute | solution.py:43
  25.3 5.6 %collective-permute-start.7 = (f32[32,128]{1,0:T(8,128)S(1)}, f32[32,128]{1,0:T(8,128)S(1)}, u32[]{:S(2)}, u32[]{:S(2)}) collective-permute-start(f32[32,128]{1,0:T(8,128)S(1)} %get-tuple-element.19), channel_id=1, source_target_pairs={{0,24},{1,7},{2,26},{3,5},{4,28},{5,3},{6,30},{7,1},{8,16},{9,15},... | collective-permute-start | bytes 49160 | tf_op jit(solution)/shard_map/ppermute | solution.py:43
  29.0 3.7 %collective-permute-start.5 = (f32[32,128]{1,0:T(8,128)S(1)}, f32[32,128]{1,0:T(8,128)S(1)}, u32[]{:S(2)}, u32[]{:S(2)}) collective-permute-start(f32[32,128]{1,0:T(8,128)S(1)} %get-tuple-element.19), channel_id=1, source_target_pairs={{0,8},{1,3},{2,10},{3,1},{4,12},{5,7},{6,14},{7,5},{8,0},{9,11},{1... | collective-permute-start | bytes 49160 | tf_op jit(solution)/shard_map/ppermute | solution.py:43
  32.8 3.8 %collective-permute-start.9 = (f32[32,128]{1,0:T(8,128)S(1)}, f32[32,128]{1,0:T(8,128)S(1)}, u32[]{:S(2)}, u32[]{:S(2)}) collective-permute-start(f32[32,128]{1,0:T(8,128)S(1)} %add_add_fusion.1), channel_id=1, source_target_pairs={{0,4},{1,17},{2,6},{3,19},{4,0},{5,21},{6,2},{7,23},{8,12},{9,25},... | collective-permute-start | bytes 49160 | tf_op jit(solution)/shard_map/ppermute | solution.py:43
  34.3 4.6 %collective-permute-start.10 = (f32[32,128]{1,0:T(8,128)S(1)}, f32[32,128]{1,0:T(8,128)S(1)}, u32[]{:S(2)}, u32[]{:S(2)}) collective-permute-start(f32[32,128]{1,0:T(8,128)S(1)} %add_add_fusion.1), channel_id=1, source_target_pairs={{0,6},{1,25},{2,4},{3,27},{4,2},{5,29},{6,0},{7,31},{8,14},{9,17},... | collective-permute-start | bytes 49160 | tf_op jit(solution)/shard_map/ppermute | solution.py:43
  34.4 4.6 %collective-permute-start.8 = (f32[32,128]{1,0:T(8,128)S(1)}, f32[32,128]{1,0:T(8,128)S(1)}, u32[]{:S(2)}, u32[]{:S(2)}) collective-permute-start(f32[32,128]{1,0:T(8,128)S(1)} %add_add_fusion.1), channel_id=1, source_target_pairs={{0,2},{1,9},{2,0},{3,11},{4,6},{5,13},{6,4},{7,15},{8,10},{9,1},{1... | collective-permute-start | bytes 49160 | tf_op jit(solution)/shard_map/ppermute | solution.py:43
  39.0 1.2 %collective-permute-start.11 = (f32[32,128]{1,0:T(8,128)S(1)}, f32[32,128]{1,0:T(8,128)S(1)}, u32[]{:S(2)}, u32[]{:S(2)}) collective-permute-start(f32[32,128]{1,0:T(8,128)S(1)} %add_add_fusion), channel_id=1, source_target_pairs={{0,1},{1,0},{2,3},{3,2},{4,5},{5,4},{6,7},{7,6},{8,9},{9,8},{10,11... | collective-permute-start | bytes 49160 | tf_op jit(solution)/shard_map/ppermute | solution.py:43
